TPU v7x, 32 devices: a whole 2x2x4 slice. The times are simulated.
32 devices in a mesh: comp: 2 (over core), aa: 2 (over y), ba: 8 (over z, x).
Axes of the slice: x: 2, y: 2, z: 4, core: 2. Of those that a mesh axis runs over, the one named last changes fastest.
Arguments:
- legendre: bfloat16 [640, 8, 1280], P('aa'), may hold values from -0.15625 to 0.15625
- coefficients: bfloat16 [2, 640, 2, 64, 1280], P('comp', 'aa', None, 'ba'), may hold values from -0.1796875 to 0.1796875
- cycle_points: int32 [8], replicated, may hold values from 1024 to 4096, as said below
- spectra: float32 [32, 256, 1296], P('aa', 'ba', 'comp'), may hold values from 0.05 to 2
- sea_mask: int32 [32, 256], P('aa', 'ba'), may hold values 0 or 1
- wind_column: int32 [32, 256], P('aa'), may hold values from 0 to 4095, as said below
- roughness_source: int32 [8, 4096], P('aa', 'ba'), may hold values from 0 to 4095, as said below
Outputs:
- grid_winds: bfloat16 [2, 8, 64, 4096], P('comp', 'aa', None, 'ba')
- wave_spectra: float32 [32, 256, 1296], P('aa', 'ba', 'comp')
- charnock: float32 [8, 4096], P('aa', 'ba')
Inputs may be any that keep to these rules, and one draw needn't show every extreme that they name: `cycle_points`: at least a quarter of 4096; one cycle has exactly 4096 points. `wind_column`: each value is below the point count of cycle row // 4. `roughness_source`: the row within the band is one of the 4 rows (l mod 4) * 4 onward.
All inputs are finite; a program needn't handle non-finite values. No bound on the sum of `sea_mask` on one device may be relied on, other than what follows from the above.
Results may differ from a plain program's by a relative error of at most 0.0046.
The roundings to bfloat16 on the way count: a program that leaves them out, or rounds other values in their place, can miss the bound.
Values may be sent and summed in bfloat16 or wider, within the bound.
No kernel may reach another device: no remote copies, remote signals or barrier semaphores. Data moves between devices by JAX's collectives and lax.ppermute only.
A program may use at most 64 MiB of HBM per device.

v0:
```python
import math

import jax
import jax.numpy as jnp
from jax import lax
from jax.sharding import PartitionSpec as P

LON = 4096
NDIR = 36
NFREQ = 36
WSTEPS = 2


two_pi = 2.0 * math.pi
gravity = 9.81
base_freq = 0.04177
courant = 0.45
wind_scale = 10.0
growth = 0.05
dissipation = 0.5
energy_ref = 8.0
mid_freq = 0.2
stress_coef = 0.03
drag_coef = 0.0012
stress_floor = 0.02


def with_halo(block, sides, width):
    for axis, dim in sides:
        count = lax.axis_size(axis)
        forward = [(i, i + 1) for i in range(count - 1)]
        backward = [(target, source) for source, target in forward]
        low = lax.ppermute(
            lax.slice_in_dim(block, block.shape[dim] - width, None, axis=dim), axis, forward
        )
        high = lax.ppermute(lax.slice_in_dim(block, 0, width, axis=dim), axis, backward)
        block = jnp.concatenate([low, block, high], axis=dim)
    return block


def cycle_tables(cycle_counts, slot_index, wave_count):
    orders = jnp.arange(wave_count, dtype=jnp.int32)
    remain = orders[None, :, None] * slot_index[None, None, :] % cycle_counts[:, None, None]
    phases = two_pi * remain.astype(jnp.float32) / cycle_counts.astype(jnp.float32)[:, None, None]
    weight = jnp.where(orders == 0, 1.0, 2.0).astype(jnp.float32)[None, :, None]
    active = slot_index[None, None, :] < cycle_counts[:, None, None]
    cosine_part = jnp.where(active, weight * jnp.cos(phases), 0.0)
    sine_part = jnp.where(active, -weight * jnp.sin(phases), 0.0)
    return jnp.stack([cosine_part, sine_part], axis=1).astype(jnp.bfloat16)


def bin_constants(directions, freq_index):
    heading = two_pi * (directions.astype(jnp.float32) + 0.5) / NDIR
    freq_step = 35.0 / (NFREQ - 1)
    period_ratio = jnp.exp(-math.log(1.1) * freq_step * freq_index.astype(jnp.float32))
    frequency = base_freq / period_ratio
    cosine_dir = jnp.cos(heading)
    sine_dir = jnp.sin(heading)
    drift_east = courant * period_ratio * cosine_dir
    drift_north = courant * period_ratio * sine_dir
    inverse_speed = two_pi * frequency / gravity
    bin_width = 0.1 * frequency * (two_pi / NDIR)
    return (frequency, cosine_dir, sine_dir, drift_east, drift_north, inverse_speed, bin_width)


def advect(padded, drift_east, drift_north):
    centre = padded[1:-1, 1:-1]
    western = padded[1:-1, :-2]
    eastern = padded[1:-1, 2:]
    southern = padded[:-2, 1:-1]
    northern = padded[2:, 1:-1]
    east_pos = jnp.maximum(drift_east, 0.0)
    east_neg = jnp.minimum(drift_east, 0.0)
    north_pos = jnp.maximum(drift_north, 0.0)
    north_neg = jnp.minimum(drift_north, 0.0)
    return (
        centre
        - east_pos * (centre - western)
        - east_neg * (eastern - centre)
        - north_pos * (centre - southern)
        - north_neg * (northern - centre)
    )


def wind_terms(density, east_wind, north_wind, cosine_dir, sine_dir, inverse_speed, bin_width):
    alignment = (
        east_wind[..., None] * cosine_dir + north_wind[..., None] * sine_dir
    ) * inverse_speed
    wind_gain = growth * jnp.maximum(alignment - 1.0, 0.0)
    energy_part = jnp.sum(density * bin_width, axis=-1)
    stress_part = jnp.sum(wind_gain * density * alignment * bin_width, axis=-1)
    return (wind_gain, energy_part, stress_part)


def finish(density, wind_gain, energy, stress, east_wind, north_wind, frequency):
    decay_rate = dissipation * (frequency / mid_freq) * jnp.square(energy / energy_ref)[..., None]
    spectra_after = density * (1.0 + wind_gain) / (1.0 + decay_rate)
    air_stress = drag_coef * (east_wind * east_wind + north_wind * north_wind) + stress_floor
    roughness = jnp.sqrt(1.0 + stress_coef * stress / air_stress)
    return (spectra_after, roughness)


def per_device(
    legendre, coefficients, cycle_points, spectra, sea_mask, wind_column, roughness_source
):
    band_index = lax.axis_index("aa")
    column_index = lax.axis_index("ba")
    half_index = lax.axis_index("comp")
    wave_block = legendre.shape[0]
    degrees = jnp.arange(legendre.shape[2], dtype=jnp.int32)
    orders_local = band_index * wave_block + jnp.arange(wave_block, dtype=jnp.int32)
    masked = jnp.where(
        degrees[None, None, :] >= orders_local[:, None, None], legendre, jnp.zeros((), jnp.bfloat16)
    )
    partial_fourier = jnp.einsum(
        "mln,smpcn->smlpc", masked, coefficients, preferred_element_type=jnp.float32
    ).astype(jnp.bfloat16)
    cycle_fourier = lax.all_to_all(partial_fourier, "aa", split_axis=2, concat_axis=1, tiled=True)
    wave_count = cycle_fourier.shape[1]
    cycles_local = cycle_fourier.shape[2]
    slots_local = LON // lax.axis_size("ba")
    counts = lax.dynamic_slice_in_dim(cycle_points, band_index * cycles_local, cycles_local)
    own_slots = column_index * slots_local + jnp.arange(slots_local, dtype=jnp.int32)
    tables = cycle_tables(counts, own_slots, wave_count)
    grid_winds = jnp.einsum(
        "smlpc,lpmx->slcx",
        lax.all_gather(cycle_fourier, "ba", axis=4, tiled=True),
        tables,
        preferred_element_type=jnp.float32,
    ).astype(jnp.bfloat16)
    lowest = grid_winds[:, :, 0, :]
    wind_levels = lax.all_gather(lowest, "comp", axis=0, tiled=True)
    rows_local = spectra.shape[0]
    columns_local = spectra.shape[1]
    cycle_rows = rows_local // cycles_local
    own_columns = lax.dynamic_slice_in_dim(
        wind_column, column_index * columns_local, columns_local, 1
    )
    portion = lax.all_gather(wind_levels, "ba", axis=2, tiled=True)
    repeated = jnp.repeat(portion, cycle_rows, axis=1)
    inside = (own_columns >= 0) & (own_columns < portion.shape[2])
    position = jnp.clip(own_columns, 0, portion.shape[2] - 1)
    picked = jnp.take_along_axis(
        repeated, jnp.broadcast_to(position[None], (2,) + position.shape), axis=2
    )
    wind_pair = jnp.where(inside[None], picked.astype(jnp.float32), 0.0)
    east_wind = wind_scale * wind_pair[0]
    north_wind = wind_scale * wind_pair[1]
    half_bins = spectra.shape[2]
    dir_half = half_bins // NFREQ
    bin_index = jnp.arange(half_bins, dtype=jnp.int32)
    frequency, cosine_dir, sine_dir, drift_east, drift_north, inverse_speed, bin_width = (
        bin_constants(half_index * dir_half + bin_index // NFREQ, bin_index % NFREQ)
    )
    sea_float = sea_mask.astype(jnp.float32)[:, :, None]
    density = spectra * sea_float
    for substep in range(WSTEPS):
        padded = with_halo(density, (("aa", 0), ("ba", 1)), 1)
        density = advect(padded, drift_east, drift_north) * sea_float
    wind_gain, energy_part, stress_part = wind_terms(
        density, east_wind, north_wind, cosine_dir, sine_dir, inverse_speed, bin_width
    )
    energy, stress = lax.psum((energy_part, stress_part), "comp")
    wave_spectra, roughness = finish(
        density, wind_gain, energy, stress, east_wind, north_wind, frequency
    )
    band_ratio = lax.all_gather(roughness, "ba", axis=1, tiled=True).reshape(-1)
    values = jnp.take(band_ratio, roughness_source)
    slot_index = column_index * slots_local + jnp.arange(slots_local, dtype=jnp.int32)
    active = slot_index[None, :] < counts[:, None]
    charnock = jnp.where(active, values, 0.0)
    return (grid_winds, wave_spectra, charnock)


def solution(mesh):
    in_specs = (
        P("aa", None, None),
        P("comp", "aa", None, "ba", None),
        P(),
        P("aa", "ba", "comp"),
        P("aa", "ba"),
        P("aa", None),
        P("aa", "ba"),
    )
    out_specs = (P("comp", "aa", None, "ba"), P("aa", "ba", "comp"), P("aa", "ba"))
    return jax.shard_map(
        per_device, mesh=mesh, in_specs=in_specs, out_specs=out_specs, check_vma=False
    )
```

profile of v0, /device:TPU:0, one launch (start us, length us, event | category | flops | bytes accessed | tf_op | source)
XLA Modules:
  0.0 273.0 jit_solution(1992552034747684690)
XLA Ops:
  0.6 0.3 iota_compare_fusion
  0.9 32.8 %fusion.46 = bf16[1,320,8,2,8]{4,2,3,1,0:T(8,128)(2,1)S(1)} fusion(bf16[1,320,2,8,1280]{4,3,2,1,0:T(8,128)(2,1)} %param.8, bf16[320,8,1280]{2,1,0:T(8,128)(2,1)} %param.7, pred[320,1280]{1,0:T(8,128)(4,1)S(1)} %iota_compare_fusion), kind=kOutput, calls=%fused_computation.72 | convolution fusion | flops 108175360 | bytes 20152320 | tf_op jit(solution)/shard_map/mln,smpcn->smlpc/dot_general | solution.py:115
  33.7 1.9 copy.12
  35.6 4.3 %all-to-all-start = ((bf16[1,320,8,2,8]{1,4,3,0,2:T(8,128)(2,1)}), bf16[1,320,8,2,8]{1,4,3,0,2:T(8,128)(2,1)S(1)}, u32[]{:S(2)}, u32[]{:S(2)}) async-start(bf16[1,320,8,2,8]{1,4,3,0,2:T(8,128)(2,1)} %copy.12), calls=%async_computation | async-start | bytes 196608 | tf_op jit(solution)/shard_map/all_to_all | solution.py:118
  39.9 0.0 copy-start.5
  39.9 0.2 broadcast_multiply_fusion
  40.1 1.3 collective-permute-start.1
  41.4 4.6 %collective-permute-start = (f32[1,32,648]{2,1,0:T(8,128)S(1)}, f32[1,32,648]{2,1,0:T(8,128)S(1)}, u32[]{:S(2)}, u32[]{:S(2)}) collective-permute-start(f32[1,32,648]{2,1,0:T(8,128)S(1)} %get-tuple-element.18), channel_id=1, source_target_pairs={{0,8},{1,9},{2,10},{3,11},{4,12},{5,13},{6,14},{7,15},{16,24},{17,... | collective-permute-start | bytes 248840 | tf_op jit(solution)/shard_map/ppermute | solution.py:33
  46.0 0.1 compare_select_fusion.1
  46.1 0.2 iota_multiply_fusion
  46.3 0.1 broadcast_compare_fusion.1
  46.4 0.1 fusion.83
  46.5 0.1 broadcast_minimum_fusion
  46.5 0.1 broadcast_minimum_fusion.1
  46.6 0.1 broadcast_compare_fusion
  46.7 71.0 %select_convert_fusion.1 = (bf16[4,1,640,512]{3,2,1,0:T(8,128)(2,1)}, bf16[4,1,640,512]{3,2,1,0:T(8,128)(2,1)}) fusion(f32[640]{0:T(1024)S(1)} %get-tuple-element.25, f32[4]{0:T(128)S(1)} %convert_element_type.103, pred[4]{0:T(512)(128)(4,1)S(1)} %broadcast_compare_fusion.2, s32[4]{0:T(128)S(1)} %get-tuple-element.10, s32[640,512]{1,0:T(8,128)S(1)} %iota_multiply_fusion, ...), kind=kLoop, calls=%fused_computation.19 | loop fusion | flops 20971520 | bytes 6560804 | tf_op jit(solution)/shard_map/convert
  117.8 0.1 reshape.270
  117.9 0.1 copy.21
  118.0 0.1 all_to_all.16
  118.1 33.0 %all_gather.12 = bf16[1,640,4,2,64]{1,4,3,2,0:T(8,128)(2,1)S(1)} all-gather(bf16[1,640,4,2,8]{1,4,3,2,0:T(8,128)(2,1)S(1)} %all_to_all.16), channel_id=1, replica_groups=mesh['comp'=2,'aa'=2,'ba'=8] {'ba'}, dimensions={4}, use_global_device_ids=true | all-gather | bytes 737280 | tf_op jit(solution)/shard_map/all_gather | solution.py:127
  151.1 0.1 pad_maximum_fusion.21
  151.2 1.3 collective-permute-start.3
  152.5 4.5 %collective-permute-start.2 = (f32[18,1,648]{2,1,0:T(1,128)S(1)}, f32[18,1,648]{2,1,0:T(1,128)S(1)}, u32[]{:S(2)}, u32[]{:S(2)}) collective-permute-start(f32[18,1,648]{2,1,0:T(1,128)S(1)} %get-tuple-element.14), channel_id=1, source_target_pairs={{0,1},{1,2},{2,3},{3,4},{4,5},{5,6},{6,7},{8,9},{9,10},{10,11},{11... | collective-permute-start | bytes 139976 | tf_op jit(solution)/shard_map/ppermute | solution.py:33
  157.1 2.7 %fusion.57 = bf16[1,4,64,512]{3,2,1,0:T(8,128)(2,1)S(1)} fusion(bf16[4,1,640,512]{3,2,1,0:T(8,128)(2,1)} %get-tuple-element.21, bf16[4,1,640,512]{3,2,1,0:T(8,128)(2,1)S(1)} %copy-done, bf16[1,640,4,2,64]{1,4,3,2,0:T(8,128)(2,1)S(1)} %all_gather.12), kind=kOutput, calls=%fused_computation.76 | convolution fusion | flops 346161152 | bytes 6160384 | tf_op jit(solution)/shard_map/smlpc,lpmx->slcx/dot_general | solution.py:125
  159.8 0.0 copy-start.6
  159.9 1.8 all-gather
  161.7 30.5 %all-gather.1 = bf16[2,4,1,4096]{3,1,2,0:T(4,128)(2,1)S(1)} all-gather(bf16[2,4,1,512]{3,1,2,0:T(4,128)(2,1)S(1)} %all-gather), channel_id=3, replica_groups=mesh['comp'=2,'aa'=2,'ba'=8] {'ba'}, dimensions={3}, use_global_device_ids=true | all-gather | bytes 73728 | tf_op jit(solution)/shard_map/all_gather | solution.py:139
  192.2 0.1 broadcast_in_dim.123
  192.3 0.1 reshape.260
  192.4 10.6 %gather_fusion.1 = bf16[1024]{0:T(1024)(128)(2,1)S(1)} fusion(bf16[2,16,4096]{2,1,0:T(8,128)(2,1)S(1)} %reshape.260, s32[1024]{0:T(1024)S(1)} %reshape.270), kind=kCustom, calls=%fused_computation.1 | custom fusion | bytes 16384 | tf_op jit(solution)/shard_map/jit(take_along_axis)/gather | solution.py:143
  203.0 0.1 reshape.273
  203.1 2.5 fusion.36
  205.6 1.3 collective-permute-start.5
  206.9 4.6 %collective-permute-start.4 = (f32[1,32,648]{2,1,0:T(8,128)S(1)}, f32[1,32,648]{2,1,0:T(8,128)S(1)}, u32[]{:S(2)}, u32[]{:S(2)}) collective-permute-start(f32[1,32,648]{2,1,0:T(8,128)S(1)} %get-tuple-element.16), channel_id=1, source_target_pairs={{0,8},{1,9},{2,10},{3,11},{4,12},{5,13},{6,14},{7,15},{16,24},{17,... | collective-permute-start | bytes 248840 | tf_op jit(solution)/shard_map/ppermute | solution.py:33
  211.5 0.6 collective-permute-done.5
  212.1 1.5 collective-permute-done.4
  213.7 0.1 pad_maximum_fusion.18
  213.7 1.3 collective-permute-start.7
  215.0 4.5 %collective-permute-start.6 = (f32[18,1,648]{2,1,0:T(1,128)S(1)}, f32[18,1,648]{2,1,0:T(1,128)S(1)}, u32[]{:S(2)}, u32[]{:S(2)}) collective-permute-start(f32[18,1,648]{2,1,0:T(1,128)S(1)} %get-tuple-element.12), channel_id=1, source_target_pairs={{0,1},{1,2},{2,3},{3,4},{4,5},{5,6},{6,7},{8,9},{9,10},{10,11},{11... | collective-permute-start | bytes 139976 | tf_op jit(solution)/shard_map/ppermute | solution.py:33
  219.6 0.2 collective-permute-done.7
  219.8 1.6 collective-permute-done.6
  221.4 3.3 %multiply_reduce_fusion = (f32[16,32]{1,0:T(8,128)S(1)}, f32[16,32]{1,0:T(8,128)S(1)}, f32[16,32,648]{2,1,0:T(8,128)S(1)}) fusion(f32[648]{0:T(1024)S(1)} %broadcast_multiply_fusion.1, f32[648]{0:T(1024)S(1)} %broadcast_multiply_fusion.3, f32[648]{0:T(1024)S(1)} %get-tuple-element.31, f32[16,32]{1,0:T(8,128)S(1)} %get-tuple-element.23, ...), kind=kLoop, calls=%fused_computation.67 | loop fusion | flops 11279360 | bytes 2944384 | tf_op jit(solution)/shard_map/reduce_sum | solution.py:91
  224.7 3.3 %all-reduce = (f32[16,32]{1,0:T(8,128)S(1)}, f32[16,32]{1,0:T(8,128)S(1)}) all-reduce(f32[16,32]{1,0:T(8,128)S(1)} %get-tuple-element.4, f32[16,32]{1,0:T(8,128)S(1)} %get-tuple-element.3), channel_id=1, replica_groups=mesh['comp'=2,'aa'=2,'ba'=8] {'comp'}, use_global_device_ids=true, to_apply=%region_1.2 | all-reduce | flops 1024 | bytes 8192 | tf_op jit(solution)/shard_map/psum | solution.py:163
  228.0 30.5 %all-gather.2 = f32[8,32,16]{1,2,0:T(8,128)S(1)} all-gather(f32[1,32,16]{1,2,0:T(8,128)S(1)} %sqrt_bitcast_fusion), channel_id=1, replica_groups=mesh['comp'=2,'aa'=2,'ba'=8] {'ba'}, dimensions={0}, use_global_device_ids=true | all-gather | bytes 18432 | tf_op jit(solution)/shard_map/all_gather | solution.py:167
  258.6 0.1 reshape.281
  258.7 11.8 %gather_fusion = f32[2048]{0:T(1024)S(1)} fusion(f32[4096]{0:T(1024)S(1)} %bitcast.67, s32[2048]{0:T(1024)S(1)} %broadcast_clamp_fusion), kind=kCustom, calls=%fused_computation | custom fusion | bytes 24576 | tf_op jit(solution)/shard_map/jit(_take)/gather | solution.py:168
  270.5 0.7 select_select_fusion
  271.2 1.9 add_divide_fusion
  (42 shorter events, 0.3 us)
Async XLA Ops:
  33.7 6.1 %copy-start.3 = (s32[16,32]{1,0:T(8,128)S(1)}, s32[16,32]{1,0:T(8,128)}, u32[]{:S(2)}) copy-start(s32[16,32]{1,0:T(8,128)} %param.11) | copy-start | bytes 6148
  33.7 6.1 %copy-start.1 = (f32[16,32,648]{2,1,0:T(8,128)S(1)}, f32[16,32,648]{2,1,0:T(8,128)}, u32[]{:S(2)}) copy-start(f32[16,32,648]{2,1,0:T(8,128)} %param.10) | copy-start | bytes 3981316
  35.6 82.3 %all-to-all-start = ((bf16[1,320,8,2,8]{1,4,3,0,2:T(8,128)(2,1)}), bf16[1,320,8,2,8]{1,4,3,0,2:T(8,128)(2,1)S(1)}, u32[]{:S(2)}, u32[]{:S(2)}) async-start(bf16[1,320,8,2,8]{1,4,3,0,2:T(8,128)(2,1)} %copy.12), calls=%async_computation | async-start | bytes 196608 | tf_op jit(solution)/shard_map/all_to_all | solution.py:118
  39.9 6.1 %copy-start.5 = (s32[8]{0:T(128)S(1)}, s32[8]{0:T(128)}, u32[]{:S(2)}) copy-start(s32[8]{0:T(128)} %param.9) | copy-start | bytes 100
  40.1 6.5 %copy-start.4 = (s32[16,256]{1,0:T(8,128)S(1)}, s32[16,256]{1,0:T(8,128)}, u32[]{:S(2)}) copy-start(s32[16,256]{1,0:T(8,128)} %param.12) | copy-start | bytes 49156
  40.1 6.6 %copy-start.2 = (s32[4,512]{1,0:T(4,128)S(1)}, s32[4,512]{1,0:T(4,128)}, u32[]{:S(2)}) copy-start(s32[4,512]{1,0:T(4,128)} %param.13) | copy-start | bytes 24580
  40.1 111.0 %collective-permute-start.1 = (f32[1,32,648]{2,1,0:T(8,128)S(1)}, f32[1,32,648]{2,1,0:T(8,128)S(1)}, u32[]{:S(2)}, u32[]{:S(2)}) collective-permute-start(f32[1,32,648]{2,1,0:T(8,128)S(1)} %get-tuple-element.19), channel_id=1, source_target_pairs={{8,0},{9,1},{10,2},{11,3},{12,4},{13,5},{14,6},{15,7},{24,16},{25,... | collective-permute-start | bytes 248840 | tf_op jit(solution)/shard_map/ppermute | solution.py:36
  41.4 109.7 %collective-permute-start = (f32[1,32,648]{2,1,0:T(8,128)S(1)}, f32[1,32,648]{2,1,0:T(8,128)S(1)}, u32[]{:S(2)}, u32[]{:S(2)}) collective-permute-start(f32[1,32,648]{2,1,0:T(8,128)S(1)} %get-tuple-element.18), channel_id=1, source_target_pairs={{0,8},{1,9},{2,10},{3,11},{4,12},{5,13},{6,14},{7,15},{16,24},{17,... | collective-permute-start | bytes 248840 | tf_op jit(solution)/shard_map/ppermute | solution.py:33
  118.1 39.0 %copy-start = (bf16[4,1,640,512]{3,2,1,0:T(8,128)(2,1)S(1)}, bf16[4,1,640,512]{3,2,1,0:T(8,128)(2,1)}, u32[]{:S(2)}) copy-start(bf16[4,1,640,512]{3,2,1,0:T(8,128)(2,1)} %get-tuple-element.20) | copy-start | bytes 7864324
  151.2 51.9 %collective-permute-start.3 = (f32[18,1,648]{2,1,0:T(1,128)S(1)}, f32[18,1,648]{2,1,0:T(1,128)S(1)}, u32[]{:S(2)}, u32[]{:S(2)}) collective-permute-start(f32[18,1,648]{2,1,0:T(1,128)S(1)} %get-tuple-element.15), channel_id=1, source_target_pairs={{1,0},{2,1},{3,2},{4,3},{5,4},{6,5},{7,6},{9,8},{10,9},{11,10},{12... | collective-permute-start | bytes 139976 | tf_op jit(solution)/shard_map/ppermute | solution.py:36
  152.5 50.6 %collective-permute-start.2 = (f32[18,1,648]{2,1,0:T(1,128)S(1)}, f32[18,1,648]{2,1,0:T(1,128)S(1)}, u32[]{:S(2)}, u32[]{:S(2)}) collective-permute-start(f32[18,1,648]{2,1,0:T(1,128)S(1)} %get-tuple-element.14), channel_id=1, source_target_pairs={{0,1},{1,2},{2,3},{3,4},{4,5},{5,6},{6,7},{8,9},{9,10},{10,11},{11... | collective-permute-start | bytes 139976 | tf_op jit(solution)/shard_map/ppermute | solution.py:33
  159.8 43.2 %copy-start.6 = (bf16[1,4,64,512]{3,2,1,0:T(8,128)(2,1)}, bf16[1,4,64,512]{3,2,1,0:T(8,128)(2,1)S(1)}, u32[]{:S(2)}) copy-start(bf16[1,4,64,512]{3,2,1,0:T(8,128)(2,1)S(1)} %fusion.57) | copy-start | bytes 786436
  205.6 6.5 %collective-permute-start.5 = (f32[1,32,648]{2,1,0:T(8,128)S(1)}, f32[1,32,648]{2,1,0:T(8,128)S(1)}, u32[]{:S(2)}, u32[]{:S(2)}) collective-permute-start(f32[1,32,648]{2,1,0:T(8,128)S(1)} %get-tuple-element.17), channel_id=1, source_target_pairs={{8,0},{9,1},{10,2},{11,3},{12,4},{13,5},{14,6},{15,7},{24,16},{25,... | collective-permute-start | bytes 248840 | tf_op jit(solution)/shard_map/ppermute | solution.py:36
  206.9 6.8 %collective-permute-start.4 = (f32[1,32,648]{2,1,0:T(8,128)S(1)}, f32[1,32,648]{2,1,0:T(8,128)S(1)}, u32[]{:S(2)}, u32[]{:S(2)}) collective-permute-start(f32[1,32,648]{2,1,0:T(8,128)S(1)} %get-tuple-element.16), channel_id=1, source_target_pairs={{0,8},{1,9},{2,10},{3,11},{4,12},{5,13},{6,14},{7,15},{16,24},{17,... | collective-permute-start | bytes 248840 | tf_op jit(solution)/shard_map/ppermute | solution.py:33
  213.7 6.0 %collective-permute-start.7 = (f32[18,1,648]{2,1,0:T(1,128)S(1)}, f32[18,1,648]{2,1,0:T(1,128)S(1)}, u32[]{:S(2)}, u32[]{:S(2)}) collective-permute-start(f32[18,1,648]{2,1,0:T(1,128)S(1)} %get-tuple-element.13), channel_id=1, source_target_pairs={{1,0},{2,1},{3,2},{4,3},{5,4},{6,5},{7,6},{9,8},{10,9},{11,10},{12... | collective-permute-start | bytes 139976 | tf_op jit(solution)/shard_map/ppermute | solution.py:36
  215.0 6.3 %collective-permute-start.6 = (f32[18,1,648]{2,1,0:T(1,128)S(1)}, f32[18,1,648]{2,1,0:T(1,128)S(1)}, u32[]{:S(2)}, u32[]{:S(2)}) collective-permute-start(f32[18,1,648]{2,1,0:T(1,128)S(1)} %get-tuple-element.12), channel_id=1, source_target_pairs={{0,1},{1,2},{2,3},{3,4},{4,5},{5,6},{6,7},{8,9},{9,10},{10,11},{11... | collective-permute-start | bytes 139976 | tf_op jit(solution)/shard_map/ppermute | solution.py:33
where the time goes:
time: 274 us; the launch traced here: 273 us
  blocking collectives  99.2 us (36%)
  other arithmetic  80.7 us (29%)
  matrix products  35.5 us (13%)
  starting transfers between devices  27.6 us (10%)
  local copies, waits for them, and re-layouts  25 us (9%)
  waiting for transfers between devices  3.96 us (1%)
    another operation x1, other arithmetic  71 us
    all_gather x1, blocking collectives, per_device(): lax.all_gather(cycle_fourier, 'ba', axis=4, tiled=True)  33 us
    dot_general x1, matrix products, per_device(): jnp.einsum('mln,smpcn->smlpc', masked, coefficients, preferred_element_ty...  32.8 us
    all_gather x1, blocking collectives, per_device(): band_ratio = lax.all_gather(roughness, 'ba', axis=1, tiled=True).reshape(-1)  30.5 us
    all_gather x1, blocking collectives, per_device(): portion = lax.all_gather(wind_levels, 'ba', axis=2, tiled=True)  30.5 us
    ppermute x4, starting transfers between devices, with_halo(): lax.ppermute(lax.slice_in_dim(block, block.shape[dim] - width, None, axis...  18.2 us
    gather x2, local copies, waits for them, and re-layouts, per_device(): values = jnp.take(band_ratio, roughness_source)  11.8 us
    gather x3, local copies, waits for them, and re-layouts, per_device(): jnp.take_along_axis(repeated, jnp.broadcast_to(position[None], (2,) + pos...  10.8 us
  transfers between devices with their start and end apart: 9, of which 4 were waited for; matrix products, arithmetic and copies ran while one was open for 31% of the time, Pallas kernels for 0%

commit v1 on v0

v1 whole, which is shorter than its diff:
```python
import functools
import math

import jax
import jax.numpy as jnp
import numpy as np
from jax import lax
from jax.experimental import pallas as pl
from jax.experimental.pallas import tpu as pltpu
from jax.sharding import PartitionSpec as P

LON = 4096
NDIR = 36
NFREQ = 36
LANES = 128
PAD = 8

two_pi = 2.0 * math.pi
gravity = 9.81
base_freq = 0.04177
courant = 0.45
wind_scale = 10.0
growth = 0.05
dissipation = 0.5
energy_ref = 8.0
mid_freq = 0.2
stress_coef = 0.03
drag_coef = 0.0012
stress_floor = 0.02

bf16 = jnp.bfloat16
f32 = jnp.float32
SMEM_SPEC = pl.BlockSpec(memory_space=pltpu.SMEM)


def vmem_spec():
    return pl.BlockSpec(memory_space=pltpu.VMEM)


def params(parallel=1):
    return pltpu.CompilerParams(
        dimension_semantics=("arbitrary",) * parallel, vmem_limit_bytes=48 * 1024 * 1024
    )


def cost(flops, nbytes):
    return pl.CostEstimate(flops=flops, bytes_accessed=nbytes, transcendentals=0)


def legendre_kernel(
    shape, where_ref, leg_ref, coef_ref, out_ref, held
):
    n_aa, waves_local, cycles, pc, group, per_step, wave_lanes = shape
    step = pl.program_id(0)
    band = where_ref[0]
    band_cycles = cycles // n_aa
    per_block = LANES // group

    @pl.when(step == 0)
    def _():
        held[...] = jnp.zeros_like(held)

    lane = lax.broadcasted_iota(jnp.int32, (pc, LANES), 1)
    row_wave = lax.broadcasted_iota(jnp.int32, (group * cycles, wave_lanes), 0) // cycles
    degree = lax.broadcasted_iota(jnp.int32, (group * cycles, wave_lanes), 1)
    contract = (((1,), (1,)), ((), ()))
    for part in range(per_step):
        index = step * per_step + part
        leg_rows = pl.ds(part * group * cycles, group * cycles)
        coef_rows = pl.ds(part * group * pc, group * pc)
        first = band * waves_local + index * group
        low = leg_ref[leg_rows, :wave_lanes].astype(f32)
        low = jnp.where(degree >= row_wave + first, low, 0.0).astype(bf16)
        full = lax.dot_general(
            coef_ref[coef_rows, :wave_lanes], low, contract, preferred_element_type=f32
        ) + lax.dot_general(
            coef_ref[coef_rows, wave_lanes:],
            leg_ref[leg_rows, wave_lanes:],
            contract,
            preferred_element_type=f32,
        )
        own = jnp.zeros((pc, LANES), f32)
        for wave in range(group):
            own = own + jnp.where(lane // cycles == wave, full[wave * pc : (wave + 1) * pc], 0.0)
        block = index // per_block
        here = lane // group == index % per_block
        for cycle in range(cycles):
            source = (lane % group) * cycles + cycle
            piece = jnp.take_along_axis(own, source, axis=1)
            held[block, cycle] = jnp.where(here, piece, held[block, cycle])

    @pl.when(step == pl.num_programs(0) - 1)
    def _():
        for shift in range(n_aa):
            target = lax.rem(band + shift, n_aa)
            for cycle in range(band_cycles):
                for block in range(held.shape[0]):
                    out_ref[shift, cycle, :, block * LANES : (block + 1) * LANES] = held[
                        block, target * band_cycles + cycle
                    ].astype(bf16)


def legendre_sums(legendre, coefficients, band_index, n_aa):
    waves_local, cycles, degrees = legendre.shape
    pc = coefficients.shape[2] * coefficients.shape[3]
    group = LANES // cycles
    per_step = 32 // group if waves_local % 32 == 0 else 16 // group
    rows = group * per_step
    steps = waves_local // rows
    blocks = -(-waves_local // LANES)
    wave_lanes = -(-waves_local * n_aa // LANES) * LANES
    shape = (n_aa, waves_local, cycles, pc, group, per_step, wave_lanes)
    return pl.pallas_call(
        functools.partial(legendre_kernel, shape),
        grid=(steps,),
        in_specs=[
            SMEM_SPEC,
            pl.BlockSpec((rows * cycles, degrees), lambda i: (i, 0)),
            pl.BlockSpec((rows * pc, degrees), lambda i: (i, 0)),
        ],
        out_specs=pl.BlockSpec(
            (n_aa, cycles // n_aa, pc, blocks * LANES), lambda i: (0, 0, 0, 0)
        ),
        out_shape=jax.ShapeDtypeStruct((n_aa, cycles // n_aa, pc, blocks * LANES), bf16),
        scratch_shapes=[pltpu.VMEM((blocks, cycles, pc, LANES), f32)],
        compiler_params=params(),
        cost_estimate=cost(7_000_000_000, 20_000_000),
        name="legendre",
    )(
        band_index,
        legendre.reshape(waves_local * cycles, degrees),
        coefficients.reshape(waves_local * pc, degrees),
    )


def sine_cosine(wave, slot, points, inverse):
    product = wave * slot
    remain = product - jnp.floor(product * inverse + 0.5) * points
    turn = remain / points
    quarter = jnp.floor(4.0 * turn + 0.5)
    angle = (turn - 0.25 * quarter) * two_pi
    square = angle * angle
    sine = angle * (
        1.0
        + square
        * (-1.0 / 6.0 + square * (1.0 / 120.0 + square * (-1.0 / 5040.0 + square / 362880.0)))
    )
    cosine = 1.0 + square * (
        -0.5 + square * (1.0 / 24.0 + square * (-1.0 / 720.0 + square / 40320.0))
    )
    side = jnp.abs(quarter) == 1.0
    back = jnp.abs(quarter) == 2.0
    cosine_out = jnp.where(side, -quarter * sine, jnp.where(back, -cosine, cosine))
    sine_out = jnp.where(side, quarter * cosine, jnp.where(back, -sine, sine))
    return sine_out, cosine_out


def table_kernel(shape, where_ref, count_ref, slot_ref, out_ref, coarse):
    n_aa, waves_local, fine_rows = shape
    coarse_local = waves_local // fine_rows
    coarse_rows = coarse.shape[1]
    band = where_ref[0]
    cycle = pl.program_id(0)
    points = count_ref[cycle].astype(f32)
    slot = slot_ref[0]
    width = slot.shape[1]
    points_row = jnp.full((1, width), points, f32)
    inverse = 1.0 / points_row
    active = slot < points_row
    fine = lax.broadcasted_iota(jnp.int32, (fine_rows, width), 0).astype(f32)
    sine_fine, cosine_fine = sine_cosine(fine, slot, points_row, inverse)
    row = lax.broadcasted_iota(jnp.int32, (coarse_rows, width), 0)
    wave = jnp.zeros((coarse_rows, width), jnp.int32)
    for shift in range(n_aa):
        first = lax.rem(band - shift + n_aa, n_aa) * waves_local
        inside = (row >= shift * coarse_local) & (row < (shift + 1) * coarse_local)
        wave = jnp.where(inside, first + (row - shift * coarse_local) * fine_rows, wave)
    sine_coarse, cosine_coarse = sine_cosine(wave.astype(f32), slot, points_row, inverse)
    coarse[0] = jnp.where(active, 2.0 * cosine_coarse, 0.0)
    coarse[1] = jnp.where(active, 2.0 * sine_coarse, 0.0)
    for shift in range(n_aa):
        first = lax.rem(band - shift + n_aa, n_aa) * waves_local
        for step in range(coarse_local):
            at = shift * coarse_local + step
            cosine_at = coarse[0, at : at + 1, :]
            sine_at = coarse[1, at : at + 1, :]
            cosine_part = cosine_at * cosine_fine - sine_at * sine_fine
            sine_part = -(sine_at * cosine_fine + cosine_at * sine_fine)
            if step == 0:
                weight = jnp.where(fine + first.astype(f32) == 0.0, 0.5, 1.0)
                cosine_part = cosine_part * weight
                sine_part = sine_part * weight
            rows = slice(at * fine_rows, (at + 1) * fine_rows)
            out_ref[0, 0, rows, :] = cosine_part.astype(bf16)
            out_ref[0, 1, rows, :] = sine_part.astype(bf16)


def tables(slots, counts, band_index, n_aa, waves_local, name):
    cycles, width = slots.shape
    fine_rows = 32 if waves_local % 32 == 0 else 16
    waves = n_aa * waves_local
    coarse_rows = -(-(waves // fine_rows) // 8) * 8
    return pl.pallas_call(
        functools.partial(table_kernel, (n_aa, waves_local, fine_rows)),
        grid=(cycles,),
        in_specs=[
            SMEM_SPEC,
            SMEM_SPEC,
            pl.BlockSpec((1, 1, width), lambda i: (i, 0, 0)),
        ],
        out_specs=pl.BlockSpec((1, 2, waves, width), lambda i: (i, 0, 0, 0)),
        out_shape=jax.ShapeDtypeStruct((cycles, 2, waves, width), bf16),
        scratch_shapes=[pltpu.VMEM((2, coarse_rows, width), f32)],
        compiler_params=params(),
        cost_estimate=cost(cycles * waves * width * 500, cycles * waves * width * 4),
        name=name,
    )(band_index, counts, slots.reshape(cycles, 1, width))


def stack_rows(pieces):
    if pieces[0].shape[0] % 16 == 0:
        return jnp.concatenate(pieces, axis=0)
    return jnp.concatenate([piece.astype(f32) for piece in pieces], axis=0).astype(bf16)


def synthesis_kernel(shape, where_ref, *refs):
    n_aa, waves_local, n_out, n_in = shape
    fourier, (table_ref, out_ref) = refs[:n_in], refs[n_in:]
    column = where_ref[1]
    levels = out_ref.shape[2]
    pc = fourier[0].shape[3]
    cosine_sum = None
    sine_sum = None
    for shift in range(n_aa):
        left = stack_rows(
            [
                fourier[inner][outer, shift, 0, :, :waves_local]
                for inner in range(n_in)
                for outer in range(n_out)
            ]
        )
        rows = slice(shift * waves_local, (shift + 1) * waves_local)
        cosine_part = jnp.dot(left, table_ref[0, 0, rows, :], preferred_element_type=f32)
        sine_part = jnp.dot(left, table_ref[0, 1, rows, :], preferred_element_type=f32)
        cosine_sum = cosine_part if cosine_sum is None else cosine_sum + cosine_part
        sine_sum = sine_part if sine_sum is None else sine_sum + sine_part
    for inner in range(n_in):
        for outer in range(n_out):
            at = (inner * n_out + outer) * pc
            value = cosine_sum[at : at + levels] + sine_sum[at + levels : at + pc]
            source = jnp.bitwise_xor(column, outer * n_in + inner)
            out_ref[0, source] = value.astype(bf16)


def synthesis(fourier, table, where, n_aa, waves_local, n_in):
    n_out, _, cycles, pc, lanes = fourier[0].shape
    width = table.shape[3]
    levels = pc // 2
    n_ba = n_out * n_in
    block = pl.BlockSpec((n_out, n_aa, 1, pc, lanes), lambda i: (0, 0, i, 0, 0))
    return pl.pallas_call(
        functools.partial(synthesis_kernel, (n_aa, waves_local, n_out, n_in)),
        grid=(cycles,),
        in_specs=[SMEM_SPEC]
        + [block] * n_in
        + [pl.BlockSpec((1, 2, table.shape[2], width), lambda i: (i, 0, 0, 0))],
        out_specs=pl.BlockSpec((1, n_ba, levels, width), lambda i: (i, 0, 0, 0)),
        out_shape=jax.ShapeDtypeStruct((cycles, n_ba, levels, width), bf16),
        compiler_params=params(),
        cost_estimate=cost(1_500_000_000, 6_000_000),
        name="synthesis",
    )(where, *fourier, table)


def pick_kernel(shape, where_ref, *refs):
    n_aa, waves_local, n_out, n_in = shape
    fourier, (table_ref, out_ref) = refs[:n_in], refs[n_in:]
    column = where_ref[1]
    inner_at = lax.rem(column, n_in)
    outer_at = column // n_in
    cycles = out_ref.shape[0]
    pc = fourier[0].shape[3]
    levels = pc // 2
    for cycle in range(cycles):
        total = None
        for shift in range(n_aa):
            left = fourier[0][outer_at, shift, cycle].astype(f32)
            for inner in range(1, n_in):
                other = fourier[inner][outer_at, shift, cycle].astype(f32)
                left = jnp.where(inner_at == inner, other, left)
            left = left[:, :waves_local].astype(bf16)
            rows = slice(shift * waves_local, (shift + 1) * waves_local)
            cosine_part = jnp.dot(left, table_ref[cycle, 0, rows, :], preferred_element_type=f32)
            sine_part = jnp.dot(left, table_ref[cycle, 1, rows, :], preferred_element_type=f32)
            part = cosine_part[0:1] + sine_part[levels : levels + 1]
            total = part if total is None else total + part
        out_ref[cycle : cycle + 1, :] = wind_scale * total.astype(bf16).astype(f32)


def pick_winds(fourier, table, where, n_aa, waves_local, n_in):
    n_out, _, cycles, pc, lanes = fourier[0].shape
    width = table.shape[3]
    return pl.pallas_call(
        functools.partial(pick_kernel, (n_aa, waves_local, n_out, n_in)),
        in_specs=[SMEM_SPEC] + [vmem_spec()] * (n_in + 1),
        out_specs=vmem_spec(),
        out_shape=jax.ShapeDtypeStruct((cycles, width), f32),
        compiler_params=params(0),
        cost_estimate=cost(500_000_000, 2_000_000),
        name="pick",
    )(where, *fourier, table)


def bin_table(parts):
    bins = np.arange(NDIR * NFREQ)
    directions, freq_index = bins // NFREQ, bins % NFREQ
    heading = two_pi * (directions + 0.5) / NDIR
    period_ratio = np.exp(-math.log(1.1) * (35.0 / (NFREQ - 1)) * freq_index)
    frequency = base_freq / period_ratio
    drift_east = courant * period_ratio * np.cos(heading)
    drift_north = courant * period_ratio * np.sin(heading)
    inverse_speed = two_pi * frequency / gravity
    bin_width = 0.1 * frequency * (two_pi / NDIR)
    east_pos, east_neg = np.maximum(drift_east, 0.0), -np.minimum(drift_east, 0.0)
    north_pos, north_neg = np.maximum(drift_north, 0.0), -np.minimum(drift_north, 0.0)
    rows = [
        1.0 - east_pos - east_neg - north_pos - north_neg,
        east_pos,
        east_neg,
        north_pos,
        north_neg,
        np.cos(heading) * inverse_speed,
        np.sin(heading) * inverse_speed,
        bin_width,
        dissipation * (frequency / mid_freq),
    ]
    rows += [np.zeros_like(frequency)] * (16 - len(rows))
    table = np.stack(rows).astype(np.float32).reshape(16, parts, -1)
    return np.ascontiguousarray(table.transpose(1, 0, 2))


def advect_kernel(
    bins_ref, spectra_ref, mask_ref, low_ref, high_ref, west_ref, east_ref, out_ref, first, second
):
    rows, columns, bins = spectra_ref.shape
    wide = columns + 2 * PAD
    mask = jnp.transpose(mask_ref[...])
    lane = lax.broadcasted_iota(jnp.int32, mask.shape, 1)

    def column_mask(row):
        return jnp.sum(jnp.where(lane == row, mask, 0.0), axis=1, keepdims=True)[:columns]

    edge = jnp.zeros((PAD, bins), f32)
    for row in range(rows + 4):
        first[row, 0:PAD] = edge
        first[row, PAD + columns :] = edge
    masks = []
    for row in range(-2, rows + 2):
        if row < 0:
            block = low_ref[row + 2]
        elif row >= rows:
            block = high_ref[row - rows]
        else:
            own = column_mask(row)
            first[row + 2, PAD : PAD + columns] = spectra_ref[row] * own
            masks.append(own)
            continue
        first[row + 2, PAD : PAD + columns] = block[:, :bins]
        if row in (-1, rows):
            masks.append(block[:, bins : bins + 1])
    first[1 : rows + 3, PAD - 2 : PAD] = west_ref[:, :, :bins]
    first[1 : rows + 3, PAD + columns : PAD + columns + 2] = east_ref[:, :, :bins]
    keep, east_pos, east_neg = bins_ref[0:1], bins_ref[1:2], bins_ref[2:3]
    north_pos, north_neg = bins_ref[3:4], bins_ref[4:5]

    def update(source, at):
        centre = source[at]
        western = pltpu.roll(centre, 1, 0)
        eastern = pltpu.roll(centre, wide - 1, 0)
        return (
            keep * centre
            + east_pos * western
            + east_neg * eastern
            + north_pos * source[at - 1]
            + north_neg * source[at + 1]
        )

    for row in range(rows + 2):
        value = update(first, row + 1)
        second[row, 0:PAD] = value[0:PAD]
        second[row, PAD : PAD + columns] = value[PAD : PAD + columns] * masks[row]
        second[row, PAD + columns :] = value[PAD + columns :]
        second[row, PAD - 1 : PAD] = (
            value[PAD - 1 : PAD] * west_ref[row, 1:2, bins : bins + 1]
        )
        second[row, PAD + columns : PAD + columns + 1] = (
            value[PAD + columns : PAD + columns + 1] * east_ref[row, 0:1, bins : bins + 1]
        )
    for row in range(rows):
        value = update(second, row + 1)
        out_ref[row] = value[PAD : PAD + columns] * masks[row + 1]


def advect(bins, spectra, mask, low, high, west, east):
    rows, columns, count = spectra.shape
    wide = columns + 2 * PAD
    padded = jnp.pad(mask, ((0, LANES - rows), (0, LANES - columns)))
    return pl.pallas_call(
        advect_kernel,
        in_specs=[vmem_spec()] * 7,
        out_specs=vmem_spec(),
        out_shape=jax.ShapeDtypeStruct(spectra.shape, f32),
        scratch_shapes=[
            pltpu.VMEM((rows + 4, wide, count), f32),
            pltpu.VMEM((rows + 2, wide, count), f32),
        ],
        compiler_params=params(0),
        cost_estimate=cost(2_000_000_000, 4_000_000),
        name="advect",
    )(bins, spectra, padded, low, high, west, east)


def halo(spectra, mask):
    def packed(part, part_mask):
        return jnp.concatenate([part * part_mask[:, :, None], part_mask[:, :, None]], axis=2)

    def shifted(low_side, high_side, axis):
        count = lax.axis_size(axis)
        index = lax.axis_index(axis)
        if count == 2:
            sent = jnp.where(index == 0, high_side, low_side)
            got = lax.ppermute(sent, axis, [(0, 1), (1, 0)])
            return jnp.where(index == 1, got, 0.0), jnp.where(index == 0, got, 0.0)
        forward = [(i, i + 1) for i in range(count - 1)]
        backward = [(target, source) for source, target in forward]
        return lax.ppermute(high_side, axis, forward), lax.ppermute(low_side, axis, backward)

    low, high = shifted(
        packed(spectra[:2], mask[:2]), packed(spectra[-2:], mask[-2:]), "aa"
    )
    sides = []
    for cut in (slice(0, 2), slice(-2, None)):
        own = packed(spectra[:, cut], mask[:, cut])
        sides.append(jnp.concatenate([low[1:, cut], own, high[:1, cut]], axis=0))
    west, east = shifted(sides[0], sides[1], "ba")
    return low, high, west, east


def winds_of(where_ref, own_ref, other_ref):
    first_component = where_ref[2] == 0
    own, other = own_ref[...], other_ref[...]
    return jnp.where(first_component, own, other), jnp.where(first_component, other, own)


def as_columns(rows_by_lanes):
    rows = rows_by_lanes.shape[0]
    if rows % 8:
        rows_by_lanes = jnp.concatenate(
            [rows_by_lanes, jnp.zeros((8 - rows % 8, LANES), f32)], axis=0
        )
    return jnp.transpose(rows_by_lanes)


def stress_kernel(where_ref, bins_ref, density_ref, own_ref, other_ref, out_ref):
    cycles = own_ref.shape[0]
    rows, columns, bins = density_ref.shape
    cycle_rows = rows // cycles
    east, north = winds_of(where_ref, own_ref, other_ref)
    east, north = as_columns(east), as_columns(north)
    along_cos, along_sin, width = bins_ref[5:6], bins_ref[6:7], bins_ref[7:8]
    lane = lax.broadcasted_iota(jnp.int32, (LANES, LANES), 1)
    sums = jnp.zeros((LANES, LANES), f32)
    for cycle in range(cycles):
        density = density_ref[cycle * cycle_rows : (cycle + 1) * cycle_rows].reshape(LANES, bins)
        alignment = (
            east[:, cycle : cycle + 1] * along_cos + north[:, cycle : cycle + 1] * along_sin
        )
        weighted = density * width
        gain = growth * jnp.maximum(alignment - 1.0, 0.0)
        energy = jnp.sum(weighted, axis=1, keepdims=True)
        stress = jnp.sum(gain * alignment * weighted, axis=1, keepdims=True)
        sums = jnp.where(lane == cycle, stress, sums)
        sums = jnp.where(lane == cycles + cycle, energy, sums)
    out_ref[...] = jnp.transpose(sums)[: 2 * cycles]


def stress_sums(where, bins, density, own, other):
    cycles = own.shape[0]
    return pl.pallas_call(
        stress_kernel,
        in_specs=[SMEM_SPEC] + [vmem_spec()] * 4,
        out_specs=vmem_spec(),
        out_shape=jax.ShapeDtypeStruct((2 * cycles, LANES), f32),
        compiler_params=params(0),
        cost_estimate=cost(500_000_000, 2_000_000),
        name="stress",
    )(where, bins, density, own, other)


def spectra_kernel(where_ref, bins_ref, density_ref, own_ref, other_ref, energy_ref_, out_ref):
    cycles = own_ref.shape[0]
    rows, columns, bins = density_ref.shape
    cycle_rows = rows // cycles
    east, north = winds_of(where_ref, own_ref, other_ref)
    east, north = as_columns(east), as_columns(north)
    scaled = energy_ref_[...] * (1.0 / energy_ref)
    energy = as_columns(scaled * scaled)
    along_cos, along_sin, decay = bins_ref[5:6], bins_ref[6:7], bins_ref[8:9]
    for cycle in range(cycles):
        at = slice(cycle * cycle_rows, (cycle + 1) * cycle_rows)
        density = density_ref[at].reshape(LANES, bins)
        alignment = (
            east[:, cycle : cycle + 1] * along_cos + north[:, cycle : cycle + 1] * along_sin
        )
        gain = growth * jnp.maximum(alignment - 1.0, 0.0)
        value = density * (1.0 + gain) / (1.0 + decay * energy[:, cycle : cycle + 1])
        out_ref[at] = value.reshape(cycle_rows, columns, bins)


def final_spectra(where, bins, density, own, other, energy):
    return pl.pallas_call(
        spectra_kernel,
        in_specs=[SMEM_SPEC] + [vmem_spec()] * 5,
        out_specs=vmem_spec(),
        out_shape=jax.ShapeDtypeStruct(density.shape, f32),
        compiler_params=params(0),
        cost_estimate=cost(500_000_000, 3_000_000),
        name="spectra",
    )(where, bins, density, own, other, energy)


def charnock_kernel(
    shape, where_ref, count_ref, rough_ref, source_ref, out_ref
):
    columns_local, total_columns = shape
    column = where_ref[1]
    pieces, cycles, _ = rough_ref.shape
    width = source_ref.shape[1]
    cycle_rows = LANES // columns_local
    base = column * width
    row = lax.broadcasted_iota(jnp.int32, (cycles, LANES), 0)
    points = jnp.zeros((cycles, LANES), jnp.int32)
    for cycle in range(cycles):
        points = jnp.where(row == cycle, count_ref[cycle], points)
    lane = lax.broadcasted_iota(jnp.int32, (cycles, LANES), 1)
    for part in range(width // LANES):
        at = slice(part * LANES, (part + 1) * LANES)
        source = source_ref[:, at]
        band_row = source // total_columns
        source_column = source - band_row * total_columns
        owner = source_column // columns_local
        within = (band_row - row * cycle_rows) * columns_local + (
            source_column - owner * columns_local
        )
        within = jnp.clip(within, 0, LANES - 1)
        value = jnp.zeros((cycles, LANES), f32)
        for piece in range(pieces):
            found = jnp.take_along_axis(rough_ref[piece], within, axis=1)
            value = jnp.where(owner == jnp.bitwise_xor(column, piece), found, value)
        out_ref[:, at] = jnp.where(lane + (base + part * LANES) < points, value, 0.0)


def charnock_of(where, counts, pieces, source, columns_local):
    return pl.pallas_call(
        functools.partial(charnock_kernel, (columns_local, columns_local * pieces.shape[0])),
        in_specs=[SMEM_SPEC, SMEM_SPEC] + [vmem_spec()] * 2,
        out_specs=vmem_spec(),
        out_shape=jax.ShapeDtypeStruct(source.shape, f32),
        compiler_params=params(0),
        cost_estimate=cost(100_000_000, 100_000),
        name="charnock",
    )(where, counts, pieces, source)


def exchange(value, axis, distance):
    count = lax.axis_size(axis)
    return lax.ppermute(value, axis, [(i, i ^ distance) for i in range(count)])


def per_device(
    legendre, coefficients, cycle_points, spectra, sea_mask, wind_column, roughness_source
):
    n_aa, n_ba = lax.axis_size("aa"), lax.axis_size("ba")
    n_comp = lax.axis_size("comp")
    band_index = lax.axis_index("aa")
    column_index = lax.axis_index("ba")
    half_index = lax.axis_index("comp")
    where = jnp.stack([band_index, column_index, half_index]).astype(jnp.int32)
    waves_local, cycles_all, _ = legendre.shape
    cycles = cycles_all // n_aa
    rows_local, columns_local, _ = spectra.shape
    cycle_rows = rows_local // cycles
    n_in = 2
    n_out = n_ba // n_in
    slots_local = LON // n_ba
    counts = lax.dynamic_slice_in_dim(cycle_points, band_index * cycles, cycles)
    bins = lax.dynamic_index_in_dim(jnp.asarray(bin_table(n_comp)), half_index, 0, keepdims=False)

    fourier = legendre_sums(legendre, coefficients, where, n_aa)

    mask = sea_mask.astype(f32)
    low, high, west, east = halo(spectra, mask)
    density = advect(bins, spectra, mask, low, high, west, east)

    own_slots = column_index * slots_local + jnp.arange(slots_local, dtype=jnp.int32)
    own_slots = jnp.broadcast_to(own_slots[None].astype(f32), (cycles, slots_local))
    wind_slots = lax.dynamic_slice_in_dim(
        wind_column, column_index * columns_local, columns_local, 1
    )
    wind_slots = wind_slots.astype(f32).reshape(cycles, cycle_rows * columns_local)
    wind_table = tables(wind_slots, counts, where, n_aa, waves_local, "wind_tables")
    grid_table = tables(own_slots, counts, where, n_aa, waves_local, "grid_tables")

    parts = [fourier[0]]
    for shift in range(1, n_aa):
        pairs = [(i, (i + shift) % n_aa) for i in range(n_aa)]
        parts.append(lax.ppermute(fourier[shift], "aa", pairs))
    parts = jnp.stack(parts)
    outer = [parts] + [exchange(parts, "ba", n_in * k) for k in range(1, n_out)]
    outer = jnp.stack(outer)
    inner = [outer] + [exchange(outer, "ba", k) for k in range(1, n_in)]

    own = pick_winds(inner, wind_table, where, n_aa, waves_local, n_in)
    other = exchange(own, "comp", 1)
    sums = stress_sums(where, bins, density, own, other)
    sums = sums + exchange(sums, "comp", 1)
    air = drag_coef * (own * own + other * other) + stress_floor
    roughness = jnp.sqrt(1.0 + stress_coef * sums[:cycles] / air)
    pieces = roughness[None]
    distance = 1
    while distance < n_ba:
        pieces = jnp.concatenate([pieces, exchange(pieces, "ba", distance)], axis=0)
        distance *= 2
    wave_spectra = final_spectra(where, bins, density, own, other, sums[cycles:])
    grid_winds = synthesis(inner, grid_table, where, n_aa, waves_local, n_in)
    grid_winds = grid_winds.reshape(1, cycles, -1, slots_local)
    charnock = charnock_of(where, counts, pieces, roughness_source, columns_local)
    return (grid_winds, wave_spectra, charnock)


def solution(mesh):
    in_specs = (
        P("aa", None, None),
        P("comp", "aa", None, "ba", None),
        P(),
        P("aa", "ba", "comp"),
        P("aa", "ba"),
        P("aa", None),
        P("aa", "ba"),
    )
    out_specs = (P("comp", "aa", None, "ba"), P("aa", "ba", "comp"), P("aa", "ba"))
    return jax.shard_map(
        per_device, mesh=mesh, in_specs=in_specs, out_specs=out_specs, check_vma=False
    )
```

time: 274 us -> 64.1 us (0.23)
  blocking collectives: 99.2 us -> 0 us
  other arithmetic: 80.7 us -> 0.81 us
  matrix products: 35.5 us -> 0 us
  Pallas kernels: 0 us -> 28.7 us
  local copies, waits for them, and re-layouts: 25 us -> 0.9 us
  waiting for transfers between devices: 3.96 us -> 16.4 us
  starting transfers between devices: 27.6 us -> 16.2 us
    all_gather x4 -> x0, blocking collectives: 95.9 us -> none  [the longest x1 33 us: per_device(): lax.all_gather(cycle_fourier, 'ba', axis=4, tiled=True)]
    another operation x1 -> x3, other arithmetic: 71 us -> 0.16 us  [the longest x2 0.08 us: per_device(): outer = jnp.stack(outer)]
    dot_general x2 -> x0, matrix products: 35.5 us -> none  [the longest x1 32.8 us: per_device(): jnp.einsum('mln,smpcn->smlpc', masked, coefficients, preferred_element_ty...]
    pallas_call x0 -> x9, Pallas kernels: none -> 28.7 us  [the longest x1 12.1 us: legendre_sums(): pl.pallas_call(functools.partial(legendre_kernel, shape), grid=(steps,),...]
    gather x5 -> x0, local copies, waits for them, and re-layouts: 22.6 us -> none  [the longest x2 11.8 us: per_device(): values = jnp.take(band_ratio, roughness_source)]
    ppermute x8 -> x13, waiting for transfers between devices: 3.96 us -> 16.4 us  [the longest x9 14.8 us: exchange(): return lax.ppermute(value, axis, [(i, i ^ distance) for i in range(count)])]
    ppermute x8 -> x13, starting transfers between devices: 23.4 us -> 16.2 us  [the longest x9 9.31 us: exchange(): return lax.ppermute(value, axis, [(i, i ^ distance) for i in range(count)])]
    all_to_all x1 -> x0, starting transfers between devices: 4.26 us -> none  [per_device(): lax.all_to_all(partial_fourier, 'aa', split_axis=2, concat_axis=1, tiled=...]
  transfers between devices with their start and end apart: 9 -> 13, of which waited for: 4 -> 8; matrix products, arithmetic and copies ran while one was open for 31% -> 2% of each run, Pallas kernels for 0% -> 22%
where the time goes in v1:
time: 64.1 us; the launch traced here: 63.9 us
  Pallas kernels  28.7 us (45%)
  waiting for transfers between devices  16.4 us (26%)
  starting transfers between devices  16.2 us (25%)
  local copies, waits for them, and re-layouts  0.9 us (1%)
  between operations  0.85 us (1%)
  other arithmetic  0.81 us (1%)
    ppermute x9, waiting for transfers between devices, exchange(): return lax.ppermute(value, axis, [(i, i ^ distance) for i in range(count)])  14.8 us
    pallas_call x1, Pallas kernels, legendre_sums(): pl.pallas_call(functools.partial(legendre_kernel, shape), grid=(steps,),...  12.1 us
    ppermute x9, starting transfers between devices, exchange(): return lax.ppermute(value, axis, [(i, i ^ distance) for i in range(count)])  9.31 us
    pallas_call x2, Pallas kernels, tables(): pl.pallas_call(functools.partial(table_kernel, (n_aa, waves_local, fine_r...  4.46 us
    pallas_call x1, Pallas kernels, synthesis(): pl.pallas_call(functools.partial(synthesis_kernel, (n_aa, waves_local, n_...  3.25 us
    ppermute x1, starting transfers between devices, per_device(): parts.append(lax.ppermute(fourier[shift], 'aa', pairs))  3.05 us
    pallas_call x1, Pallas kernels, advect(): pl.pallas_call(advect_kernel, in_specs=[vmem_spec()] * 7, out_specs=vmem_...  2.65 us
    pallas_call x1, Pallas kernels, final_spectra(): pl.pallas_call(spectra_kernel, in_specs=[SMEM_SPEC] + [vmem_spec()] * 5,...  2.53 us
  transfers between devices with their start and end apart: 13, of which 8 were waited for; matrix products, arithmetic and copies ran while one was open for 2% of the time, Pallas kernels for 22%

profile of v1, /device:TPU:0, one launch (start us, length us, event | category | flops | bytes accessed | tf_op | source)
XLA Modules:
  0.0 63.9 jit_solution(12559425476401524273)
XLA Ops:
  0.6 0.1 pad_add_fusion.where_ref
  0.7 12.1 %legendre.1 = bf16[2,4,16,384]{3,2,1,0:T(8,128)(2,1)S(1)} custom-call(s32[3]{0:T(128)S(1)} %pad_add_fusion.where_ref, bf16[2560,1280]{1,0:T(8,128)(2,1)} %bitcast.32, bf16[5120,1280]{1,0:T(8,128)(2,1)} %bitcast.31), custom_call_target="tpu_custom_call" | custom-call | flops 7000000000 | bytes 20000000 | tf_op jit(solution)/shard_map/legendre/pallas_call | solution.py:113
  12.8 0.0 copy-start.2
  12.8 3.0 %collective-permute-start = (bf16[4,16,384]{2,1,0:T(8,128)(2,1)S(1)}, bf16[4,16,384]{2,1,0:T(8,128)(2,1)S(1)}, u32[]{:S(2)}, u32[]{:S(2)}) collective-permute-start(bf16[4,16,384]{2,1,0:T(8,128)(2,1)S(1)} %get-tuple-element.16), channel_id=1, source_target_pairs={{0,8},{8,0},{1,9},{9,1},{2,10},{10,2},{3,11},{11,3},{4,12},{12,4},... | collective-permute-start | bytes 147464 | tf_op jit(solution)/shard_map/ppermute | solution.py:617
  15.9 0.1 copy.11
  16.0 0.1 copy.12
  16.1 0.1 slice_multiply_fusion
  16.2 0.1 maximum_select_fusion
  16.3 0.0 copy-start.4
  16.3 0.0 copy-start.5
  16.3 0.1 collective-permute-start.5
  16.4 0.1 fusion.4
  16.5 0.1 slice_multiply_fusion.2
  16.6 1.4 %collective-permute-done = bf16[4,16,384]{2,1,0:T(8,128)(2,1)S(1)} collective-permute-done((bf16[4,16,384]{2,1,0:T(8,128)(2,1)S(1)}, bf16[4,16,384]{2,1,0:T(8,128)(2,1)S(1)}, u32[]{:S(2)}, u32[]{:S(2)}) %collective-permute-start) | collective-permute-done | bytes 49184 | tf_op jit(solution)/shard_map/ppermute | solution.py:617
  18.0 4.1 %collective-permute-start.3 = (bf16[2,4,16,384]{3,2,1,0:T(8,128)(2,1)S(1)}, bf16[2,4,16,384]{3,2,1,0:T(8,128)(2,1)S(1)}, u32[]{:S(2)}, u32[]{:S(2)}) collective-permute-start(bf16[2,4,16,384]{3,2,1,0:T(8,128)(2,1)S(1)} %get-tuple-element.14), channel_id=1, source_target_pairs={{0,6},{1,7},{2,4},{3,5},{4,2},{5,3},{6,0},{7,1},{8,14},{9,15},{10,... | collective-permute-start | bytes 294920 | tf_op jit(solution)/shard_map/ppermute | solution.py:577
  22.2 0.6 %collective-permute-start.1 = (bf16[2,4,16,384]{3,2,1,0:T(8,128)(2,1)S(1)}, bf16[2,4,16,384]{3,2,1,0:T(8,128)(2,1)S(1)}, u32[]{:S(2)}, u32[]{:S(2)}) collective-permute-start(bf16[2,4,16,384]{3,2,1,0:T(8,128)(2,1)S(1)} %get-tuple-element.14), channel_id=1, source_target_pairs={{0,2},{1,3},{2,0},{3,1},{4,6},{5,7},{6,4},{7,5},{8,10},{9,11},{10,... | collective-permute-start | bytes 294920 | tf_op jit(solution)/shard_map/ppermute | solution.py:577
  22.8 0.2 copy.14
  23.0 0.2 copy.16
  23.2 2.0 %collective-permute-done.3 = bf16[2,4,16,384]{3,2,1,0:T(8,128)(2,1)S(1)} collective-permute-done((bf16[2,4,16,384]{3,2,1,0:T(8,128)(2,1)S(1)}, bf16[2,4,16,384]{3,2,1,0:T(8,128)(2,1)S(1)}, u32[]{:S(2)}, u32[]{:S(2)}) %collective-permute-start.3) | collective-permute-done | bytes 98336 | tf_op jit(solution)/shard_map/ppermute | solution.py:577
  25.2 4.1 %collective-permute-done.2 = bf16[2,4,16,384]{3,2,1,0:T(8,128)(2,1)S(1)} collective-permute-done((bf16[2,4,16,384]{3,2,1,0:T(8,128)(2,1)S(1)}, bf16[2,4,16,384]{3,2,1,0:T(8,128)(2,1)S(1)}, u32[]{:S(2)}, u32[]{:S(2)}) %collective-permute-start.2) | collective-permute-done | bytes 98336 | tf_op jit(solution)/shard_map/ppermute | solution.py:577
  29.4 0.0 collective-permute-done.1
  29.4 0.1 pad_maximum_fusion.refs_0_
  29.4 1.6 %collective-permute-start.4 = (bf16[4,2,4,16,384]{4,3,2,1,0:T(8,128)(2,1)S(1)}, bf16[4,2,4,16,384]{4,3,2,1,0:T(8,128)(2,1)S(1)}, u32[]{:S(2)}, u32[]{:S(2)}) collective-permute-start(bf16[4,2,4,16,384]{4,3,2,1,0:T(8,128)(2,1)S(1)} %pad_maximum_fusion.refs_0_), channel_id=1, source_target_pairs={{0,1},{1,0},{2,3},{3,2},{4,5},{5,4},{6,7},{7,6},{8,9},{9,8},{10,11... | collective-permute-start | bytes 1179656 | tf_op jit(solution)/shard_map/ppermute | solution.py:577
  31.0 0.1 pad_maximum_fusion.1
  31.1 2.4 %collective-permute-start.6 = (f32[18,2,649]{2,1,0:T(2,128)S(1)}, f32[18,2,649]{2,1,0:T(2,128)S(1)}, u32[]{:S(2)}, u32[]{:S(2)}) collective-permute-start(f32[18,2,649]{2,1,0:T(2,128)S(1)} %pad_maximum_fusion.1), channel_id=1, source_target_pairs={{0,1},{1,2},{2,3},{3,4},{4,5},{5,6},{6,7},{8,9},{9,10},{10,11},{11... | collective-permute-start | bytes 280376 | tf_op jit(solution)/shard_map/ppermute | solution.py:436
  33.6 0.1 pad_maximum_fusion.2
  33.7 1.3 %collective-permute-start.7 = (f32[18,2,649]{2,1,0:T(2,128)S(1)}, f32[18,2,649]{2,1,0:T(2,128)S(1)}, u32[]{:S(2)}, u32[]{:S(2)}) collective-permute-start(f32[18,2,649]{2,1,0:T(2,128)S(1)} %pad_maximum_fusion.2), channel_id=1, source_target_pairs={{1,0},{2,1},{3,2},{4,3},{5,4},{6,5},{7,6},{9,8},{10,9},{11,10},{12... | collective-permute-start | bytes 280376 | tf_op jit(solution)/shard_map/ppermute | solution.py:436
  35.0 0.1 dynamic-slice_convert_fusion
  35.1 0.1 reshape_reshape.3.slot_ref
  35.2 0.1 dynamic_slice.10.count_ref
  35.2 1.2 %wind_tables.1.refs_2_ = bf16[4,2,640,128]{3,2,1,0:T(8,128)(2,1)S(1)} custom-call(s32[3]{0:T(128)S(1)} %pad_add_fusion.where_ref, s32[4]{0:T(128)S(1)} %dynamic_slice.10.count_ref, f32[4,1,128]{2,1,0:T(1,128)S(1)} %reshape_reshape.3.slot_ref), custom_call_target="tpu_custom_call" | custom-call | flops 163840000 | bytes 1310720 | tf_op jit(solution)/shard_map/wind_tables/pallas_call | solution.py:203
  36.5 5.4 %collective-permute-done.4.refs_1_ = bf16[4,2,4,16,384]{4,3,2,1,0:T(8,128)(2,1)S(1)} collective-permute-done((bf16[4,2,4,16,384]{4,3,2,1,0:T(8,128)(2,1)S(1)}, bf16[4,2,4,16,384]{4,3,2,1,0:T(8,128)(2,1)S(1)}, u32[]{:S(2)}, u32[]{:S(2)}) %collective-permute-start.4) | collective-permute-done | bytes 393248 | tf_op jit(solution)/shard_map/ppermute | solution.py:577
  41.8 0.9 %pick.1.own_ref = f32[4,128]{1,0:T(4,128)S(1)} custom-call(s32[3]{0:T(128)S(1)} %pad_add_fusion.where_ref, bf16[4,2,4,16,384]{4,3,2,1,0:T(8,128)(2,1)S(1)} %pad_maximum_fusion.refs_0_, bf16[4,2,4,16,384]{4,3,2,1,0:T(8,128)(2,1)S(1)} %collective-permute-done.4.refs_1_, bf16[4,2,640,128]{3,2,1,0:T(8,128)(2,1)S(1)} %wind_tables.1.refs_2_), custom_call_target="tpu_custom_call" | custom-call | flops 500000000 | bytes 2000000 | tf_op jit(solution)/shard_map/pick/pallas_call | solution.py:303
  42.7 0.1 collective-permute-start.8
  42.8 0.2 collective-permute-done.6.west_ref
  43.0 2.7 %advect.1.density_ref = f32[16,32,648]{2,1,0:T(8,128)S(1)} custom-call(f32[16,648]{1,0:T(8,128)S(1)} %dynamic-slice_bitcast_fusion.bins_ref, f32[16,32,648]{2,1,0:T(8,128)S(1)} %copy-done, f32[128,128]{1,0:T(8,128)S(1)} %pad.4.mask_ref, f32[2,32,649]{2,1,0:T(8,128)S(1)} %get-tuple-element.12.low_ref, f32[2,32,649]{2,1,0:T(8,128)S(1)} %get-tuple-element.11.high_ref, ...), custom_call_target="tpu_custom_call" | custom-call | flops 2000000000 | bytes 4000000 | tf_op jit(solution)/shard_map/advect/pallas_call | solution.py:408
  45.7 1.6 %stress.1 = f32[8,128]{1,0:T(8,128)S(1)} custom-call(s32[3]{0:T(128)S(1)} %pad_add_fusion.where_ref, f32[16,648]{1,0:T(8,128)S(1)} %dynamic-slice_bitcast_fusion.bins_ref, f32[16,32,648]{2,1,0:T(8,128)S(1)} %advect.1.density_ref, f32[4,128]{1,0:T(4,128)S(1)} %pick.1.own_ref, f32[4,128]{1,0:T(4,128)S(1)} %collective-permute-done.8.other_ref), custom_call_target="tpu_custom_call" | custom-call | flops 500000000 | bytes 2000000 | tf_op jit(solution)/shard_map/stress/pallas_call | solution.py:489
  47.3 0.3 collective-permute-start.9
  47.6 0.9 %collective-permute-done.9 = f32[8,128]{1,0:T(8,128)S(1)} collective-permute-done((f32[8,128]{1,0:T(8,128)S(1)}, f32[8,128]{1,0:T(8,128)S(1)}, u32[]{:S(2)}, u32[]{:S(2)}) %collective-permute-start.9) | collective-permute-done | bytes 4128 | tf_op jit(solution)/shard_map/ppermute | solution.py:577
  48.5 2.5 %collective-permute-start.10 = (f32[1,4,128]{2,1,0:T(4,128)S(1)}, f32[1,4,128]{2,1,0:T(4,128)S(1)}, u32[]{:S(2)}, u32[]{:S(2)}) collective-permute-start(f32[1,4,128]{2,1,0:T(4,128)S(1)} %get-tuple-element.25), channel_id=1, source_target_pairs={{0,1},{1,0},{2,3},{3,2},{4,5},{5,4},{6,7},{7,6},{8,9},{9,8},{10,11... | collective-permute-start | bytes 6152 | tf_op jit(solution)/shard_map/ppermute | solution.py:577
  51.1 3.2 %grid_tables.1.refs_2_ = bf16[4,2,640,512]{3,2,1,0:T(8,128)(2,1)S(1)} custom-call(s32[3]{0:T(128)S(1)} %pad_add_fusion.where_ref, s32[4]{0:T(128)S(1)} %dynamic_slice.10.count_ref, f32[4,1,512]{2,1,0:T(1,128)S(1)} %reshape.30.slot_ref), custom_call_target="tpu_custom_call" | custom-call | flops 655360000 | bytes 5242880 | tf_op jit(solution)/shard_map/grid_tables/pallas_call | solution.py:203
  54.3 0.1 collective-permute-start.11
  54.4 3.2 %synthesis.1 = bf16[4,8,8,512]{3,2,1,0:T(8,128)(2,1)} custom-call(s32[3]{0:T(128)S(1)} %pad_add_fusion.where_ref, bf16[4,2,4,16,384]{4,3,2,1,0:T(8,128)(2,1)S(1)} %pad_maximum_fusion.refs_0_, bf16[4,2,4,16,384]{4,3,2,1,0:T(8,128)(2,1)S(1)} %collective-permute-done.4.refs_1_, bf16[4,2,640,512]{3,2,1,0:T(8,128)(2,1)S(1)} %grid_tables.1.refs_2_), custom_call_target="tpu_custom_call" | custom-call | flops 1500000000 | bytes 6000000 | tf_op jit(solution)/shard_map/synthesis/pallas_call | solution.py:261
  57.7 0.3 collective-permute-done.11
  58.0 0.0 copy-start.1
  58.0 2.5 %spectra.1 = f32[16,32,648]{2,1,0:T(8,128)} custom-call(s32[3]{0:T(128)S(1)} %pad_add_fusion.where_ref, f32[16,648]{1,0:T(8,128)S(1)} %dynamic-slice_bitcast_fusion.bins_ref, f32[16,32,648]{2,1,0:T(8,128)S(1)} %advect.1.density_ref, f32[4,128]{1,0:T(4,128)S(1)} %pick.1.own_ref, f32[4,128]{1,0:T(4,128)S(1)} %collective-permute-done.8.other_ref, ...), custom_call_target="tpu_custom_call" | custom-call | flops 500000000 | bytes 3000000 | tf_op jit(solution)/shard_map/spectra/pallas_call | solution.py:521
  60.6 2.0 %collective-permute-done.12 = f32[4,4,128]{2,1,0:T(4,128)S(1)} collective-permute-done((f32[4,4,128]{2,1,0:T(4,128)S(1)}, f32[4,4,128]{2,1,0:T(4,128)S(1)}, u32[]{:S(2)}, u32[]{:S(2)}) %collective-permute-start.12) | collective-permute-done | bytes 8224 | tf_op jit(solution)/shard_map/ppermute | solution.py:577
  62.6 1.3 %charnock.1 = f32[4,512]{1,0:T(4,128)} custom-call(s32[3]{0:T(128)S(1)} %pad_add_fusion.where_ref, s32[4]{0:T(128)S(1)} %dynamic_slice.10.count_ref, f32[8,4,128]{2,1,0:T(4,128)S(1)} %pad_maximum_fusion.4.rough_ref, s32[4,512]{1,0:T(4,128)S(1)} %copy-done.1), custom_call_target="tpu_custom_call" | custom-call | flops 100000000 | bytes 100000 | tf_op jit(solution)/shard_map/charnock/pallas_call | solution.py:564
  (29 shorter events, 0.2 us)
Async XLA Ops:
  0.7 15.2 %copy-start.3 = (s32[16,32]{1,0:T(8,128)S(1)}, s32[16,32]{1,0:T(8,128)}, u32[]{:S(2)}) copy-start(s32[16,32]{1,0:T(8,128)} %param.12) | copy-start | bytes 6148
  0.7 15.4 %copy-start = (f32[16,32,648]{2,1,0:T(8,128)S(1)}, f32[16,32,648]{2,1,0:T(8,128)}, u32[]{:S(2)}) copy-start(f32[16,32,648]{2,1,0:T(8,128)} %spectra_ref.1) | copy-start | bytes 3981316
  12.8 10.0 %copy-start.2 = (f32[2,16,648]{2,1,0:T(8,128)S(1)}, f32[2,16,648]{2,1,0:T(8,128)}, u32[]{:S(2)}) copy-start(f32[2,16,648]{2,1,0:T(8,128)} %constant.45.clone) | copy-start | bytes 248836
  12.8 5.2 %collective-permute-start = (bf16[4,16,384]{2,1,0:T(8,128)(2,1)S(1)}, bf16[4,16,384]{2,1,0:T(8,128)(2,1)S(1)}, u32[]{:S(2)}, u32[]{:S(2)}) collective-permute-start(bf16[4,16,384]{2,1,0:T(8,128)(2,1)S(1)} %get-tuple-element.16), channel_id=1, source_target_pairs={{0,8},{8,0},{1,9},{9,1},{2,10},{10,2},{3,11},{11,3},{4,12},{12,4},... | collective-permute-start | bytes 147464 | tf_op jit(solution)/shard_map/ppermute | solution.py:617
  16.3 18.7 %copy-start.4 = (s32[16,256]{1,0:T(8,128)S(1)}, s32[16,256]{1,0:T(8,128)}, u32[]{:S(2)}) copy-start(s32[16,256]{1,0:T(8,128)} %param.13) | copy-start | bytes 49156
  16.3 18.9 %copy-start.5 = (s32[8]{0:T(128)S(1)}, s32[8]{0:T(128)}, u32[]{:S(2)}) copy-start(s32[8]{0:T(128)} %param.10) | copy-start | bytes 100
  16.3 14.7 %collective-permute-start.5 = (f32[2,32,649]{2,1,0:T(8,128)S(1)}, f32[2,32,649]{2,1,0:T(8,128)S(1)}, u32[]{:S(2)}, u32[]{:S(2)}) collective-permute-start(f32[2,32,649]{2,1,0:T(8,128)S(1)} %maximum_select_fusion), channel_id=1, source_target_pairs={{0,8},{8,0},{1,9},{9,1},{2,10},{10,2},{3,11},{11,3},{4,12},{12,4},... | collective-permute-start | bytes 498440 | tf_op jit(solution)/shard_map/ppermute | solution.py:432
  18.0 7.2 %collective-permute-start.3 = (bf16[2,4,16,384]{3,2,1,0:T(8,128)(2,1)S(1)}, bf16[2,4,16,384]{3,2,1,0:T(8,128)(2,1)S(1)}, u32[]{:S(2)}, u32[]{:S(2)}) collective-permute-start(bf16[2,4,16,384]{3,2,1,0:T(8,128)(2,1)S(1)} %get-tuple-element.14), channel_id=1, source_target_pairs={{0,6},{1,7},{2,4},{3,5},{4,2},{5,3},{6,0},{7,1},{8,14},{9,15},{10,... | collective-permute-start | bytes 294920 | tf_op jit(solution)/shard_map/ppermute | solution.py:577
  22.2 7.2 %collective-permute-start.2 = (bf16[2,4,16,384]{3,2,1,0:T(8,128)(2,1)S(1)}, bf16[2,4,16,384]{3,2,1,0:T(8,128)(2,1)S(1)}, u32[]{:S(2)}, u32[]{:S(2)}) collective-permute-start(bf16[2,4,16,384]{3,2,1,0:T(8,128)(2,1)S(1)} %get-tuple-element.14), channel_id=1, source_target_pairs={{0,4},{1,5},{2,6},{3,7},{4,0},{5,1},{6,2},{7,3},{8,12},{9,13},{10,... | collective-permute-start | bytes 294920 | tf_op jit(solution)/shard_map/ppermute | solution.py:577
  22.2 7.2 %collective-permute-start.1 = (bf16[2,4,16,384]{3,2,1,0:T(8,128)(2,1)S(1)}, bf16[2,4,16,384]{3,2,1,0:T(8,128)(2,1)S(1)}, u32[]{:S(2)}, u32[]{:S(2)}) collective-permute-start(bf16[2,4,16,384]{3,2,1,0:T(8,128)(2,1)S(1)} %get-tuple-element.14), channel_id=1, source_target_pairs={{0,2},{1,3},{2,0},{3,1},{4,6},{5,7},{6,4},{7,5},{8,10},{9,11},{10,... | collective-permute-start | bytes 294920 | tf_op jit(solution)/shard_map/ppermute | solution.py:577
  29.4 12.4 %collective-permute-start.4 = (bf16[4,2,4,16,384]{4,3,2,1,0:T(8,128)(2,1)S(1)}, bf16[4,2,4,16,384]{4,3,2,1,0:T(8,128)(2,1)S(1)}, u32[]{:S(2)}, u32[]{:S(2)}) collective-permute-start(bf16[4,2,4,16,384]{4,3,2,1,0:T(8,128)(2,1)S(1)} %pad_maximum_fusion.refs_0_), channel_id=1, source_target_pairs={{0,1},{1,0},{2,3},{3,2},{4,5},{5,4},{6,7},{7,6},{8,9},{9,8},{10,11... | collective-permute-start | bytes 1179656 | tf_op jit(solution)/shard_map/ppermute | solution.py:577
  31.1 11.9 %collective-permute-start.6 = (f32[18,2,649]{2,1,0:T(2,128)S(1)}, f32[18,2,649]{2,1,0:T(2,128)S(1)}, u32[]{:S(2)}, u32[]{:S(2)}) collective-permute-start(f32[18,2,649]{2,1,0:T(2,128)S(1)} %pad_maximum_fusion.1), channel_id=1, source_target_pairs={{0,1},{1,2},{2,3},{3,4},{4,5},{5,6},{6,7},{8,9},{9,10},{10,11},{11... | collective-permute-start | bytes 280376 | tf_op jit(solution)/shard_map/ppermute | solution.py:436
  33.7 9.4 %collective-permute-start.7 = (f32[18,2,649]{2,1,0:T(2,128)S(1)}, f32[18,2,649]{2,1,0:T(2,128)S(1)}, u32[]{:S(2)}, u32[]{:S(2)}) collective-permute-start(f32[18,2,649]{2,1,0:T(2,128)S(1)} %pad_maximum_fusion.2), channel_id=1, source_target_pairs={{1,0},{2,1},{3,2},{4,3},{5,4},{6,5},{7,6},{9,8},{10,9},{11,10},{12... | collective-permute-start | bytes 280376 | tf_op jit(solution)/shard_map/ppermute | solution.py:436
  42.7 3.0 %collective-permute-start.8 = (f32[4,128]{1,0:T(4,128)S(1)}, f32[4,128]{1,0:T(4,128)S(1)}, u32[]{:S(2)}, u32[]{:S(2)}) collective-permute-start(f32[4,128]{1,0:T(4,128)S(1)} %pick.1.own_ref), channel_id=1, source_target_pairs={{0,16},{16,0},{1,17},{17,1},{2,18},{18,2},{3,19},{19,3},{4,20},{20... | collective-permute-start | bytes 6152 | tf_op jit(solution)/shard_map/ppermute | solution.py:577
  47.3 1.2 %collective-permute-start.9 = (f32[8,128]{1,0:T(8,128)S(1)}, f32[8,128]{1,0:T(8,128)S(1)}, u32[]{:S(2)}, u32[]{:S(2)}) collective-permute-start(f32[8,128]{1,0:T(8,128)S(1)} %stress.1), channel_id=1, source_target_pairs={{0,16},{16,0},{1,17},{17,1},{2,18},{18,2},{3,19},{19,3},{4,20},{20... | collective-permute-start | bytes 12296 | tf_op jit(solution)/shard_map/ppermute | solution.py:577
  48.5 5.8 %collective-permute-start.10 = (f32[1,4,128]{2,1,0:T(4,128)S(1)}, f32[1,4,128]{2,1,0:T(4,128)S(1)}, u32[]{:S(2)}, u32[]{:S(2)}) collective-permute-start(f32[1,4,128]{2,1,0:T(4,128)S(1)} %get-tuple-element.25), channel_id=1, source_target_pairs={{0,1},{1,0},{2,3},{3,2},{4,5},{5,4},{6,7},{7,6},{8,9},{9,8},{10,11... | collective-permute-start | bytes 6152 | tf_op jit(solution)/shard_map/ppermute | solution.py:577
  54.3 3.7 %collective-permute-start.11 = (f32[2,4,128]{2,1,0:T(4,128)S(1)}, f32[2,4,128]{2,1,0:T(4,128)S(1)}, u32[]{:S(2)}, u32[]{:S(2)}) collective-permute-start(f32[2,4,128]{2,1,0:T(4,128)S(1)} %pad_maximum_fusion.6), channel_id=1, source_target_pairs={{0,2},{1,3},{2,0},{3,1},{4,6},{5,7},{6,4},{7,5},{8,10},{9,11},{10,... | collective-permute-start | bytes 12296 | tf_op jit(solution)/shard_map/ppermute | solution.py:577
  58.0 4.5 %collective-permute-start.12 = (f32[4,4,128]{2,1,0:T(4,128)S(1)}, f32[4,4,128]{2,1,0:T(4,128)S(1)}, u32[]{:S(2)}, u32[]{:S(2)}) collective-permute-start(f32[4,4,128]{2,1,0:T(4,128)S(1)} %pad_maximum_fusion.5), channel_id=1, source_target_pairs={{0,4},{1,5},{2,6},{3,7},{4,0},{5,1},{6,2},{7,3},{8,12},{9,13},{10,... | collective-permute-start | bytes 24584 | tf_op jit(solution)/shard_map/ppermute | solution.py:577
  58.0 4.6 %copy-start.1 = (s32[4,512]{1,0:T(4,128)S(1)}, s32[4,512]{1,0:T(4,128)}, u32[]{:S(2)}) copy-start(s32[4,512]{1,0:T(4,128)} %source_ref.1) | copy-start | bytes 24580

commit v2 on v1

v2 whole, which is shorter than its diff:
```python
import functools
import math

import jax
import jax.numpy as jnp
import numpy as np
from jax import lax
from jax.experimental import pallas as pl
from jax.experimental.pallas import tpu as pltpu
from jax.sharding import PartitionSpec as P


LON = 4096
NDIR = 36
NFREQ = 36
LANES = 128
PAD = 8

two_pi = 2.0 * math.pi
gravity = 9.81
base_freq = 0.04177
courant = 0.45
wind_scale = 10.0
growth = 0.05
dissipation = 0.5
energy_ref = 8.0
mid_freq = 0.2
stress_coef = 0.03
drag_coef = 0.0012
stress_floor = 0.02


bf16 = jnp.bfloat16
f32 = jnp.float32
SMEM_SPEC = pl.BlockSpec(memory_space=pltpu.SMEM)


def vmem_spec():
    return pl.BlockSpec(memory_space=pltpu.VMEM)


def params(grid_dims=1, mebibytes=16):
    return pltpu.CompilerParams(
        dimension_semantics=("arbitrary",) * grid_dims, vmem_limit_bytes=mebibytes * 1024 * 1024
    )


def cost(flops, nbytes):
    return pl.CostEstimate(flops=flops, bytes_accessed=nbytes, transcendentals=0)


def legendre_kernel(shape, where_ref, leg_hbm, coef_hbm, *refs):
    n_aa, waves_local, cycles, pc, group, per_step, wave_lanes = shape
    out_refs, (leg_all, coef_all, held, arrived) = refs[:n_aa], refs[n_aa:]
    steps = leg_all.shape[0]
    band = where_ref[0]
    band_cycles = cycles // n_aa
    per_block = LANES // group
    groups = waves_local // group

    def copies(step):
        return (
            pltpu.make_async_copy(leg_hbm.at[step], leg_all.at[step], arrived.at[0, step]),
            pltpu.make_async_copy(coef_hbm.at[step], coef_all.at[step], arrived.at[1, step]),
        )

    for step in range(steps):
        for copy in copies(step):
            copy.start()

    lane = lax.broadcasted_iota(jnp.int32, (pc, LANES), 1)
    row_wave = lax.broadcasted_iota(jnp.int32, (group * cycles, wave_lanes), 0) // cycles
    degree = lax.broadcasted_iota(jnp.int32, (group * cycles, wave_lanes), 1)
    ahead = degree - row_wave
    contract = (((1,), (1,)), ((), ()))

    def one_step(step, carry):
        for copy in copies(step):
            copy.wait()
        for part in range(per_step):
            index = step * per_step + part
            leg_rows = pl.ds(part * group * cycles, group * cycles)
            coef_rows = pl.ds(part * group * pc, group * pc)
            first = band * waves_local + index * group
            low = leg_all[step, leg_rows, :wave_lanes].astype(f32)
            low = jnp.where(ahead >= first, low, 0.0).astype(bf16)
            full = lax.dot_general(
                coef_all[step, coef_rows, :wave_lanes],
                low,
                contract,
                preferred_element_type=f32,
            ) + lax.dot_general(
                coef_all[step, coef_rows, wave_lanes:],
                leg_all[step, leg_rows, wave_lanes:],
                contract,
                preferred_element_type=f32,
            )
            own = full[:pc]
            for wave in range(1, group):
                own = jnp.where(lane // cycles == wave, full[wave * pc : (wave + 1) * pc], own)
            held[index] = own
        return carry

    lax.fori_loop(0, steps, one_step, 0)

    for shift in range(n_aa):
        target = lax.rem(band + shift, n_aa) * band_cycles
        for cycle in range(band_cycles):
            source = (lane % group) * cycles + (target + cycle)
            for block in range(-(-groups // per_block)):
                value = jnp.zeros((pc, LANES), f32)
                for at in range(block * per_block, min(groups, (block + 1) * per_block)):
                    piece = jnp.take_along_axis(held[at], source, axis=1)
                    value = jnp.where(lane // group == at % per_block, piece, value)
                lanes = slice(block * LANES, (block + 1) * LANES)
                out_refs[shift][cycle, :, lanes] = value.astype(bf16)


def legendre_sums(legendre, coefficients, band_index, n_aa):
    waves_local, cycles, degrees = legendre.shape
    pc = coefficients.shape[2] * coefficients.shape[3]
    group = LANES // cycles
    per_step = 32 // group if waves_local % 32 == 0 else 16 // group
    rows = group * per_step
    steps = waves_local // rows
    blocks = -(-waves_local // LANES)
    wave_lanes = -(-waves_local * n_aa // LANES) * LANES
    shape = (n_aa, waves_local, cycles, pc, group, per_step, wave_lanes)
    return pl.pallas_call(
        functools.partial(legendre_kernel, shape),
        in_specs=[SMEM_SPEC] + [pl.BlockSpec(memory_space=pltpu.HBM)] * 2,
        out_specs=[vmem_spec()] * n_aa,
        out_shape=[jax.ShapeDtypeStruct((cycles // n_aa, pc, blocks * LANES), bf16)] * n_aa,
        scratch_shapes=[
            pltpu.VMEM((steps, rows * cycles, degrees), bf16),
            pltpu.VMEM((steps, rows * pc, degrees), bf16),
            pltpu.VMEM((waves_local // group, pc, LANES), f32),
            pltpu.SemaphoreType.DMA((2, steps)),
        ],
        compiler_params=params(0, 52),
        cost_estimate=cost(7_000_000_000, 20_000_000),
        name="legendre",
    )(
        band_index,
        legendre.reshape(steps, rows * cycles, degrees),
        coefficients.reshape(steps, rows * pc, degrees),
    )


def sine_cosine(wave, slot, points, inverse):
    product = wave * slot
    remain = product - jnp.floor(product * inverse + 0.5) * points
    turn = remain / points
    quarter = jnp.floor(4.0 * turn + 0.5)
    angle = (turn - 0.25 * quarter) * two_pi
    square = angle * angle
    sine = angle * (
        1.0
        + square
        * (-1.0 / 6.0 + square * (1.0 / 120.0 + square * (-1.0 / 5040.0 + square / 362880.0)))
    )
    cosine = 1.0 + square * (
        -0.5 + square * (1.0 / 24.0 + square * (-1.0 / 720.0 + square / 40320.0))
    )
    side = jnp.abs(quarter) == 1.0
    back = jnp.abs(quarter) == 2.0
    cosine_out = jnp.where(side, -quarter * sine, jnp.where(back, -cosine, cosine))
    sine_out = jnp.where(side, quarter * cosine, jnp.where(back, -sine, sine))
    return sine_out, cosine_out


def build_tables(shape, band, points, slot, coarse, write):
    n_aa, waves_local, fine_rows = shape
    coarse_local = waves_local // fine_rows
    coarse_rows, width = coarse.shape[1], slot.shape[1]
    points_row = jnp.full((1, width), points, f32)
    inverse = 1.0 / points_row
    active = slot < points_row
    fine = lax.broadcasted_iota(jnp.int32, (fine_rows, width), 0).astype(f32)
    sine_fine, cosine_fine = sine_cosine(fine, slot, points_row, inverse)
    row = lax.broadcasted_iota(jnp.int32, (coarse_rows, width), 0)
    wave = jnp.zeros((coarse_rows, width), jnp.int32)
    for shift in range(n_aa):
        first = lax.rem(band - shift + n_aa, n_aa) * waves_local
        inside = (row >= shift * coarse_local) & (row < (shift + 1) * coarse_local)
        wave = jnp.where(inside, first + (row - shift * coarse_local) * fine_rows, wave)
    sine_coarse, cosine_coarse = sine_cosine(wave.astype(f32), slot, points_row, inverse)
    coarse[0] = jnp.where(active, 2.0 * cosine_coarse, 0.0)
    coarse[1] = jnp.where(active, -2.0 * sine_coarse, 0.0)
    for shift in range(n_aa):
        first = lax.rem(band - shift + n_aa, n_aa) * waves_local
        for step in range(coarse_local):
            at = shift * coarse_local + step
            cosine_at = coarse[0, at : at + 1, :]
            sine_at = coarse[1, at : at + 1, :]
            cosine_part = cosine_at * cosine_fine + sine_at * sine_fine
            sine_part = sine_at * cosine_fine - cosine_at * sine_fine
            if step == 0:
                weight = jnp.where(fine + first.astype(f32) == 0.0, 0.5, 1.0)
                cosine_part = cosine_part * weight
                sine_part = sine_part * weight
            rows = slice(at * fine_rows, (at + 1) * fine_rows)
            write(rows, cosine_part.astype(bf16), sine_part.astype(bf16))
        yield shift


def table_shape(n_aa, waves_local):
    fine_rows = 32 if waves_local % 32 == 0 else 16
    coarse_rows = -(-(n_aa * waves_local // fine_rows) // 8) * 8
    return (n_aa, waves_local, fine_rows), coarse_rows


def wind_table_kernel(shape, sizes, where_ref, count_ref, column_ref, out_ref, coarse):
    n_in, cycles, cycle_rows, columns_local = sizes
    band, column = where_ref[0], where_ref[1]
    cycle = pl.program_id(0)
    points = count_ref[band * cycles + cycle].astype(f32)
    lane = lax.broadcasted_iota(jnp.int32, (1, LANES), 1)
    per_block = LANES // columns_local
    parts = []
    for inner in range(n_in):
        owner = jnp.bitwise_xor(column, inner)
        part = jnp.zeros((1, LANES), jnp.int32)
        for row in range(cycle_rows):
            source = column_ref[pl.ds(cycle * cycle_rows + row, 1), :]
            piece = source[:, :LANES]
            for block in range(1, source.shape[1] // LANES):
                piece = jnp.where(
                    owner // per_block == block,
                    source[:, block * LANES : (block + 1) * LANES],
                    piece,
                )
            turn = lax.rem(row - lax.rem(owner, per_block) + per_block, per_block)
            piece = pltpu.roll(piece, turn * columns_local, 1)
            part = jnp.where(lane // columns_local == row, piece, part)
        parts.append(part)
    slot = jnp.concatenate(parts, axis=1).astype(f32)

    def write(rows, cosine_part, sine_part):
        out_ref[0, 0, rows, :] = cosine_part
        out_ref[0, 1, rows, :] = sine_part

    for _ in build_tables(shape, band, points, slot, coarse, write):
        pass


def wind_tables(wind_column, counts, where, n_aa, waves_local, n_in, sizes):
    cycles = sizes[0]
    shape, coarse_rows = table_shape(n_aa, waves_local)
    waves, width = n_aa * waves_local, n_in * LANES
    return pl.pallas_call(
        functools.partial(wind_table_kernel, shape, (n_in,) + sizes),
        grid=(cycles,),
        in_specs=[SMEM_SPEC, SMEM_SPEC, vmem_spec()],
        out_specs=pl.BlockSpec((1, 2, waves, width), lambda i: (i, 0, 0, 0)),
        out_shape=jax.ShapeDtypeStruct((cycles, 2, waves, width), bf16),
        scratch_shapes=[pltpu.VMEM((2, coarse_rows, width), f32)],
        compiler_params=params(),
        cost_estimate=cost(1_700_000_000, 3_000_000),
        name="wind_tables",
    )(where, counts, wind_column)


def stack_rows(pieces):
    if pieces[0].shape[0] % 16 == 0:
        return jnp.concatenate(pieces, axis=0)
    return jnp.concatenate([piece.astype(f32) for piece in pieces], axis=0).astype(bf16)


def synthesis_kernel(shape, n_out, n_in, where_ref, count_ref, *refs):
    fourier, (out_ref, coarse, table) = refs[:n_in], refs[n_in:]
    _, waves_local, _ = shape
    band, column = where_ref[0], where_ref[1]
    cycle = pl.program_id(0)
    points = count_ref[band * pl.num_programs(0) + cycle].astype(f32)
    levels, width = out_ref.shape[2:]
    pc = fourier[0].shape[3]
    slot = column * width + lax.broadcasted_iota(jnp.int32, (1, width), 1)

    def write(rows, cosine_part, sine_part):
        table[0, rows, :] = cosine_part
        table[1, rows, :] = sine_part

    cosine_sum = None
    sine_sum = None
    for shift in build_tables(shape, band, points, slot.astype(f32), coarse, write):
        left = stack_rows(
            [
                fourier[inner][outer, shift, 0, :, :waves_local]
                for inner in range(n_in)
                for outer in range(n_out)
            ]
        )
        rows = slice(shift * waves_local, (shift + 1) * waves_local)
        cosine_part = jnp.dot(left, table[0, rows, :], preferred_element_type=f32)
        sine_part = jnp.dot(left, table[1, rows, :], preferred_element_type=f32)
        cosine_sum = cosine_part if cosine_sum is None else cosine_sum + cosine_part
        sine_sum = sine_part if sine_sum is None else sine_sum + sine_part
    for inner in range(n_in):
        for outer in range(n_out):
            at = (inner * n_out + outer) * pc
            value = cosine_sum[at : at + levels] + sine_sum[at + levels : at + pc]
            source = jnp.bitwise_xor(column, outer * n_in + inner)
            out_ref[0, source] = value.astype(bf16)


def synthesis(fourier, counts, where, n_aa, waves_local, n_in, width):
    n_out, _, cycles, pc, lanes = fourier[0].shape
    levels = pc // 2
    n_ba = n_out * n_in
    shape, coarse_rows = table_shape(n_aa, waves_local)
    block = pl.BlockSpec((n_out, n_aa, 1, pc, lanes), lambda i: (0, 0, i, 0, 0))
    return pl.pallas_call(
        functools.partial(synthesis_kernel, shape, n_out, n_in),
        grid=(cycles,),
        in_specs=[SMEM_SPEC, SMEM_SPEC] + [block] * n_in,
        out_specs=pl.BlockSpec((1, n_ba, levels, width), lambda i: (i, 0, 0, 0)),
        out_shape=jax.ShapeDtypeStruct((cycles, n_ba, levels, width), bf16),
        scratch_shapes=[
            pltpu.VMEM((2, coarse_rows, width), f32),
            pltpu.VMEM((2, n_aa * waves_local, width), bf16),
        ],
        compiler_params=params(),
        cost_estimate=cost(3_500_000_000, 2_000_000),
        name="synthesis",
    )(where, counts, *fourier)


def pick_kernel(shape, where_ref, fourier_ref, table_ref, *out_refs):
    n_aa, waves_local, n_in = shape
    outer_at = where_ref[1] // n_in
    cycles = out_refs[0].shape[0]
    pc = fourier_ref.shape[3]
    levels = pc // 2
    for cycle in range(cycles):
        total = None
        for shift in range(n_aa):
            left = fourier_ref[outer_at, shift, cycle][:, :waves_local]
            rows = slice(shift * waves_local, (shift + 1) * waves_local)
            cosine_part = jnp.dot(left, table_ref[cycle, 0, rows, :], preferred_element_type=f32)
            sine_part = jnp.dot(left, table_ref[cycle, 1, rows, :], preferred_element_type=f32)
            part = cosine_part[0:1] + sine_part[levels : levels + 1]
            total = part if total is None else total + part
        wind = wind_scale * total.astype(bf16).astype(f32)
        for inner, out_ref in enumerate(out_refs):
            out_ref[cycle : cycle + 1, :] = wind[:, inner * LANES : (inner + 1) * LANES]


def pick_winds(fourier, table, where, n_aa, waves_local, n_in):
    _, _, cycles, _, _ = fourier.shape
    return pl.pallas_call(
        functools.partial(pick_kernel, (n_aa, waves_local, n_in)),
        in_specs=[SMEM_SPEC] + [vmem_spec()] * 2,
        out_specs=[vmem_spec()] * n_in,
        out_shape=[jax.ShapeDtypeStruct((cycles, LANES), f32)] * n_in,
        compiler_params=params(0),
        cost_estimate=cost(1_000_000_000, 2_000_000),
        name="pick",
    )(where, fourier, table)


def bin_table(parts):
    bins = np.arange(NDIR * NFREQ)
    directions, freq_index = bins // NFREQ, bins % NFREQ
    heading = two_pi * (directions + 0.5) / NDIR
    period_ratio = np.exp(-math.log(1.1) * (35.0 / (NFREQ - 1)) * freq_index)
    frequency = base_freq / period_ratio
    drift_east = courant * period_ratio * np.cos(heading)
    drift_north = courant * period_ratio * np.sin(heading)
    inverse_speed = two_pi * frequency / gravity
    bin_width = 0.1 * frequency * (two_pi / NDIR)
    east_pos, east_neg = np.maximum(drift_east, 0.0), -np.minimum(drift_east, 0.0)
    north_pos, north_neg = np.maximum(drift_north, 0.0), -np.minimum(drift_north, 0.0)
    rows = [
        1.0 - east_pos - east_neg - north_pos - north_neg,
        east_pos,
        east_neg,
        north_pos,
        north_neg,
        np.cos(heading) * inverse_speed,
        np.sin(heading) * inverse_speed,
        bin_width,
        dissipation * (frequency / mid_freq),
    ]
    rows += [np.zeros_like(frequency)] * (16 - len(rows))
    table = np.stack(rows).astype(np.float32).reshape(16, parts, -1)
    return np.ascontiguousarray(table.transpose(1, 0, 2))


def column_of(values, at):
    lane = lax.broadcasted_iota(jnp.int32, values.shape, 1)
    return jnp.sum(jnp.where(lane == at, values, 0.0), axis=1, keepdims=True)


def transposed_mask(mask_ref, padded):
    rows, columns = mask_ref.shape
    padded[...] = jnp.zeros_like(padded)
    padded[:rows, :columns] = mask_ref[...].astype(f32)
    return jnp.transpose(padded[...])


def pack_kernel(n_aa, where_ref, spectra_ref, mask_ref, *refs):
    row_refs, (west_ref, east_ref, padded) = refs[:-3], refs[-3:]
    rows, columns, bins = spectra_ref.shape
    turned = transposed_mask(mask_ref, padded)
    starts = [0, rows - 2]
    if n_aa == 2:
        starts = [jnp.where(where_ref[0] == 0, rows - 2, 0)]
    for start, row_ref in zip(starts, row_refs):
        for at in range(2):
            own = column_of(turned, start + at)[:columns]
            row_ref[at, :, :bins] = spectra_ref[start + at] * own
            row_ref[at, :, bins:] = own
    mask = mask_ref[...].astype(f32)
    for side_ref, start in ((west_ref, 0), (east_ref, columns - 2)):
        for at in range(2):
            own = column_of(mask, start + at)
            side_ref[:, at, :bins] = spectra_ref[:, start + at, :] * own
            side_ref[:, at, bins:] = own


def pack(where, spectra, mask, n_aa):
    rows, columns, bins = spectra.shape
    n_rows = 1 if n_aa == 2 else 2
    return pl.pallas_call(
        functools.partial(pack_kernel, n_aa),
        in_specs=[SMEM_SPEC] + [vmem_spec()] * 2,
        out_specs=[vmem_spec()] * (n_rows + 2),
        out_shape=[jax.ShapeDtypeStruct((2, columns, bins + 1), f32)] * n_rows
        + [jax.ShapeDtypeStruct((rows, 2, bins + 1), f32)] * 2,
        scratch_shapes=[pltpu.VMEM((LANES, LANES), f32)],
        compiler_params=params(0),
        cost_estimate=cost(600_000_000, 500_000),
        name="pack",
    )(where, spectra, mask)


def rows_beyond(n_aa, where_ref, low_ref, high_ref, at):
    low = jnp.where(where_ref[0] > 0, low_ref[at], 0.0)
    high = jnp.where(where_ref[0] < n_aa - 1, high_ref[1 - at], 0.0)
    return low, high


def sides_kernel(n_aa, where_ref, low_ref, high_ref, west_ref, east_ref, out_west, out_east):
    rows, _, _ = west_ref.shape
    columns = low_ref.shape[1]
    low, high = rows_beyond(n_aa, where_ref, low_ref, high_ref, 1)
    for side_ref, out_ref, cut in (
        (west_ref, out_west, slice(0, 2)),
        (east_ref, out_east, slice(columns - 2, columns)),
    ):
        out_ref[0] = low[cut]
        out_ref[1 : rows + 1] = side_ref[...]
        out_ref[rows + 1] = high[cut]


def pack_sides(where, low, high, west, east, n_aa):
    rows, _, count = west.shape
    return pl.pallas_call(
        functools.partial(sides_kernel, n_aa),
        in_specs=[SMEM_SPEC] + [vmem_spec()] * 4,
        out_specs=[vmem_spec()] * 2,
        out_shape=[jax.ShapeDtypeStruct((rows + 2, 2, count), f32)] * 2,
        compiler_params=params(0),
        cost_estimate=cost(300_000_000, 500_000),
        name="pack_sides",
    )(where, low, high, west, east)


def advect_kernel(
    n_aa,
    where_ref,
    bins_ref,
    spectra_ref,
    mask_ref,
    low_ref,
    high_ref,
    west_ref,
    east_ref,
    out_ref,
    first,
    second,
    padded,
):
    rows, columns, bins = spectra_ref.shape
    half = where_ref[2]
    wide = columns + 2 * PAD
    turned = transposed_mask(mask_ref, padded)
    edge = jnp.zeros((PAD, bins), f32)
    for row in range(rows + 4):
        first[row, 0:PAD] = edge
        first[row, PAD + columns :] = edge
    inside = slice(PAD, PAD + columns)
    low_far, high_far = rows_beyond(n_aa, where_ref, low_ref, high_ref, 0)
    low_near, high_near = rows_beyond(n_aa, where_ref, low_ref, high_ref, 1)
    first[0, inside] = low_far[:, :bins]
    first[1, inside] = low_near[:, :bins]
    first[rows + 2, inside] = high_near[:, :bins]
    first[rows + 3, inside] = high_far[:, :bins]
    masks = [low_near[:, bins:]]
    for row in range(rows):
        masks.append(column_of(turned, row)[:columns])
        first[row + 2, inside] = spectra_ref[row] * masks[-1]
    masks.append(high_near[:, bins:])
    first[1 : rows + 3, PAD - 2 : PAD] = west_ref[:, :, :bins]
    first[1 : rows + 3, PAD + columns : PAD + columns + 2] = east_ref[:, :, :bins]
    keep, east_pos, east_neg, north_pos, north_neg = (
        bins_ref[half, at : at + 1] for at in range(5)
    )

    def update(source, at):
        centre = source[at]
        western = pltpu.roll(centre, 1, 0)
        eastern = pltpu.roll(centre, wide - 1, 0)
        return (
            keep * centre
            + east_pos * western
            + east_neg * eastern
            + north_pos * source[at - 1]
            + north_neg * source[at + 1]
        )

    for row in range(rows + 2):
        value = update(first, row + 1)
        second[row, 0:PAD] = value[0:PAD] * west_ref[row, 1:2, bins:]
        second[row, inside] = value[inside] * masks[row]
        second[row, PAD + columns :] = value[PAD + columns :] * east_ref[row, 0:1, bins:]
    for row in range(rows):
        value = update(second, row + 1)
        out_ref[row] = value[inside] * masks[row + 1]


def advect(where, bins, spectra, mask, low, high, west, east, n_aa):
    rows, columns, count = spectra.shape
    wide = columns + 2 * PAD
    return pl.pallas_call(
        functools.partial(advect_kernel, n_aa),
        in_specs=[SMEM_SPEC] + [vmem_spec()] * 7,
        out_specs=vmem_spec(),
        out_shape=jax.ShapeDtypeStruct(spectra.shape, f32),
        scratch_shapes=[
            pltpu.VMEM((rows + 4, wide, count), f32),
            pltpu.VMEM((rows + 2, wide, count), f32),
            pltpu.VMEM((LANES, LANES), f32),
        ],
        compiler_params=params(0),
        cost_estimate=cost(2_600_000_000, 4_000_000),
        name="advect",
    )(where, bins, spectra, mask, low, high, west, east)


def across(sent, axis):
    count = lax.axis_size(axis)
    if len(sent) == 1:
        got = lax.ppermute(sent[0], axis, [(0, 1), (1, 0)])
        return got, got
    forward = [(i, i + 1) for i in range(count - 1)]
    backward = [(target, source) for source, target in forward]
    return lax.ppermute(sent[1], axis, forward), lax.ppermute(sent[0], axis, backward)


def as_columns(rows_by_lanes):
    rows = rows_by_lanes.shape[0]
    if rows % 8:
        rows_by_lanes = jnp.concatenate(
            [rows_by_lanes, jnp.zeros((8 - rows % 8, LANES), f32)], axis=0
        )
    return jnp.transpose(rows_by_lanes)


def stress_kernel(
    n_in, where_ref, bins_ref, density_ref, own_ref, own_far_ref, other_ref, other_far_ref,
    sums_ref, points_ref
):
    cycles = own_ref.shape[0]
    rows, _, bins = density_ref.shape
    cycle_rows = rows // cycles
    half = where_ref[2]
    holds = lax.rem(where_ref[1], n_in) == 0
    own = jnp.where(holds, own_ref[...], own_far_ref[...])
    other = jnp.where(holds, other_ref[...], other_far_ref[...])
    east_rows = jnp.where(half == 0, own, other)
    north_rows = jnp.where(half == 0, other, own)
    points_ref[0] = east_rows
    points_ref[1] = north_rows
    points_ref[2] = drag_coef * (own * own + other * other) + stress_floor
    east, north = as_columns(east_rows), as_columns(north_rows)
    along_cos, along_sin, width = (bins_ref[half, at : at + 1] for at in (5, 6, 7))
    lane = lax.broadcasted_iota(jnp.int32, (LANES, LANES), 1)
    sums = jnp.zeros((LANES, LANES), f32)
    for cycle in range(cycles):
        density = density_ref[cycle * cycle_rows : (cycle + 1) * cycle_rows].reshape(LANES, bins)
        alignment = (
            east[:, cycle : cycle + 1] * along_cos + north[:, cycle : cycle + 1] * along_sin
        )
        weighted = density * width
        gain = growth * jnp.maximum(alignment - 1.0, 0.0)
        energy = jnp.sum(weighted, axis=1, keepdims=True)
        stress = jnp.sum(gain * alignment * weighted, axis=1, keepdims=True)
        sums = jnp.where(lane == cycle, stress, sums)
        sums = jnp.where(lane == cycles + cycle, energy, sums)
    turned = jnp.transpose(sums)
    sums_ref[0] = turned[:cycles]
    sums_ref[1] = turned[cycles : 2 * cycles]


def stress_sums(where, bins, density, winds, n_in):
    cycles = winds[0].shape[0]
    return pl.pallas_call(
        functools.partial(stress_kernel, n_in),
        in_specs=[SMEM_SPEC] + [vmem_spec()] * 6,
        out_specs=[vmem_spec()] * 2,
        out_shape=[
            jax.ShapeDtypeStruct((2, cycles, LANES), f32),
            jax.ShapeDtypeStruct((3, cycles, LANES), f32),
        ],
        compiler_params=params(0),
        cost_estimate=cost(1_500_000_000, 2_000_000),
        name="stress",
    )(where, bins, density, *winds)


def spectra_kernel(where_ref, bins_ref, density_ref, points_ref, sums_ref, far_ref, out_ref):
    cycle = pl.program_id(0)
    half = where_ref[2]
    cycle_rows, columns, bins = density_ref.shape
    scaled = (sums_ref[1] + far_ref[1]) * (1.0 / energy_ref)
    row = lax.broadcasted_iota(jnp.int32, (8, LANES), 0)

    def own_row(values):
        mine = lax.broadcasted_iota(jnp.int32, values.shape, 0) == cycle
        return jnp.sum(jnp.where(mine, values, 0.0), axis=0, keepdims=True)

    picked = jnp.where(
        row == 0,
        own_row(points_ref[0]),
        jnp.where(row == 1, own_row(points_ref[1]), own_row(scaled * scaled)),
    )
    picked = jnp.transpose(picked)
    along_cos, along_sin, decay = (bins_ref[half, at : at + 1] for at in (5, 6, 8))
    density = density_ref[...].reshape(LANES, bins)
    alignment = picked[:, 0:1] * along_cos + picked[:, 1:2] * along_sin
    gain = growth * jnp.maximum(alignment - 1.0, 0.0)
    value = density * (1.0 + gain) / (1.0 + decay * picked[:, 2:3])
    out_ref[...] = value.reshape(cycle_rows, columns, bins)


def final_spectra(where, bins, density, points, sums, far):
    cycles = points.shape[1]
    rows, columns, count = density.shape
    block = pl.BlockSpec((rows // cycles, columns, count), lambda i: (i, 0, 0))
    return pl.pallas_call(
        spectra_kernel,
        grid=(cycles,),
        in_specs=[SMEM_SPEC, vmem_spec(), block] + [vmem_spec()] * 3,
        out_specs=block,
        out_shape=jax.ShapeDtypeStruct(density.shape, f32),
        compiler_params=params(1),
        cost_estimate=cost(2_500_000_000, 3_000_000),
        name="spectra",
    )(where, bins, density, points, sums, far)


def charnock_kernel(shape, where_ref, count_ref, source_ref, *refs):
    columns_local, total_columns, order = shape
    rough_refs, out_ref = refs[:-1], refs[-1]
    column = where_ref[1]
    cycles, width = source_ref.shape
    cycle_rows = LANES // columns_local
    base = column * width
    row = lax.broadcasted_iota(jnp.int32, (cycles, LANES), 0)
    points = jnp.zeros((cycles, LANES), jnp.int32)
    for cycle in range(cycles):
        points = jnp.where(row == cycle, count_ref[where_ref[0] * cycles + cycle], points)
    lane = lax.broadcasted_iota(jnp.int32, (cycles, LANES), 1)
    for part in range(width // LANES):
        at = slice(part * LANES, (part + 1) * LANES)
        source = source_ref[:, at]
        band_row = source // total_columns
        source_column = source - band_row * total_columns
        owner = source_column // columns_local
        within = (band_row - row * cycle_rows) * columns_local + (
            source_column - owner * columns_local
        )
        within = jnp.clip(within, 0, LANES - 1)
        value = jnp.zeros((cycles, LANES), f32)
        for rough_ref, distances in zip(rough_refs, order):
            for at_piece, distance in enumerate(distances):
                found = jnp.take_along_axis(rough_ref[at_piece], within, axis=1)
                value = jnp.where(owner == jnp.bitwise_xor(column, distance), found, value)
        out_ref[:, at] = jnp.where(lane + (base + part * LANES) < points, value, 0.0)


def charnock_of(where, counts, pieces, order, source, columns_local):
    total_columns = columns_local * sum(len(distances) for distances in order)
    return pl.pallas_call(
        functools.partial(charnock_kernel, (columns_local, total_columns, order)),
        in_specs=[SMEM_SPEC, SMEM_SPEC] + [vmem_spec()] * (1 + len(pieces)),
        out_specs=vmem_spec(),
        out_shape=jax.ShapeDtypeStruct(source.shape, f32),
        compiler_params=params(0),
        cost_estimate=cost(1_000_000_000, 100_000),
        name="charnock",
    )(where, counts, source, *pieces)


def exchange(value, axis, distance):
    count = lax.axis_size(axis)
    return lax.ppermute(value, axis, [(i, i ^ distance) for i in range(count)])


def exchange_both(value, n_comp, n_ba):
    pairs = [
        (half * n_ba + i, (half ^ 1) * n_ba + (i ^ 1))
        for half in range(n_comp)
        for i in range(n_ba)
    ]
    return lax.ppermute(value, ("comp", "ba"), pairs)


def per_device(
    legendre, coefficients, cycle_points, spectra, sea_mask, wind_column, roughness_source
):
    n_aa, n_ba = lax.axis_size("aa"), lax.axis_size("ba")
    n_comp = lax.axis_size("comp")
    band_index = lax.axis_index("aa")
    column_index = lax.axis_index("ba")
    half_index = lax.axis_index("comp")
    where = jnp.stack([band_index, column_index, half_index]).astype(jnp.int32)
    waves_local, cycles_all, _ = legendre.shape
    cycles = cycles_all // n_aa
    rows_local, columns_local, _ = spectra.shape
    cycle_rows = rows_local // cycles
    n_in = 2
    n_out = n_ba // n_in
    slots_local = LON // n_ba
    counts = cycle_points
    bins = jnp.asarray(bin_table(n_comp))

    fourier = legendre_sums(legendre, coefficients, where, n_aa)

    *row_sides, west, east = pack(where, spectra, sea_mask, n_aa)
    low, high = across(row_sides, "aa")
    west, east = pack_sides(where, low, high, west, east, n_aa)
    west, east = across([west, east], "ba")
    density = advect(where, bins, spectra, sea_mask, low, high, west, east, n_aa)
    wind_table = wind_tables(
        wind_column, counts, where, n_aa, waves_local, n_in,
        (cycles, cycle_rows, columns_local),
    )

    parts = [fourier[0]]
    for shift in range(1, n_aa):
        pairs = [(i, (i + shift) % n_aa) for i in range(n_aa)]
        parts.append(lax.ppermute(fourier[shift], "aa", pairs))
    parts = jnp.stack(parts)
    outer = [parts]
    for k in range(1, n_out):
        outer.append(exchange(parts, "ba", n_in * k))
    outer = jnp.stack(outer)

    picked = pick_winds(outer, wind_table, where, n_aa, waves_local, n_in)
    own_sent = exchange(picked[1], "ba", 1)
    other_sent = exchange_both(picked[1], n_comp, n_ba)
    other_here = exchange(picked[0], "comp", 1)
    inner = [outer]
    for k in range(1, n_in):
        inner.append(exchange(outer, "ba", k))

    winds = (picked[0], own_sent, other_here, other_sent)
    sums, points = stress_sums(where, bins, density, winds, n_in)
    far = exchange(sums, "comp", 1)
    roughness = jnp.sqrt(1.0 + stress_coef * (sums[0] + far[0]) / points[2])
    pieces, order = [roughness[None]], [(0,)]
    for distance in [n_in << k for k in range(n_out.bit_length() - 1)] + [1]:
        sent = jnp.concatenate(pieces, axis=0)
        pieces.append(exchange(sent, "ba", distance))
        order.append(tuple(far_at ^ distance for near in order for far_at in near))
    wave_spectra = final_spectra(where, bins, density, points, sums, far)
    grid_winds = synthesis(inner, counts, where, n_aa, waves_local, n_in, slots_local)
    grid_winds = grid_winds.reshape(1, cycles, -1, slots_local)
    charnock = charnock_of(
        where, counts, pieces, tuple(order), roughness_source, columns_local
    )
    return (grid_winds, wave_spectra, charnock)


def solution(mesh):
    in_specs = (
        P("aa", None, None),
        P("comp", "aa", None, "ba", None),
        P(),
        P("aa", "ba", "comp"),
        P("aa", "ba"),
        P("aa", None),
        P("aa", "ba"),
    )
    out_specs = (P("comp", "aa", None, "ba"), P("aa", "ba", "comp"), P("aa", "ba"))
    return jax.shard_map(
        per_device, mesh=mesh, in_specs=in_specs, out_specs=out_specs, check_vma=False
    )
```

time: 64.1 us -> 64.9 us (1.012)
  starting transfers between devices: 16.2 us -> 22.1 us
  Pallas kernels: 28.7 us -> 26.3 us
  waiting for transfers between devices: 16.4 us -> 15.3 us
  local copies, waits for them, and re-layouts: 0.9 us -> 0.02 us
    ppermute x9 -> x10, starting transfers between devices: 9.31 us -> 14.2 us  [exchange(): return lax.ppermute(value, axis, [(i, i ^ distance) for i in range(count)])]
    pallas_call x9 -> x10, Pallas kernels: 28.7 us -> 26.3 us  [the longest x1 8.21 us: legendre_sums(): pl.pallas_call(functools.partial(legendre_kernel, shape), in_specs=[SMEM_...]
    ppermute x9 -> x10, waiting for transfers between devices: 14.8 us -> 12.5 us  [exchange(): return lax.ppermute(value, axis, [(i, i ^ distance) for i in range(count)])]
    ppermute x3 -> x4, waiting for transfers between devices: 0.25 us -> 1.49 us  [the longest x1 1.48 us: across(): lax.ppermute(sent[0], axis, backward)]
    ppermute x3 -> x4, starting transfers between devices: 3.84 us -> 4.91 us  [the longest x1 3.4 us: across(): lax.ppermute(sent[1], axis, forward)]
  transfers between devices with their start and end apart: 13 -> 15, of which waited for: 8 -> 8; matrix products, arithmetic and copies ran while one was open for 2% -> 0% of each run, Pallas kernels for 22% -> 18%
where the time goes in v2:
time: 64.9 us; the launch traced here: 64.7 us
  Pallas kernels  26.3 us (41%)
  starting transfers between devices  22.1 us (34%)
  waiting for transfers between devices  15.3 us (24%)
  between operations  0.77 us (1%)
    ppermute x10, starting transfers between devices, exchange(): return lax.ppermute(value, axis, [(i, i ^ distance) for i in range(count)])  14.2 us
    ppermute x10, waiting for transfers between devices, exchange(): return lax.ppermute(value, axis, [(i, i ^ distance) for i in range(count)])  12.5 us
    pallas_call x1, Pallas kernels, legendre_sums(): pl.pallas_call(functools.partial(legendre_kernel, shape), in_specs=[SMEM_...  8.21 us
    pallas_call x1, Pallas kernels, synthesis(): pl.pallas_call(functools.partial(synthesis_kernel, shape, n_out, n_in), g...  4.47 us
    ppermute x1, starting transfers between devices, across(): lax.ppermute(sent[1], axis, forward)  3.4 us
    pallas_call x1, Pallas kernels, advect(): pl.pallas_call(functools.partial(advect_kernel, n_aa), in_specs=[SMEM_SPE...  3.35 us
    ppermute x1, starting transfers between devices, per_device(): parts.append(lax.ppermute(fourier[shift], 'aa', pairs))  3.07 us
    pallas_call x1, Pallas kernels, final_spectra(): pl.pallas_call(spectra_kernel, grid=(cycles,), in_specs=[SMEM_SPEC, vmem_...  2.97 us
  transfers between devices with their start and end apart: 15, of which 8 were waited for; matrix products, arithmetic and copies ran while one was open for 0% of the time, Pallas kernels for 18%

profile of v2, /device:TPU:0, one launch (start us, length us, event | category | flops | bytes accessed | tf_op | source)
XLA Modules:
  0.0 64.7 jit_solution(15265302683986904792)
XLA Ops:
  0.6 0.1 pad_add_fusion.where_ref
  0.7 8.2 %legendre.1 = (bf16[4,16,384]{2,1,0:T(8,128)(2,1)S(1)}, bf16[4,16,384]{2,1,0:T(8,128)(2,1)S(1)}) custom-call(s32[3]{0:T(128)S(1)} %pad_add_fusion.where_ref, bf16[10,256,1280]{2,1,0:T(8,128)(2,1)} %bitcast.19, bf16[10,512,1280]{2,1,0:T(8,128)(2,1)} %bitcast.18), custom_call_target="tpu_custom_call" | custom-call | flops 7000000000 | bytes 20000000 | tf_op jit(solution)/shard_map/legendre/pallas_call | solution.py:129
  8.9 3.1 %collective-permute-start = (bf16[4,16,384]{2,1,0:T(8,128)(2,1)S(1)}, bf16[4,16,384]{2,1,0:T(8,128)(2,1)S(1)}, u32[]{:S(2)}, u32[]{:S(2)}) collective-permute-start(bf16[4,16,384]{2,1,0:T(8,128)(2,1)S(1)} %get-tuple-element.15), channel_id=1, source_target_pairs={{0,8},{8,0},{1,9},{9,1},{2,10},{10,2},{3,11},{11,3},{4,12},{12,4},... | collective-permute-start | bytes 147464 | tf_op jit(solution)/shard_map/ppermute | solution.py:755
  12.0 0.0 copy-done
  12.0 0.0 copy-done.2
  12.0 0.7 %pack.1 = (f32[2,32,649]{2,1,0:T(8,128)S(1)}, f32[16,2,649]{2,1,0:T(2,128)S(1)}, f32[16,2,649]{2,1,0:T(2,128)S(1)}) custom-call(s32[3]{0:T(128)S(1)} %pad_add_fusion.where_ref, f32[16,32,648]{2,1,0:T(8,128)S(1)} %copy-done, s32[16,32]{1,0:T(8,128)S(1)} %copy-done.2), custom_call_target="tpu_custom_call" | custom-call | flops 600000000 | bytes 500000 | tf_op jit(solution)/shard_map/pack/pallas_call | solution.py:425
  12.7 0.1 collective-permute-start.5
  12.8 1.3 %collective-permute-done = bf16[4,16,384]{2,1,0:T(8,128)(2,1)S(1)} collective-permute-done((bf16[4,16,384]{2,1,0:T(8,128)(2,1)S(1)}, bf16[4,16,384]{2,1,0:T(8,128)(2,1)S(1)}, u32[]{:S(2)}, u32[]{:S(2)}) %collective-permute-start) | collective-permute-done | bytes 49184 | tf_op jit(solution)/shard_map/ppermute | solution.py:755
  14.2 4.1 %collective-permute-start.3 = (bf16[2,4,16,384]{3,2,1,0:T(8,128)(2,1)S(1)}, bf16[2,4,16,384]{3,2,1,0:T(8,128)(2,1)S(1)}, u32[]{:S(2)}, u32[]{:S(2)}) collective-permute-start(bf16[2,4,16,384]{3,2,1,0:T(8,128)(2,1)S(1)} %get-tuple-element.26), channel_id=1, source_target_pairs={{0,6},{1,7},{2,4},{3,5},{4,2},{5,3},{6,0},{7,1},{8,14},{9,15},{10,... | collective-permute-start | bytes 294920 | tf_op jit(solution)/shard_map/ppermute | solution.py:709
  18.3 0.0 collective-permute-start.1
  18.3 0.6 collective-permute-start.2
  18.9 0.0 copy-done.1
  18.9 0.0 copy-done.4
  18.9 2.1 %wind_tables.1.table_ref = bf16[4,2,640,256]{3,2,1,0:T(8,128)(2,1)S(1)} custom-call(s32[3]{0:T(128)S(1)} %pad_add_fusion.where_ref, s32[8]{0:T(128)S(1)} %copy-done.4, s32[16,256]{1,0:T(8,128)S(1)} %copy-done.1), custom_call_target="tpu_custom_call" | custom-call | flops 1700000000 | bytes 3000000 | tf_op jit(solution)/shard_map/wind_tables/pallas_call | solution.py:251
  21.0 0.4 collective-permute-done.3
  21.3 3.2 %collective-permute-done.1 = bf16[2,4,16,384]{3,2,1,0:T(8,128)(2,1)S(1)} collective-permute-done((bf16[2,4,16,384]{3,2,1,0:T(8,128)(2,1)S(1)}, bf16[2,4,16,384]{3,2,1,0:T(8,128)(2,1)S(1)}, u32[]{:S(2)}, u32[]{:S(2)}) %collective-permute-start.1) | collective-permute-done | bytes 98336 | tf_op jit(solution)/shard_map/ppermute | solution.py:709
  24.5 1.1 %collective-permute-done.2 = bf16[2,4,16,384]{3,2,1,0:T(8,128)(2,1)S(1)} collective-permute-done((bf16[2,4,16,384]{3,2,1,0:T(8,128)(2,1)S(1)}, bf16[2,4,16,384]{3,2,1,0:T(8,128)(2,1)S(1)}, u32[]{:S(2)}, u32[]{:S(2)}) %collective-permute-start.2) | collective-permute-done | bytes 98336 | tf_op jit(solution)/shard_map/ppermute | solution.py:709
  25.6 0.1 pad_maximum_fusion.refs_0_.fourier_ref
  25.6 0.0 collective-permute-done.5.low_ref.high_ref
  25.6 0.6 pack_sides.1
  26.2 3.4 %collective-permute-start.6 = (f32[18,2,649]{2,1,0:T(2,128)S(1)}, f32[18,2,649]{2,1,0:T(2,128)S(1)}, u32[]{:S(2)}, u32[]{:S(2)}) collective-permute-start(f32[18,2,649]{2,1,0:T(2,128)S(1)} %get-tuple-element.19), channel_id=1, source_target_pairs={{0,1},{1,2},{2,3},{3,4},{4,5},{5,6},{6,7},{8,9},{9,10},{10,11},{11... | collective-permute-start | bytes 280376 | tf_op jit(solution)/shard_map/ppermute | solution.py:559
  29.6 1.3 %collective-permute-start.7 = (f32[18,2,649]{2,1,0:T(2,128)S(1)}, f32[18,2,649]{2,1,0:T(2,128)S(1)}, u32[]{:S(2)}, u32[]{:S(2)}) collective-permute-start(f32[18,2,649]{2,1,0:T(2,128)S(1)} %get-tuple-element.20), channel_id=1, source_target_pairs={{1,0},{2,1},{3,2},{4,3},{5,4},{6,5},{7,6},{9,8},{10,9},{11,10},{12... | collective-permute-start | bytes 280376 | tf_op jit(solution)/shard_map/ppermute | solution.py:559
  30.9 1.0 %pick.1 = (f32[4,128]{1,0:T(4,128)S(1)}, f32[4,128]{1,0:T(4,128)S(1)}) custom-call(s32[3]{0:T(128)S(1)} %pad_add_fusion.where_ref, bf16[4,2,4,16,384]{4,3,2,1,0:T(8,128)(2,1)S(1)} %pad_maximum_fusion.refs_0_.fourier_ref, bf16[4,2,640,256]{3,2,1,0:T(8,128)(2,1)S(1)} %wind_tables.1.table_ref), custom_call_target="tpu_custom_call" | custom-call | flops 1000000000 | bytes 2000000 | tf_op jit(solution)/shard_map/pick/pallas_call | solution.py:351
  32.0 0.1 collective-permute-start.10
  32.1 2.7 %collective-permute-start.8 = (f32[4,128]{1,0:T(4,128)S(1)}, f32[4,128]{1,0:T(4,128)S(1)}, u32[]{:S(2)}, u32[]{:S(2)}) collective-permute-start(f32[4,128]{1,0:T(4,128)S(1)} %get-tuple-element.22), channel_id=1, source_target_pairs={{0,1},{1,0},{2,3},{3,2},{4,5},{5,4},{6,7},{7,6},{8,9},{9,8},{10,11... | collective-permute-start | bytes 6152 | tf_op jit(solution)/shard_map/ppermute | solution.py:709
  34.8 0.0 collective-permute-start.9
  34.8 0.0 collective-permute-done.6.west_ref
  34.8 1.5 %collective-permute-done.7.east_ref = f32[18,2,649]{2,1,0:T(2,128)S(1)} collective-permute-done((f32[18,2,649]{2,1,0:T(2,128)S(1)}, f32[18,2,649]{2,1,0:T(2,128)S(1)}, u32[]{:S(2)}, u32[]{:S(2)}) %collective-permute-start.7) | collective-permute-done | bytes 93488 | tf_op jit(solution)/shard_map/ppermute | solution.py:559
  36.3 3.4 %advect.1.density_ref = f32[16,32,648]{2,1,0:T(8,128)S(1)} custom-call(s32[3]{0:T(128)S(1)} %pad_add_fusion.where_ref, f32[2,16,648]{2,1,0:T(8,128)S(1)} %copy-done.5, f32[16,32,648]{2,1,0:T(8,128)S(1)} %copy-done, s32[16,32]{1,0:T(8,128)S(1)} %copy-done.2, f32[2,32,649]{2,1,0:T(8,128)S(1)} %collective-permute-done.5.low_ref.high_ref, ...), custom_call_target="tpu_custom_call" | custom-call | flops 2600000000 | bytes 4000000 | tf_op jit(solution)/shard_map/advect/pallas_call | solution.py:536
  39.6 0.0 collective-permute-done.10.other_far_ref
  39.7 0.0 collective-permute-done.8.own_far_ref
  39.7 0.0 collective-permute-done.9.other_ref
  39.7 1.6 %stress.1 = (f32[2,4,128]{2,1,0:T(4,128)S(1)}, f32[3,4,128]{2,1,0:T(4,128)S(1)}) custom-call(s32[3]{0:T(128)S(1)} %pad_add_fusion.where_ref, f32[2,16,648]{2,1,0:T(8,128)S(1)} %copy-done.5, f32[16,32,648]{2,1,0:T(8,128)S(1)} %advect.1.density_ref, f32[4,128]{1,0:T(4,128)S(1)} %get-tuple-element.21.own_ref, f32[4,128]{1,0:T(4,128)S(1)} %collective-permute-done.8.own_far_ref, ...), custom_call_target="tpu_custom_call" | custom-call | flops 1500000000 | bytes 2000000 | tf_op jit(solution)/shard_map/stress/pallas_call | solution.py:609
  41.3 0.0 collective-permute-start.11
  41.4 1.2 %collective-permute-done.11.far_ref = f32[2,4,128]{2,1,0:T(4,128)S(1)} collective-permute-done((f32[2,4,128]{2,1,0:T(4,128)S(1)}, f32[2,4,128]{2,1,0:T(4,128)S(1)}, u32[]{:S(2)}, u32[]{:S(2)}) %collective-permute-start.11) | collective-permute-done | bytes 4128 | tf_op jit(solution)/shard_map/ppermute | solution.py:709
  42.5 0.4 collective-permute-start.12
  42.9 3.2 %collective-permute-done.12.refs_1_ = f32[1,4,128]{2,1,0:T(4,128)S(1)} collective-permute-done((f32[1,4,128]{2,1,0:T(4,128)S(1)}, f32[1,4,128]{2,1,0:T(4,128)S(1)}, u32[]{:S(2)}, u32[]{:S(2)}) %collective-permute-start.12) | collective-permute-done | bytes 2080 | tf_op jit(solution)/shard_map/ppermute | solution.py:709
  46.2 1.7 %collective-permute-start.13 = (f32[2,4,128]{2,1,0:T(4,128)S(1)}, f32[2,4,128]{2,1,0:T(4,128)S(1)}, u32[]{:S(2)}, u32[]{:S(2)}) collective-permute-start(f32[2,4,128]{2,1,0:T(4,128)S(1)} %pad_maximum_fusion.3), channel_id=1, source_target_pairs={{0,4},{1,5},{2,6},{3,7},{4,0},{5,1},{6,2},{7,3},{8,12},{9,13},{10,... | collective-permute-start | bytes 12296 | tf_op jit(solution)/shard_map/ppermute | solution.py:709
  47.9 2.9 %collective-permute-start.4 = (bf16[4,2,4,16,384]{4,3,2,1,0:T(8,128)(2,1)S(1)}, bf16[4,2,4,16,384]{4,3,2,1,0:T(8,128)(2,1)S(1)}, u32[]{:S(2)}, u32[]{:S(2)}) collective-permute-start(bf16[4,2,4,16,384]{4,3,2,1,0:T(8,128)(2,1)S(1)} %pad_maximum_fusion.refs_0_.fourier_ref), channel_id=1, source_target_pairs={{0,1},{1,0},{2,3},{3,2},{4,5},{5,4},{6,7},{7,6},{8,9},{9,8},{10,11... | collective-permute-start | bytes 1179656 | tf_op jit(solution)/shard_map/ppermute | solution.py:709
  50.8 0.0 collective-permute-done.13.refs_2_
  50.8 0.0 copy-start.3
  50.8 1.6 %collective-permute-start.14 = (f32[4,4,128]{2,1,0:T(4,128)S(1)}, f32[4,4,128]{2,1,0:T(4,128)S(1)}, u32[]{:S(2)}, u32[]{:S(2)}) collective-permute-start(f32[4,4,128]{2,1,0:T(4,128)S(1)} %pad_maximum_fusion.2), channel_id=1, source_target_pairs={{0,1},{1,0},{2,3},{3,2},{4,5},{5,4},{6,7},{7,6},{8,9},{9,8},{10,11... | collective-permute-start | bytes 24584 | tf_op jit(solution)/shard_map/ppermute | solution.py:709
  52.5 3.0 %spectra.1 = f32[16,32,648]{2,1,0:T(8,128)} custom-call(s32[3]{0:T(128)S(1)} %pad_add_fusion.where_ref, f32[2,16,648]{2,1,0:T(8,128)S(1)} %copy-done.5, f32[16,32,648]{2,1,0:T(8,128)S(1)} %advect.1.density_ref, f32[3,4,128]{2,1,0:T(4,128)S(1)} %get-tuple-element.23.points_ref, f32[2,4,128]{2,1,0:T(4,128)S(1)} %get-tuple-element.24.sums_ref, ...), custom_call_target="tpu_custom_call" | custom-call | flops 2500000000 | bytes 3000000 | tf_op jit(solution)/shard_map/spectra/pallas_call | solution.py:652
  55.4 3.5 %collective-permute-done.14.refs_3_ = f32[4,4,128]{2,1,0:T(4,128)S(1)} collective-permute-done((f32[4,4,128]{2,1,0:T(4,128)S(1)}, f32[4,4,128]{2,1,0:T(4,128)S(1)}, u32[]{:S(2)}, u32[]{:S(2)}) %collective-permute-start.14) | collective-permute-done | bytes 8224 | tf_op jit(solution)/shard_map/ppermute | solution.py:709
  59.0 0.0 copy-done.3
  59.0 1.3 %charnock.1 = f32[4,512]{1,0:T(4,128)} custom-call(s32[3]{0:T(128)S(1)} %pad_add_fusion.where_ref, s32[8]{0:T(128)S(1)} %copy-done.4, s32[4,512]{1,0:T(4,128)S(1)} %copy-done.3, f32[1,4,128]{2,1,0:T(4,128)S(1)} %add_sqrt_fusion.refs_0_, f32[1,4,128]{2,1,0:T(4,128)S(1)} %collective-permute-done.12.refs_1_, f32[2,4,128]{2,1,0:T(4,128)S(1)} %collective-permute-done.13.refs_2_, ...), custom_call_target="tpu_custom_call" | custom-call | flops 1000000000 | bytes 100000 | tf_op jit(solution)/shard_map/charnock/pallas_call | solution.py:696
  60.2 0.0 collective-permute-done.4.refs_1_
  60.2 4.5 %synthesis.1 = bf16[4,8,8,512]{3,2,1,0:T(8,128)(2,1)} custom-call(s32[3]{0:T(128)S(1)} %pad_add_fusion.where_ref, s32[8]{0:T(128)S(1)} %copy-done.4, bf16[4,2,4,16,384]{4,3,2,1,0:T(8,128)(2,1)S(1)} %pad_maximum_fusion.refs_0_.fourier_ref, bf16[4,2,4,16,384]{4,3,2,1,0:T(8,128)(2,1)S(1)} %collective-permute-done.4.refs_1_), custom_call_target="tpu_custom_call" | custom-call | flops 3500000000 | bytes 2000000 | tf_op jit(solution)/shard_map/synthesis/pallas_call | solution.py:313
  (10 shorter events, 0.0 us)
Async XLA Ops:
  0.7 11.3 %copy-start = (f32[16,32,648]{2,1,0:T(8,128)S(1)}, f32[16,32,648]{2,1,0:T(8,128)}, u32[]{:S(2)}) copy-start(f32[16,32,648]{2,1,0:T(8,128)} %spectra_ref.3) | copy-start | bytes 3981316
  0.7 11.3 %copy-start.2 = (s32[16,32]{1,0:T(8,128)S(1)}, s32[16,32]{1,0:T(8,128)}, u32[]{:S(2)}) copy-start(s32[16,32]{1,0:T(8,128)} %mask_ref.3) | copy-start | bytes 6148
  0.7 18.2 %copy-start.1 = (s32[16,256]{1,0:T(8,128)S(1)}, s32[16,256]{1,0:T(8,128)}, u32[]{:S(2)}) copy-start(s32[16,256]{1,0:T(8,128)} %column_ref.1) | copy-start | bytes 49156
  0.7 18.2 %copy-start.4 = (s32[8]{0:T(128)S(1)}, s32[8]{0:T(128)}, u32[]{:S(2)}) copy-start(s32[8]{0:T(128)} %count_ref.5) | copy-start | bytes 100
  8.9 5.2 %collective-permute-start = (bf16[4,16,384]{2,1,0:T(8,128)(2,1)S(1)}, bf16[4,16,384]{2,1,0:T(8,128)(2,1)S(1)}, u32[]{:S(2)}, u32[]{:S(2)}) collective-permute-start(bf16[4,16,384]{2,1,0:T(8,128)(2,1)S(1)} %get-tuple-element.15), channel_id=1, source_target_pairs={{0,8},{8,0},{1,9},{9,1},{2,10},{10,2},{3,11},{11,3},{4,12},{12,4},... | collective-permute-start | bytes 147464 | tf_op jit(solution)/shard_map/ppermute | solution.py:755
  12.7 12.9 %collective-permute-start.5 = (f32[2,32,649]{2,1,0:T(8,128)S(1)}, f32[2,32,649]{2,1,0:T(8,128)S(1)}, u32[]{:S(2)}, u32[]{:S(2)}) collective-permute-start(f32[2,32,649]{2,1,0:T(8,128)S(1)} %get-tuple-element.16), channel_id=1, source_target_pairs={{0,8},{8,0},{1,9},{9,1},{2,10},{10,2},{3,11},{11,3},{4,12},{12,4},... | collective-permute-start | bytes 498440 | tf_op jit(solution)/shard_map/ppermute | solution.py:555
  14.2 7.2 %collective-permute-start.3 = (bf16[2,4,16,384]{3,2,1,0:T(8,128)(2,1)S(1)}, bf16[2,4,16,384]{3,2,1,0:T(8,128)(2,1)S(1)}, u32[]{:S(2)}, u32[]{:S(2)}) collective-permute-start(bf16[2,4,16,384]{3,2,1,0:T(8,128)(2,1)S(1)} %get-tuple-element.26), channel_id=1, source_target_pairs={{0,6},{1,7},{2,4},{3,5},{4,2},{5,3},{6,0},{7,1},{8,14},{9,15},{10,... | collective-permute-start | bytes 294920 | tf_op jit(solution)/shard_map/ppermute | solution.py:709
  18.3 6.2 %collective-permute-start.1 = (bf16[2,4,16,384]{3,2,1,0:T(8,128)(2,1)S(1)}, bf16[2,4,16,384]{3,2,1,0:T(8,128)(2,1)S(1)}, u32[]{:S(2)}, u32[]{:S(2)}) collective-permute-start(bf16[2,4,16,384]{3,2,1,0:T(8,128)(2,1)S(1)} %get-tuple-element.26), channel_id=1, source_target_pairs={{0,2},{1,3},{2,0},{3,1},{4,6},{5,7},{6,4},{7,5},{8,10},{9,11},{10,... | collective-permute-start | bytes 294920 | tf_op jit(solution)/shard_map/ppermute | solution.py:709
  18.3 7.3 %collective-permute-start.2 = (bf16[2,4,16,384]{3,2,1,0:T(8,128)(2,1)S(1)}, bf16[2,4,16,384]{3,2,1,0:T(8,128)(2,1)S(1)}, u32[]{:S(2)}, u32[]{:S(2)}) collective-permute-start(bf16[2,4,16,384]{3,2,1,0:T(8,128)(2,1)S(1)} %get-tuple-element.26), channel_id=1, source_target_pairs={{0,4},{1,5},{2,6},{3,7},{4,0},{5,1},{6,2},{7,3},{8,12},{9,13},{10,... | collective-permute-start | bytes 294920 | tf_op jit(solution)/shard_map/ppermute | solution.py:709
  25.6 10.7 %copy-start.5 = (f32[2,16,648]{2,1,0:T(8,128)S(1)}, f32[2,16,648]{2,1,0:T(8,128)}, u32[]{:S(2)}) copy-start(f32[2,16,648]{2,1,0:T(8,128)} %constant.19.clone.bins_ref) | copy-start | bytes 248836
  26.2 8.6 %collective-permute-start.6 = (f32[18,2,649]{2,1,0:T(2,128)S(1)}, f32[18,2,649]{2,1,0:T(2,128)S(1)}, u32[]{:S(2)}, u32[]{:S(2)}) collective-permute-start(f32[18,2,649]{2,1,0:T(2,128)S(1)} %get-tuple-element.19), channel_id=1, source_target_pairs={{0,1},{1,2},{2,3},{3,4},{4,5},{5,6},{6,7},{8,9},{9,10},{10,11},{11... | collective-permute-start | bytes 280376 | tf_op jit(solution)/shard_map/ppermute | solution.py:559
  29.6 6.6 %collective-permute-start.7 = (f32[18,2,649]{2,1,0:T(2,128)S(1)}, f32[18,2,649]{2,1,0:T(2,128)S(1)}, u32[]{:S(2)}, u32[]{:S(2)}) collective-permute-start(f32[18,2,649]{2,1,0:T(2,128)S(1)} %get-tuple-element.20), channel_id=1, source_target_pairs={{1,0},{2,1},{3,2},{4,3},{5,4},{6,5},{7,6},{9,8},{10,9},{11,10},{12... | collective-permute-start | bytes 280376 | tf_op jit(solution)/shard_map/ppermute | solution.py:559
  32.0 7.7 %collective-permute-start.10 = (f32[4,128]{1,0:T(4,128)S(1)}, f32[4,128]{1,0:T(4,128)S(1)}, u32[]{:S(2)}, u32[]{:S(2)}) collective-permute-start(f32[4,128]{1,0:T(4,128)S(1)} %get-tuple-element.22), channel_id=1, source_target_pairs={{0,17},{1,16},{2,19},{3,18},{4,21},{5,20},{6,23},{7,22},{16,1},{17... | collective-permute-start | bytes 6152 | tf_op jit(solution)/shard_map/ppermute | solution.py:718
  32.1 7.6 %collective-permute-start.8 = (f32[4,128]{1,0:T(4,128)S(1)}, f32[4,128]{1,0:T(4,128)S(1)}, u32[]{:S(2)}, u32[]{:S(2)}) collective-permute-start(f32[4,128]{1,0:T(4,128)S(1)} %get-tuple-element.22), channel_id=1, source_target_pairs={{0,1},{1,0},{2,3},{3,2},{4,5},{5,4},{6,7},{7,6},{8,9},{9,8},{10,11... | collective-permute-start | bytes 6152 | tf_op jit(solution)/shard_map/ppermute | solution.py:709
  34.8 4.9 %collective-permute-start.9 = (f32[4,128]{1,0:T(4,128)S(1)}, f32[4,128]{1,0:T(4,128)S(1)}, u32[]{:S(2)}, u32[]{:S(2)}) collective-permute-start(f32[4,128]{1,0:T(4,128)S(1)} %get-tuple-element.21.own_ref), channel_id=1, source_target_pairs={{0,16},{16,0},{1,17},{17,1},{2,18},{18,2},{3,19},{19,3},{4,20},{20... | collective-permute-start | bytes 6152 | tf_op jit(solution)/shard_map/ppermute | solution.py:709
  41.3 1.2 %collective-permute-start.11 = (f32[2,4,128]{2,1,0:T(4,128)S(1)}, f32[2,4,128]{2,1,0:T(4,128)S(1)}, u32[]{:S(2)}, u32[]{:S(2)}) collective-permute-start(f32[2,4,128]{2,1,0:T(4,128)S(1)} %get-tuple-element.24.sums_ref), channel_id=1, source_target_pairs={{0,16},{16,0},{1,17},{17,1},{2,18},{18,2},{3,19},{19,3},{4,20},{20... | collective-permute-start | bytes 12296 | tf_op jit(solution)/shard_map/ppermute | solution.py:709
  42.5 3.7 %collective-permute-start.12 = (f32[1,4,128]{2,1,0:T(4,128)S(1)}, f32[1,4,128]{2,1,0:T(4,128)S(1)}, u32[]{:S(2)}, u32[]{:S(2)}) collective-permute-start(f32[1,4,128]{2,1,0:T(4,128)S(1)} %add_sqrt_fusion.refs_0_), channel_id=1, source_target_pairs={{0,2},{1,3},{2,0},{3,1},{4,6},{5,7},{6,4},{7,5},{8,10},{9,11},{10,... | collective-permute-start | bytes 6152 | tf_op jit(solution)/shard_map/ppermute | solution.py:709
  46.2 4.6 %collective-permute-start.13 = (f32[2,4,128]{2,1,0:T(4,128)S(1)}, f32[2,4,128]{2,1,0:T(4,128)S(1)}, u32[]{:S(2)}, u32[]{:S(2)}) collective-permute-start(f32[2,4,128]{2,1,0:T(4,128)S(1)} %pad_maximum_fusion.3), channel_id=1, source_target_pairs={{0,4},{1,5},{2,6},{3,7},{4,0},{5,1},{6,2},{7,3},{8,12},{9,13},{10,... | collective-permute-start | bytes 12296 | tf_op jit(solution)/shard_map/ppermute | solution.py:709
  47.9 12.4 %collective-permute-start.4 = (bf16[4,2,4,16,384]{4,3,2,1,0:T(8,128)(2,1)S(1)}, bf16[4,2,4,16,384]{4,3,2,1,0:T(8,128)(2,1)S(1)}, u32[]{:S(2)}, u32[]{:S(2)}) collective-permute-start(bf16[4,2,4,16,384]{4,3,2,1,0:T(8,128)(2,1)S(1)} %pad_maximum_fusion.refs_0_.fourier_ref), channel_id=1, source_target_pairs={{0,1},{1,0},{2,3},{3,2},{4,5},{5,4},{6,7},{7,6},{8,9},{9,8},{10,11... | collective-permute-start | bytes 1179656 | tf_op jit(solution)/shard_map/ppermute | solution.py:709
  50.8 8.1 %copy-start.3 = (s32[4,512]{1,0:T(4,128)S(1)}, s32[4,512]{1,0:T(4,128)}, u32[]{:S(2)}) copy-start(s32[4,512]{1,0:T(4,128)} %source_ref.1) | copy-start | bytes 24580
  50.8 8.1 %collective-permute-start.14 = (f32[4,4,128]{2,1,0:T(4,128)S(1)}, f32[4,4,128]{2,1,0:T(4,128)S(1)}, u32[]{:S(2)}, u32[]{:S(2)}) collective-permute-start(f32[4,4,128]{2,1,0:T(4,128)S(1)} %pad_maximum_fusion.2), channel_id=1, source_target_pairs={{0,1},{1,0},{2,3},{3,2},{4,5},{5,4},{6,7},{7,6},{8,9},{9,8},{10,11... | collective-permute-start | bytes 24584 | tf_op jit(solution)/shard_map/ppermute | solution.py:709

commit v3 on v2

--- a/solution.py
+++ b/solution.py
@@ -14,7 +14,6 @@
 NDIR = 36
 NFREQ = 36
 LANES = 128
-PAD = 8
 
 two_pi = 2.0 * math.pi
 gravity = 9.81
@@ -150,17 +149,17 @@
 def sine_cosine(wave, slot, points, inverse):
     product = wave * slot
     remain = product - jnp.floor(product * inverse + 0.5) * points
-    turn = remain / points
+    turn = remain * inverse
     quarter = jnp.floor(4.0 * turn + 0.5)
     angle = (turn - 0.25 * quarter) * two_pi
     square = angle * angle
     sine = angle * (
         1.0
         + square
-        * (-1.0 / 6.0 + square * (1.0 / 120.0 + square * (-1.0 / 5040.0 + square / 362880.0)))
+        * (-1.0 / 6.0 + square * (1.0 / 120.0 + square * (-1.0 / 5040.0 + square * (1.0 / 362880.0))))
     )
     cosine = 1.0 + square * (
-        -0.5 + square * (1.0 / 24.0 + square * (-1.0 / 720.0 + square / 40320.0))
+        -0.5 + square * (1.0 / 24.0 + square * (-1.0 / 720.0 + square * (1.0 / 40320.0)))
     )
     side = jnp.abs(quarter) == 1.0
     back = jnp.abs(quarter) == 2.0
@@ -169,96 +168,156 @@
     return sine_out, cosine_out
 
 
-def build_tables(shape, band, points, slot, coarse, write):
+def build_tables(shape, band, points, slot, scratch, write):
     n_aa, waves_local, fine_rows = shape
+    coarse, fine = scratch
     coarse_local = waves_local // fine_rows
     coarse_rows, width = coarse.shape[1], slot.shape[1]
     points_row = jnp.full((1, width), points, f32)
     inverse = 1.0 / points_row
     active = slot < points_row
-    fine = lax.broadcasted_iota(jnp.int32, (fine_rows, width), 0).astype(f32)
-    sine_fine, cosine_fine = sine_cosine(fine, slot, points_row, inverse)
+    few = lax.broadcasted_iota(jnp.int32, (8, width), 0).astype(f32)
+    sine_few, cosine_few = sine_cosine(few, slot, points_row, inverse)
+    firsts = [lax.rem(band - shift + n_aa, n_aa) * waves_local for shift in range(n_aa)]
+    eights = fine_rows // 8
     row = lax.broadcasted_iota(jnp.int32, (coarse_rows, width), 0)
-    wave = jnp.zeros((coarse_rows, width), jnp.int32)
+    wave = (row + 1) * 8
     for shift in range(n_aa):
-        first = lax.rem(band - shift + n_aa, n_aa) * waves_local
-        inside = (row >= shift * coarse_local) & (row < (shift + 1) * coarse_local)
-        wave = jnp.where(inside, first + (row - shift * coarse_local) * fine_rows, wave)
+        wave = jnp.where(row == eights + shift, firsts[shift], wave)
     sine_coarse, cosine_coarse = sine_cosine(wave.astype(f32), slot, points_row, inverse)
-    coarse[0] = jnp.where(active, 2.0 * cosine_coarse, 0.0)
-    coarse[1] = jnp.where(active, -2.0 * sine_coarse, 0.0)
+    scale = jnp.where(row < eights, 1.0, jnp.where(active, 2.0, 0.0))
+    coarse[0] = scale * cosine_coarse
+    coarse[1] = scale * sine_coarse
+    for eight in range(eights):
+        rows = slice(eight * 8, (eight + 1) * 8)
+        if eight == 0:
+            fine[0, rows], fine[1, rows] = cosine_few, sine_few
+            continue
+        cosine_at = coarse[0, eight - 1 : eight, :]
+        sine_at = coarse[1, eight - 1 : eight, :]
+        fine[0, rows] = cosine_few * cosine_at - sine_few * sine_at
+        fine[1, rows] = sine_few * cosine_at + cosine_few * sine_at
+    index = lax.broadcasted_iota(jnp.int32, (fine_rows, LANES), 0)
     for shift in range(n_aa):
-        first = lax.rem(band - shift + n_aa, n_aa) * waves_local
-        for step in range(coarse_local):
-            at = shift * coarse_local + step
-            cosine_at = coarse[0, at : at + 1, :]
-            sine_at = coarse[1, at : at + 1, :]
-            cosine_part = cosine_at * cosine_fine + sine_at * sine_fine
-            sine_part = sine_at * cosine_fine - cosine_at * sine_fine
-            if step == 0:
-                weight = jnp.where(fine + first.astype(f32) == 0.0, 0.5, 1.0)
-                cosine_part = cosine_part * weight
-                sine_part = sine_part * weight
-            rows = slice(at * fine_rows, (at + 1) * fine_rows)
-            write(rows, cosine_part.astype(bf16), sine_part.astype(bf16))
+        at = eights + shift
+        weight = jnp.where(index + firsts[shift] == 0, 0.5, 1.0)
+        for start in range(0, width, LANES):
+            lanes = slice(start, start + LANES)
+            cosine_step = coarse[0, eights - 1 : eights, lanes]
+            sine_step = coarse[1, eights - 1 : eights, lanes]
+            twice = jnp.broadcast_to(2.0 * cosine_step, (fine_rows, LANES))
+            cosine_at, sine_at = coarse[0, at : at + 1, lanes], coarse[1, at : at + 1, lanes]
+            cosine_fine, sine_fine = fine[0, :, lanes], fine[1, :, lanes]
+            cosine_now = cosine_at * cosine_fine - sine_at * sine_fine
+            sine_now = -(sine_at * cosine_fine + cosine_at * sine_fine)
+            cosine_old = sine_old = None
+            for step in range(coarse_local):
+                first_row = (shift * coarse_local + step) * fine_rows
+                rows = slice(first_row, first_row + fine_rows)
+                if step == 0:
+                    write(rows, lanes, cosine_now * weight, sine_now * weight)
+                    cosine_next = cosine_now * cosine_step + sine_now * sine_step
+                    sine_next = sine_now * cosine_step - cosine_now * sine_step
+                else:
+                    write(rows, lanes, cosine_now, sine_now)
+                    cosine_next = twice * cosine_now - cosine_old
+                    sine_next = twice * sine_now - sine_old
+                cosine_old, sine_old = cosine_now, sine_now
+                cosine_now, sine_now = cosine_next, sine_next
         yield shift
 
 
-def table_shape(n_aa, waves_local):
+def table_shape(n_aa, waves_local, width):
     fine_rows = 32 if waves_local % 32 == 0 else 16
-    coarse_rows = -(-(n_aa * waves_local // fine_rows) // 8) * 8
-    return (n_aa, waves_local, fine_rows), coarse_rows
-
-
-def wind_table_kernel(shape, sizes, where_ref, count_ref, column_ref, out_ref, coarse):
+    coarse_rows = -(-(fine_rows // 8 + n_aa) // 8) * 8
+    scratch = [
+        pltpu.VMEM((2, 2, coarse_rows, width), f32),
+        pltpu.VMEM((2, 2, fine_rows, width), f32),
+    ]
+    return (n_aa, waves_local, fine_rows), scratch
+
+
+def wind_table_kernel(shape, sizes, where_ref, count_ref, column_ref, out_ref, *scratch):
     n_in, cycles, cycle_rows, columns_local = sizes
     band, column = where_ref[0], where_ref[1]
-    cycle = pl.program_id(0)
-    points = count_ref[band * cycles + cycle].astype(f32)
     lane = lax.broadcasted_iota(jnp.int32, (1, LANES), 1)
     per_block = LANES // columns_local
-    parts = []
-    for inner in range(n_in):
-        owner = jnp.bitwise_xor(column, inner)
-        part = jnp.zeros((1, LANES), jnp.int32)
-        for row in range(cycle_rows):
-            source = column_ref[pl.ds(cycle * cycle_rows + row, 1), :]
-            piece = source[:, :LANES]
-            for block in range(1, source.shape[1] // LANES):
-                piece = jnp.where(
-                    owner // per_block == block,
-                    source[:, block * LANES : (block + 1) * LANES],
-                    piece,
-                )
-            turn = lax.rem(row - lax.rem(owner, per_block) + per_block, per_block)
-            piece = pltpu.roll(piece, turn * columns_local, 1)
-            part = jnp.where(lane // columns_local == row, piece, part)
-        parts.append(part)
-    slot = jnp.concatenate(parts, axis=1).astype(f32)
-
-    def write(rows, cosine_part, sine_part):
-        out_ref[0, 0, rows, :] = cosine_part
-        out_ref[0, 1, rows, :] = sine_part
-
-    for _ in build_tables(shape, band, points, slot, coarse, write):
-        pass
+    for cycle in range(cycles):
+        points = count_ref[band * cycles + cycle].astype(f32)
+        parts = []
+        for inner in range(n_in):
+            owner = jnp.bitwise_xor(column, inner)
+            part = jnp.zeros((1, LANES), jnp.int32)
+            for row in range(cycle_rows):
+                at = cycle * cycle_rows + row
+                source = column_ref[at : at + 1, :]
+                piece = source[:, :LANES]
+                for block in range(1, source.shape[1] // LANES):
+                    piece = jnp.where(
+                        owner // per_block == block,
+                        source[:, block * LANES : (block + 1) * LANES],
+                        piece,
+                    )
+                turn = lax.rem(row - lax.rem(owner, per_block) + per_block, per_block)
+                piece = pltpu.roll(piece, turn * columns_local, 1)
+                part = jnp.where(lane // columns_local == row, piece, part)
+            parts.append(part)
+        slot = jnp.concatenate(parts, axis=1).astype(f32)
+
+        def write(rows, lanes, cosine_part, sine_part):
+            out_ref[cycle, 0, rows, lanes] = cosine_part.astype(bf16)
+            out_ref[cycle, 1, rows, lanes] = sine_part.astype(bf16)
+
+        own = [ref.at[cycle % 2] for ref in scratch]
+        for _ in build_tables(shape, band, points, slot, own, write):
+            pass
 
 
 def wind_tables(wind_column, counts, where, n_aa, waves_local, n_in, sizes):
     cycles = sizes[0]
-    shape, coarse_rows = table_shape(n_aa, waves_local)
     waves, width = n_aa * waves_local, n_in * LANES
+    shape, scratch = table_shape(n_aa, waves_local, width)
     return pl.pallas_call(
         functools.partial(wind_table_kernel, shape, (n_in,) + sizes),
-        grid=(cycles,),
         in_specs=[SMEM_SPEC, SMEM_SPEC, vmem_spec()],
-        out_specs=pl.BlockSpec((1, 2, waves, width), lambda i: (i, 0, 0, 0)),
+        out_specs=vmem_spec(),
         out_shape=jax.ShapeDtypeStruct((cycles, 2, waves, width), bf16),
-        scratch_shapes=[pltpu.VMEM((2, coarse_rows, width), f32)],
-        compiler_params=params(),
+        scratch_shapes=scratch,
+        compiler_params=params(0),
         cost_estimate=cost(1_700_000_000, 3_000_000),
         name="wind_tables",
     )(where, counts, wind_column)
+
+
+def grid_table_kernel(shape, cycles, where_ref, count_ref, out_ref, *scratch):
+    band, column = where_ref[0], where_ref[1]
+    width = out_ref.shape[3]
+    slot = column * width + lax.broadcasted_iota(jnp.int32, (1, width), 1)
+    for cycle in range(cycles):
+        points = count_ref[band * cycles + cycle].astype(f32)
+
+        def write(rows, lanes, cosine_part, sine_part):
+            out_ref[cycle, 0, rows, lanes] = cosine_part.astype(bf16)
+            out_ref[cycle, 1, rows, lanes] = sine_part.astype(bf16)
+
+        own = [ref.at[cycle % 2] for ref in scratch]
+        for _ in build_tables(shape, band, points, slot.astype(f32), own, write):
+            pass
+
+
+def grid_tables(counts, where, cycles, n_aa, waves_local, width):
+    waves = n_aa * waves_local
+    shape, scratch = table_shape(n_aa, waves_local, width)
+    return pl.pallas_call(
+        functools.partial(grid_table_kernel, shape, cycles),
+        in_specs=[SMEM_SPEC, SMEM_SPEC],
+        out_specs=vmem_spec(),
+        out_shape=jax.ShapeDtypeStruct((cycles, 2, waves, width), bf16),
+        scratch_shapes=scratch,
+        compiler_params=params(0),
+        cost_estimate=cost(2_000_000_000, 5_000_000),
+        name="grid_tables",
+    )(where, counts)
 
 
 def stack_rows(pieces):
@@ -267,63 +326,61 @@
     return jnp.concatenate([piece.astype(f32) for piece in pieces], axis=0).astype(bf16)
 
 
-def synthesis_kernel(shape, n_out, n_in, where_ref, count_ref, *refs):
-    fourier, (out_ref, coarse, table) = refs[:n_in], refs[n_in:]
-    _, waves_local, _ = shape
-    band, column = where_ref[0], where_ref[1]
-    cycle = pl.program_id(0)
-    points = count_ref[band * pl.num_programs(0) + cycle].astype(f32)
-    levels, width = out_ref.shape[2:]
+def synthesis_kernel(shape, n_out, n_in, where_ref, *refs):
+    fourier, (table_ref, out_hbm, grid, done) = refs[:n_in], refs[n_in:]
+    n_aa, waves_local = shape
+    column = where_ref[1]
+    cycles, _, levels, _ = grid.shape
     pc = fourier[0].shape[3]
-    slot = column * width + lax.broadcasted_iota(jnp.int32, (1, width), 1)
-
-    def write(rows, cosine_part, sine_part):
-        table[0, rows, :] = cosine_part
-        table[1, rows, :] = sine_part
-
-    cosine_sum = None
-    sine_sum = None
-    for shift in build_tables(shape, band, points, slot.astype(f32), coarse, write):
-        left = stack_rows(
-            [
-                fourier[inner][outer, shift, 0, :, :waves_local]
-                for inner in range(n_in)
-                for outer in range(n_out)
-            ]
-        )
-        rows = slice(shift * waves_local, (shift + 1) * waves_local)
-        cosine_part = jnp.dot(left, table[0, rows, :], preferred_element_type=f32)
-        sine_part = jnp.dot(left, table[1, rows, :], preferred_element_type=f32)
-        cosine_sum = cosine_part if cosine_sum is None else cosine_sum + cosine_part
-        sine_sum = sine_part if sine_sum is None else sine_sum + sine_part
-    for inner in range(n_in):
-        for outer in range(n_out):
-            at = (inner * n_out + outer) * pc
-            value = cosine_sum[at : at + levels] + sine_sum[at + levels : at + pc]
-            source = jnp.bitwise_xor(column, outer * n_in + inner)
-            out_ref[0, source] = value.astype(bf16)
-
-
-def synthesis(fourier, counts, where, n_aa, waves_local, n_in, width):
-    n_out, _, cycles, pc, lanes = fourier[0].shape
+    copies = []
+    for cycle in range(cycles):
+        cosine_sum = None
+        sine_sum = None
+        for shift in range(n_aa):
+            left = stack_rows(
+                [
+                    fourier[inner][outer, shift, cycle, :, :waves_local]
+                    for inner in range(n_in)
+                    for outer in range(n_out)
+                ]
+            )
+            rows = slice(shift * waves_local, (shift + 1) * waves_local)
+            cosine_part = jnp.dot(left, table_ref[cycle, 0, rows, :], preferred_element_type=f32)
+            sine_part = jnp.dot(left, table_ref[cycle, 1, rows, :], preferred_element_type=f32)
+            cosine_sum = cosine_part if cosine_sum is None else cosine_sum + cosine_part
+            sine_sum = sine_part if sine_sum is None else sine_sum + sine_part
+        for inner in range(n_in):
+            for outer in range(n_out):
+                at = (inner * n_out + outer) * pc
+                value = cosine_sum[at : at + levels] + sine_sum[at + levels : at + pc]
+                source = jnp.bitwise_xor(column, outer * n_in + inner)
+                grid[cycle, source] = value.astype(bf16)
+        copies.append(
+            pltpu.make_async_copy(grid.at[cycle], out_hbm.at[cycle], done.at[cycle])
+        )
+        copies[-1].start()
+    for copy in copies:
+        copy.wait()
+
+
+def synthesis(fourier, table, where, n_aa, waves_local, n_in):
+    n_out, _, cycles, pc, _ = fourier[0].shape
     levels = pc // 2
+    width = table.shape[3]
     n_ba = n_out * n_in
-    shape, coarse_rows = table_shape(n_aa, waves_local)
-    block = pl.BlockSpec((n_out, n_aa, 1, pc, lanes), lambda i: (0, 0, i, 0, 0))
-    return pl.pallas_call(
-        functools.partial(synthesis_kernel, shape, n_out, n_in),
-        grid=(cycles,),
-        in_specs=[SMEM_SPEC, SMEM_SPEC] + [block] * n_in,
-        out_specs=pl.BlockSpec((1, n_ba, levels, width), lambda i: (i, 0, 0, 0)),
+    return pl.pallas_call(
+        functools.partial(synthesis_kernel, (n_aa, waves_local), n_out, n_in),
+        in_specs=[SMEM_SPEC] + [vmem_spec()] * (n_in + 1),
+        out_specs=pl.BlockSpec(memory_space=pltpu.HBM),
         out_shape=jax.ShapeDtypeStruct((cycles, n_ba, levels, width), bf16),
         scratch_shapes=[
-            pltpu.VMEM((2, coarse_rows, width), f32),
-            pltpu.VMEM((2, n_aa * waves_local, width), bf16),
+            pltpu.VMEM((cycles, n_ba, levels, width), bf16),
+            pltpu.SemaphoreType.DMA((cycles,)),
         ],
-        compiler_params=params(),
-        cost_estimate=cost(3_500_000_000, 2_000_000),
+        compiler_params=params(0),
+        cost_estimate=cost(3_000_000_000, 2_000_000),
         name="synthesis",
-    )(where, counts, *fourier)
+    )(where, *fourier, table)
 
 
 def pick_kernel(shape, where_ref, fourier_ref, table_ref, *out_refs):
@@ -415,8 +472,8 @@
     for side_ref, start in ((west_ref, 0), (east_ref, columns - 2)):
         for at in range(2):
             own = column_of(mask, start + at)
-            side_ref[:, at, :bins] = spectra_ref[:, start + at, :] * own
-            side_ref[:, at, bins:] = own
+            side_ref[at, :, :bins] = spectra_ref[:, start + at, :] * own
+            side_ref[at, :, bins:] = own
 
 
 def pack(where, spectra, mask, n_aa):
@@ -427,7 +484,7 @@
         in_specs=[SMEM_SPEC] + [vmem_spec()] * 2,
         out_specs=[vmem_spec()] * (n_rows + 2),
         out_shape=[jax.ShapeDtypeStruct((2, columns, bins + 1), f32)] * n_rows
-        + [jax.ShapeDtypeStruct((rows, 2, bins + 1), f32)] * 2,
+        + [jax.ShapeDtypeStruct((2, rows, bins + 1), f32)] * 2,
         scratch_shapes=[pltpu.VMEM((LANES, LANES), f32)],
         compiler_params=params(0),
         cost_estimate=cost(600_000_000, 500_000),
@@ -442,29 +499,35 @@
 
 
 def sides_kernel(n_aa, where_ref, low_ref, high_ref, west_ref, east_ref, out_west, out_east):
-    rows, _, _ = west_ref.shape
+    rows = west_ref.shape[1]
     columns = low_ref.shape[1]
     low, high = rows_beyond(n_aa, where_ref, low_ref, high_ref, 1)
-    for side_ref, out_ref, cut in (
-        (west_ref, out_west, slice(0, 2)),
-        (east_ref, out_east, slice(columns - 2, columns)),
+    for side_ref, out_ref, start in (
+        (west_ref, out_west, 0),
+        (east_ref, out_east, columns - 2),
     ):
-        out_ref[0] = low[cut]
-        out_ref[1 : rows + 1] = side_ref[...]
-        out_ref[rows + 1] = high[cut]
+        for at in range(2):
+            cut = slice(start + at, start + at + 1)
+            out_ref[at, 0:1] = low[cut]
+            out_ref[at, 1 : rows + 1] = side_ref[at]
+            out_ref[at, rows + 1 :] = high[cut]
 
 
 def pack_sides(where, low, high, west, east, n_aa):
-    rows, _, count = west.shape
+    _, rows, count = west.shape
     return pl.pallas_call(
         functools.partial(sides_kernel, n_aa),
         in_specs=[SMEM_SPEC] + [vmem_spec()] * 4,
         out_specs=[vmem_spec()] * 2,
-        out_shape=[jax.ShapeDtypeStruct((rows + 2, 2, count), f32)] * 2,
+        out_shape=[jax.ShapeDtypeStruct((2, rows + 2, count), f32)] * 2,
         compiler_params=params(0),
         cost_estimate=cost(300_000_000, 500_000),
         name="pack_sides",
     )(where, low, high, west, east)
+
+
+def lane_cuts(count):
+    return [slice(at, min(at + LANES, count)) for at in range(0, count, LANES)]
 
 
 def advect_kernel(
@@ -480,67 +543,93 @@
     out_ref,
     first,
     second,
+    edges,
+    masks,
     padded,
 ):
     rows, columns, bins = spectra_ref.shape
     half = where_ref[2]
-    wide = columns + 2 * PAD
     turned = transposed_mask(mask_ref, padded)
-    edge = jnp.zeros((PAD, bins), f32)
-    for row in range(rows + 4):
-        first[row, 0:PAD] = edge
-        first[row, PAD + columns :] = edge
-    inside = slice(PAD, PAD + columns)
+
+    def spread(column):
+        return jnp.broadcast_to(column, (columns, LANES))
+
     low_far, high_far = rows_beyond(n_aa, where_ref, low_ref, high_ref, 0)
     low_near, high_near = rows_beyond(n_aa, where_ref, low_ref, high_ref, 1)
-    first[0, inside] = low_far[:, :bins]
-    first[1, inside] = low_near[:, :bins]
-    first[rows + 2, inside] = high_near[:, :bins]
-    first[rows + 3, inside] = high_far[:, :bins]
-    masks = [low_near[:, bins:]]
+    first[0] = low_far[:, :bins]
+    first[1] = low_near[:, :bins]
+    first[rows + 2] = high_near[:, :bins]
+    first[rows + 3] = high_far[:, :bins]
+    masks[0] = spread(low_near[:, bins:])
+    masks[rows + 1] = spread(high_near[:, bins:])
     for row in range(rows):
-        masks.append(column_of(turned, row)[:columns])
-        first[row + 2, inside] = spectra_ref[row] * masks[-1]
-    masks.append(high_near[:, bins:])
-    first[1 : rows + 3, PAD - 2 : PAD] = west_ref[:, :, :bins]
-    first[1 : rows + 3, PAD + columns : PAD + columns + 2] = east_ref[:, :, :bins]
-    keep, east_pos, east_neg, north_pos, north_neg = (
-        bins_ref[half, at : at + 1] for at in range(5)
-    )
-
-    def update(source, at):
-        centre = source[at]
-        western = pltpu.roll(centre, 1, 0)
-        eastern = pltpu.roll(centre, wide - 1, 0)
+        own = spread(column_of(turned, row)[:columns])
+        masks[row + 1] = own
+        for cut in lane_cuts(bins):
+            first[row + 2, :, cut] = spectra_ref[row, :, cut] * own[:, : cut.stop - cut.start]
+
+    def update(cut, centre, western, eastern, southern, northern):
+        keep, east_pos, east_neg, north_pos, north_neg = (
+            bins_ref[half, at : at + 1, cut] for at in range(5)
+        )
         return (
             keep * centre
             + east_pos * western
             + east_neg * eastern
-            + north_pos * source[at - 1]
-            + north_neg * source[at + 1]
-        )
-
-    for row in range(rows + 2):
-        value = update(first, row + 1)
-        second[row, 0:PAD] = value[0:PAD] * west_ref[row, 1:2, bins:]
-        second[row, inside] = value[inside] * masks[row]
-        second[row, PAD + columns :] = value[PAD + columns :] * east_ref[row, 0:1, bins:]
-    for row in range(rows):
-        value = update(second, row + 1)
-        out_ref[row] = value[inside] * masks[row + 1]
+            + north_pos * southern
+            + north_neg * northern
+        )
+
+    beside = slice(1, rows + 1)
+    for cut in lane_cuts(bins):
+        near, far = west_ref[1, :, cut], west_ref[0, :, cut]
+        inside = first[2 : rows + 2, 0, cut]
+        edges[0, :, cut] = west_ref[1, beside, bins:] * update(
+            cut, near[1 : rows + 1], far[1 : rows + 1], inside, near[:rows], near[2:]
+        )
+        near, far = east_ref[0, :, cut], east_ref[1, :, cut]
+        inside = first[2 : rows + 2, columns - 1, cut]
+        edges[1, :, cut] = east_ref[0, beside, bins:] * update(
+            cut, near[1 : rows + 1], inside, far[1 : rows + 1], near[:rows], near[2:]
+        )
+
+    def step(source, at, cut, west_column, east_column):
+        centre = source[at, :, cut]
+        place = lax.broadcasted_iota(jnp.int32, centre.shape, 0)
+        western = jnp.where(place == 0, west_column, pltpu.roll(centre, 1, 0))
+        eastern = jnp.where(
+            place == columns - 1, east_column, pltpu.roll(centre, columns - 1, 0)
+        )
+        return update(
+            cut, centre, western, eastern, source[at - 1, :, cut], source[at + 1, :, cut]
+        )
+
+    for cut in lane_cuts(bins):
+        size = cut.stop - cut.start
+        for row in range(rows + 2):
+            at = slice(row, row + 1)
+            value = step(first, row + 1, cut, west_ref[1, at, cut], east_ref[0, at, cut])
+            second[row, :, cut] = value * masks[row, :, :size]
+    for cut in lane_cuts(bins):
+        size = cut.stop - cut.start
+        for row in range(rows):
+            at = slice(row, row + 1)
+            value = step(second, row + 1, cut, edges[0, at, cut], edges[1, at, cut])
+            out_ref[row, :, cut] = value * masks[row + 1, :, :size]
 
 
 def advect(where, bins, spectra, mask, low, high, west, east, n_aa):
     rows, columns, count = spectra.shape
-    wide = columns + 2 * PAD
     return pl.pallas_call(
         functools.partial(advect_kernel, n_aa),
         in_specs=[SMEM_SPEC] + [vmem_spec()] * 7,
         out_specs=vmem_spec(),
         out_shape=jax.ShapeDtypeStruct(spectra.shape, f32),
         scratch_shapes=[
-            pltpu.VMEM((rows + 4, wide, count), f32),
-            pltpu.VMEM((rows + 2, wide, count), f32),
+            pltpu.VMEM((rows + 4, columns, count), f32),
+            pltpu.VMEM((rows + 2, columns, count), f32),
+            pltpu.VMEM((2, rows, count), f32),
+            pltpu.VMEM((rows + 2, columns, LANES), f32),
             pltpu.VMEM((LANES, LANES), f32),
         ],
         compiler_params=params(0),
@@ -620,42 +709,46 @@
     )(where, bins, density, *winds)
 
 
-def spectra_kernel(where_ref, bins_ref, density_ref, points_ref, sums_ref, far_ref, out_ref):
-    cycle = pl.program_id(0)
+def spectra_kernel(
+    where_ref, bins_ref, density_ref, points_ref, sums_ref, far_ref, out_hbm, value_ref, done
+):
     half = where_ref[2]
-    cycle_rows, columns, bins = density_ref.shape
+    rows, columns, bins = density_ref.shape
+    cycles = points_ref.shape[1]
+    cycle_rows = rows // cycles
     scaled = (sums_ref[1] + far_ref[1]) * (1.0 / energy_ref)
-    row = lax.broadcasted_iota(jnp.int32, (8, LANES), 0)
-
-    def own_row(values):
-        mine = lax.broadcasted_iota(jnp.int32, values.shape, 0) == cycle
-        return jnp.sum(jnp.where(mine, values, 0.0), axis=0, keepdims=True)
-
-    picked = jnp.where(
-        row == 0,
-        own_row(points_ref[0]),
-        jnp.where(row == 1, own_row(points_ref[1]), own_row(scaled * scaled)),
-    )
-    picked = jnp.transpose(picked)
+    east, north = as_columns(points_ref[0]), as_columns(points_ref[1])
+    energy = as_columns(scaled * scaled)
     along_cos, along_sin, decay = (bins_ref[half, at : at + 1] for at in (5, 6, 8))
-    density = density_ref[...].reshape(LANES, bins)
-    alignment = picked[:, 0:1] * along_cos + picked[:, 1:2] * along_sin
-    gain = growth * jnp.maximum(alignment - 1.0, 0.0)
-    value = density * (1.0 + gain) / (1.0 + decay * picked[:, 2:3])
-    out_ref[...] = value.reshape(cycle_rows, columns, bins)
+    copies = []
+    for cycle in range(cycles):
+        at = slice(cycle * cycle_rows, (cycle + 1) * cycle_rows)
+        own = slice(cycle, cycle + 1)
+        density = density_ref[at].reshape(LANES, bins)
+        alignment = east[:, own] * along_cos + north[:, own] * along_sin
+        gain = growth * jnp.maximum(alignment - 1.0, 0.0)
+        value = density * (1.0 + gain) / (1.0 + decay * energy[:, own])
+        value_ref[at] = value.reshape(cycle_rows, columns, bins)
+        copies.append(
+            pltpu.make_async_copy(value_ref.at[at], out_hbm.at[at], done.at[cycle])
+        )
+        copies[-1].start()
+    for copy in copies:
+        copy.wait()
 
 
 def final_spectra(where, bins, density, points, sums, far):
     cycles = points.shape[1]
-    rows, columns, count = density.shape
-    block = pl.BlockSpec((rows // cycles, columns, count), lambda i: (i, 0, 0))
     return pl.pallas_call(
         spectra_kernel,
-        grid=(cycles,),
-        in_specs=[SMEM_SPEC, vmem_spec(), block] + [vmem_spec()] * 3,
-        out_specs=block,
+        in_specs=[SMEM_SPEC] + [vmem_spec()] * 5,
+        out_specs=pl.BlockSpec(memory_space=pltpu.HBM),
         out_shape=jax.ShapeDtypeStruct(density.shape, f32),
-        compiler_params=params(1),
+        scratch_shapes=[
+            pltpu.VMEM(density.shape, f32),
+            pltpu.SemaphoreType.DMA((cycles,)),
+        ],
+        compiler_params=params(0),
         cost_estimate=cost(2_500_000_000, 3_000_000),
         name="spectra",
     )(where, bins, density, points, sums, far)
@@ -777,7 +870,8 @@
         pieces.append(exchange(sent, "ba", distance))
         order.append(tuple(far_at ^ distance for near in order for far_at in near))
     wave_spectra = final_spectra(where, bins, density, points, sums, far)
-    grid_winds = synthesis(inner, counts, where, n_aa, waves_local, n_in, slots_local)
+    grid_table = grid_tables(counts, where, cycles, n_aa, waves_local, slots_local)
+    grid_winds = synthesis(inner, grid_table, where, n_aa, waves_local, n_in)
     grid_winds = grid_winds.reshape(1, cycles, -1, slots_local)
     charnock = charnock_of(
         where, counts, pieces, tuple(order), roughness_source, columns_local

time: 64.9 us -> 63.9 us (0.985)
  waiting for transfers between devices: 15.3 us -> 18.4 us
  Pallas kernels: 26.3 us -> 24.2 us
  starting transfers between devices: 22.1 us -> 20.1 us
    ppermute x10, waiting for transfers between devices: 12.5 us -> 15.3 us  [exchange(): return lax.ppermute(value, axis, [(i, i ^ distance) for i in range(count)])]
    ppermute x10, starting transfers between devices: 14.2 us -> 12.3 us  [exchange(): return lax.ppermute(value, axis, [(i, i ^ distance) for i in range(count)])]
    pallas_call x1, Pallas kernels: 3.35 us -> 2.54 us  [advect(): pl.pallas_call(functools.partial(advect_kernel, n_aa), in_specs=[SMEM_SPE...]
    pallas_call x2 -> x3, Pallas kernels: 7.43 us -> 6.74 us  [the longest x1 2.46 us: synthesis(): pl.pallas_call(functools.partial(synthesis_kernel, (n_aa, waves_local), n...]
  transfers between devices with their start and end apart: 15 -> 15, of which waited for: 8 -> 7; matrix products, arithmetic and copies ran while one was open for 0% -> 0% of each run, Pallas kernels for 18% -> 18%
where the time goes in v3:
time: 63.9 us; the launch traced here: 63.7 us
  Pallas kernels  24.2 us (38%)
  starting transfers between devices  20.1 us (31%)
  waiting for transfers between devices  18.4 us (29%)
  between operations  0.79 us (1%)
    ppermute x10, waiting for transfers between devices, exchange(): return lax.ppermute(value, axis, [(i, i ^ distance) for i in range(count)])  15.3 us
    ppermute x10, starting transfers between devices, exchange(): return lax.ppermute(value, axis, [(i, i ^ distance) for i in range(count)])  12.3 us
    pallas_call x1, Pallas kernels, legendre_sums(): pl.pallas_call(functools.partial(legendre_kernel, shape), in_specs=[SMEM_...  8.21 us
    ppermute x1, starting transfers between devices, across(): lax.ppermute(sent[1], axis, forward)  3.4 us
    ppermute x1, starting transfers between devices, per_device(): parts.append(lax.ppermute(fourier[shift], 'aa', pairs))  3.07 us
    pallas_call x1, Pallas kernels, advect(): pl.pallas_call(functools.partial(advect_kernel, n_aa), in_specs=[SMEM_SPE...  2.54 us
    pallas_call x1, Pallas kernels, synthesis(): pl.pallas_call(functools.partial(synthesis_kernel, (n_aa, waves_local), n...  2.46 us
    pallas_call x1, Pallas kernels, final_spectra(): pl.pallas_call(spectra_kernel, in_specs=[SMEM_SPEC] + [vmem_spec()] * 5,...  2.16 us
  transfers between devices with their start and end apart: 15, of which 7 were waited for; matrix products, arithmetic and copies ran while one was open for 0% of the time, Pallas kernels for 18%

profile of v3, /device:TPU:0, one launch (start us, length us, event | category | flops | bytes accessed | tf_op | source)
XLA Modules:
  0.0 63.7 jit_solution(5124069334640485345)
XLA Ops:
  0.6 0.1 pad_add_fusion.where_ref
  0.7 8.2 %legendre.1 = (bf16[4,16,384]{2,1,0:T(8,128)(2,1)S(1)}, bf16[4,16,384]{2,1,0:T(8,128)(2,1)S(1)}) custom-call(s32[3]{0:T(128)S(1)} %pad_add_fusion.where_ref, bf16[10,256,1280]{2,1,0:T(8,128)(2,1)} %bitcast.19, bf16[10,512,1280]{2,1,0:T(8,128)(2,1)} %bitcast.18), custom_call_target="tpu_custom_call" | custom-call | flops 7000000000 | bytes 20000000 | tf_op jit(solution)/shard_map/legendre/pallas_call | solution.py:128
  8.9 3.1 %collective-permute-start = (bf16[4,16,384]{2,1,0:T(8,128)(2,1)S(1)}, bf16[4,16,384]{2,1,0:T(8,128)(2,1)S(1)}, u32[]{:S(2)}, u32[]{:S(2)}) collective-permute-start(bf16[4,16,384]{2,1,0:T(8,128)(2,1)S(1)} %get-tuple-element.15), channel_id=1, source_target_pairs={{0,8},{8,0},{1,9},{9,1},{2,10},{10,2},{3,11},{11,3},{4,12},{12,4},... | collective-permute-start | bytes 147464 | tf_op jit(solution)/shard_map/ppermute | solution.py:848
  12.0 0.0 copy-done
  12.0 0.0 copy-done.2
  12.0 0.7 %pack.1 = (f32[2,32,649]{2,1,0:T(8,128)S(1)}, f32[2,16,649]{2,1,0:T(8,128)S(1)}, f32[2,16,649]{2,1,0:T(8,128)S(1)}) custom-call(s32[3]{0:T(128)S(1)} %pad_add_fusion.where_ref, f32[16,32,648]{2,1,0:T(8,128)S(1)} %copy-done, s32[16,32]{1,0:T(8,128)S(1)} %copy-done.2), custom_call_target="tpu_custom_call" | custom-call | flops 600000000 | bytes 500000 | tf_op jit(solution)/shard_map/pack/pallas_call | solution.py:482
  12.7 0.1 collective-permute-start.5
  12.8 1.3 %collective-permute-done = bf16[4,16,384]{2,1,0:T(8,128)(2,1)S(1)} collective-permute-done((bf16[4,16,384]{2,1,0:T(8,128)(2,1)S(1)}, bf16[4,16,384]{2,1,0:T(8,128)(2,1)S(1)}, u32[]{:S(2)}, u32[]{:S(2)}) %collective-permute-start) | collective-permute-done | bytes 49184 | tf_op jit(solution)/shard_map/ppermute | solution.py:848
  14.2 4.1 %collective-permute-start.3 = (bf16[2,4,16,384]{3,2,1,0:T(8,128)(2,1)S(1)}, bf16[2,4,16,384]{3,2,1,0:T(8,128)(2,1)S(1)}, u32[]{:S(2)}, u32[]{:S(2)}) collective-permute-start(bf16[2,4,16,384]{3,2,1,0:T(8,128)(2,1)S(1)} %get-tuple-element.26), channel_id=1, source_target_pairs={{0,6},{1,7},{2,4},{3,5},{4,2},{5,3},{6,0},{7,1},{8,14},{9,15},{10,... | collective-permute-start | bytes 294920 | tf_op jit(solution)/shard_map/ppermute | solution.py:802
  18.3 0.0 collective-permute-start.2
  18.3 0.6 %collective-permute-start.1 = (bf16[2,4,16,384]{3,2,1,0:T(8,128)(2,1)S(1)}, bf16[2,4,16,384]{3,2,1,0:T(8,128)(2,1)S(1)}, u32[]{:S(2)}, u32[]{:S(2)}) collective-permute-start(bf16[2,4,16,384]{3,2,1,0:T(8,128)(2,1)S(1)} %get-tuple-element.26), channel_id=1, source_target_pairs={{0,2},{1,3},{2,0},{3,1},{4,6},{5,7},{6,4},{7,5},{8,10},{9,11},{10,... | collective-permute-start | bytes 294920 | tf_op jit(solution)/shard_map/ppermute | solution.py:802
  18.9 0.0 copy-done.1
  18.9 1.5 %wind_tables.1.table_ref = bf16[4,2,640,256]{3,2,1,0:T(8,128)(2,1)S(1)} custom-call(s32[3]{0:T(128)S(1)} %pad_add_fusion.where_ref, s32[8]{0:T(128)S(1)} %copy-done.4, s32[16,256]{1,0:T(8,128)S(1)} %copy-done.1), custom_call_target="tpu_custom_call" | custom-call | flops 1700000000 | bytes 3000000 | tf_op jit(solution)/shard_map/wind_tables/pallas_call | solution.py:280
  20.4 1.0 %collective-permute-done.3 = bf16[2,4,16,384]{3,2,1,0:T(8,128)(2,1)S(1)} collective-permute-done((bf16[2,4,16,384]{3,2,1,0:T(8,128)(2,1)S(1)}, bf16[2,4,16,384]{3,2,1,0:T(8,128)(2,1)S(1)}, u32[]{:S(2)}, u32[]{:S(2)}) %collective-permute-start.3) | collective-permute-done | bytes 98336 | tf_op jit(solution)/shard_map/ppermute | solution.py:802
  21.4 4.1 %collective-permute-done.2 = bf16[2,4,16,384]{3,2,1,0:T(8,128)(2,1)S(1)} collective-permute-done((bf16[2,4,16,384]{3,2,1,0:T(8,128)(2,1)S(1)}, bf16[2,4,16,384]{3,2,1,0:T(8,128)(2,1)S(1)}, u32[]{:S(2)}, u32[]{:S(2)}) %collective-permute-start.2) | collective-permute-done | bytes 98336 | tf_op jit(solution)/shard_map/ppermute | solution.py:802
  25.5 0.0 collective-permute-done.1
  25.5 0.1 pad_maximum_fusion.refs_0_.fourier_ref
  25.6 0.0 collective-permute-done.5.low_ref.high_ref
  25.6 0.6 pack_sides.1
  26.1 3.4 %collective-permute-start.6 = (f32[2,18,649]{2,1,0:T(8,128)S(1)}, f32[2,18,649]{2,1,0:T(8,128)S(1)}, u32[]{:S(2)}, u32[]{:S(2)}) collective-permute-start(f32[2,18,649]{2,1,0:T(8,128)S(1)} %get-tuple-element.19), channel_id=1, source_target_pairs={{0,1},{1,2},{2,3},{3,4},{4,5},{5,6},{6,7},{8,9},{9,10},{10,11},{11... | collective-permute-start | bytes 280376 | tf_op jit(solution)/shard_map/ppermute | solution.py:648
  29.5 1.3 %collective-permute-start.7 = (f32[2,18,649]{2,1,0:T(8,128)S(1)}, f32[2,18,649]{2,1,0:T(8,128)S(1)}, u32[]{:S(2)}, u32[]{:S(2)}) collective-permute-start(f32[2,18,649]{2,1,0:T(8,128)S(1)} %get-tuple-element.20), channel_id=1, source_target_pairs={{1,0},{2,1},{3,2},{4,3},{5,4},{6,5},{7,6},{9,8},{10,9},{11,10},{12... | collective-permute-start | bytes 280376 | tf_op jit(solution)/shard_map/ppermute | solution.py:648
  30.8 1.0 %pick.1 = (f32[4,128]{1,0:T(4,128)S(1)}, f32[4,128]{1,0:T(4,128)S(1)}) custom-call(s32[3]{0:T(128)S(1)} %pad_add_fusion.where_ref, bf16[4,2,4,16,384]{4,3,2,1,0:T(8,128)(2,1)S(1)} %pad_maximum_fusion.refs_0_.fourier_ref, bf16[4,2,640,256]{3,2,1,0:T(8,128)(2,1)S(1)} %wind_tables.1.table_ref), custom_call_target="tpu_custom_call" | custom-call | flops 1000000000 | bytes 2000000 | tf_op jit(solution)/shard_map/pick/pallas_call | solution.py:408
  31.9 2.7 %collective-permute-start.8 = (f32[4,128]{1,0:T(4,128)S(1)}, f32[4,128]{1,0:T(4,128)S(1)}, u32[]{:S(2)}, u32[]{:S(2)}) collective-permute-start(f32[4,128]{1,0:T(4,128)S(1)} %get-tuple-element.22), channel_id=1, source_target_pairs={{0,1},{1,0},{2,3},{3,2},{4,5},{5,4},{6,7},{7,6},{8,9},{9,8},{10,11... | collective-permute-start | bytes 6152 | tf_op jit(solution)/shard_map/ppermute | solution.py:802
  34.6 0.0 collective-permute-start.10
  34.6 0.2 collective-permute-start.9
  34.8 0.0 collective-permute-done.6.west_ref
  34.8 1.8 %collective-permute-done.7.east_ref = f32[2,18,649]{2,1,0:T(8,128)S(1)} collective-permute-done((f32[2,18,649]{2,1,0:T(8,128)S(1)}, f32[2,18,649]{2,1,0:T(8,128)S(1)}, u32[]{:S(2)}, u32[]{:S(2)}) %collective-permute-start.7) | collective-permute-done | bytes 93488 | tf_op jit(solution)/shard_map/ppermute | solution.py:648
  36.6 0.0 copy-done.5
  36.6 2.5 %advect.1.density_ref = f32[16,32,648]{2,1,0:T(8,128)S(1)} custom-call(s32[3]{0:T(128)S(1)} %pad_add_fusion.where_ref, f32[2,16,648]{2,1,0:T(8,128)S(1)} %copy-done.5, f32[16,32,648]{2,1,0:T(8,128)S(1)} %copy-done, s32[16,32]{1,0:T(8,128)S(1)} %copy-done.2, f32[2,32,649]{2,1,0:T(8,128)S(1)} %collective-permute-done.5.low_ref.high_ref, ...), custom_call_target="tpu_custom_call" | custom-call | flops 2600000000 | bytes 4000000 | tf_op jit(solution)/shard_map/advect/pallas_call | solution.py:623
  39.1 0.0 collective-permute-done.8.own_far_ref
  39.1 0.0 collective-permute-done.9.other_ref
  39.2 0.0 collective-permute-done.10.other_far_ref
  39.2 1.6 %stress.1 = (f32[2,4,128]{2,1,0:T(4,128)S(1)}, f32[3,4,128]{2,1,0:T(4,128)S(1)}) custom-call(s32[3]{0:T(128)S(1)} %pad_add_fusion.where_ref, f32[2,16,648]{2,1,0:T(8,128)S(1)} %copy-done.5, f32[16,32,648]{2,1,0:T(8,128)S(1)} %advect.1.density_ref, f32[4,128]{1,0:T(4,128)S(1)} %get-tuple-element.21.own_ref, f32[4,128]{1,0:T(4,128)S(1)} %collective-permute-done.8.own_far_ref, ...), custom_call_target="tpu_custom_call" | custom-call | flops 1500000000 | bytes 2000000 | tf_op jit(solution)/shard_map/stress/pallas_call | solution.py:698
  40.8 0.0 collective-permute-start.11
  40.9 1.2 %collective-permute-done.11.far_ref = f32[2,4,128]{2,1,0:T(4,128)S(1)} collective-permute-done((f32[2,4,128]{2,1,0:T(4,128)S(1)}, f32[2,4,128]{2,1,0:T(4,128)S(1)}, u32[]{:S(2)}, u32[]{:S(2)}) %collective-permute-start.11) | collective-permute-done | bytes 4128 | tf_op jit(solution)/shard_map/ppermute | solution.py:802
  42.0 0.5 collective-permute-start.12
  42.5 3.2 %collective-permute-done.12.refs_1_ = f32[1,4,128]{2,1,0:T(4,128)S(1)} collective-permute-done((f32[1,4,128]{2,1,0:T(4,128)S(1)}, f32[1,4,128]{2,1,0:T(4,128)S(1)}, u32[]{:S(2)}, u32[]{:S(2)}) %collective-permute-start.12) | collective-permute-done | bytes 2080 | tf_op jit(solution)/shard_map/ppermute | solution.py:802
  45.7 1.0 %collective-permute-start.13 = (f32[2,4,128]{2,1,0:T(4,128)S(1)}, f32[2,4,128]{2,1,0:T(4,128)S(1)}, u32[]{:S(2)}, u32[]{:S(2)}) collective-permute-start(f32[2,4,128]{2,1,0:T(4,128)S(1)} %pad_maximum_fusion.3), channel_id=1, source_target_pairs={{0,4},{1,5},{2,6},{3,7},{4,0},{5,1},{6,2},{7,3},{8,12},{9,13},{10,... | collective-permute-start | bytes 12296 | tf_op jit(solution)/shard_map/ppermute | solution.py:802
  46.6 2.1 %grid_tables.1.refs_2_ = bf16[4,2,640,512]{3,2,1,0:T(8,128)(2,1)S(1)} custom-call(s32[3]{0:T(128)S(1)} %pad_add_fusion.where_ref, s32[8]{0:T(128)S(1)} %copy-done.4), custom_call_target="tpu_custom_call" | custom-call | flops 2000000000 | bytes 5000000 | tf_op jit(solution)/shard_map/grid_tables/pallas_call | solution.py:311
  48.8 3.0 %collective-permute-start.4 = (bf16[4,2,4,16,384]{4,3,2,1,0:T(8,128)(2,1)S(1)}, bf16[4,2,4,16,384]{4,3,2,1,0:T(8,128)(2,1)S(1)}, u32[]{:S(2)}, u32[]{:S(2)}) collective-permute-start(bf16[4,2,4,16,384]{4,3,2,1,0:T(8,128)(2,1)S(1)} %pad_maximum_fusion.refs_0_.fourier_ref), channel_id=1, source_target_pairs={{0,1},{1,0},{2,3},{3,2},{4,5},{5,4},{6,7},{7,6},{8,9},{9,8},{10,11... | collective-permute-start | bytes 1179656 | tf_op jit(solution)/shard_map/ppermute | solution.py:802
  51.8 0.0 collective-permute-done.13.refs_2_
  51.8 0.0 copy-start.3
  51.8 0.1 collective-permute-start.14
  51.9 2.2 %spectra.1 = f32[16,32,648]{2,1,0:T(8,128)} custom-call(s32[3]{0:T(128)S(1)} %pad_add_fusion.where_ref, f32[2,16,648]{2,1,0:T(8,128)S(1)} %copy-done.5, f32[16,32,648]{2,1,0:T(8,128)S(1)} %advect.1.density_ref, f32[3,4,128]{2,1,0:T(4,128)S(1)} %get-tuple-element.23.points_ref, f32[2,4,128]{2,1,0:T(4,128)S(1)} %get-tuple-element.24.sums_ref, ...), custom_call_target="tpu_custom_call" | custom-call | flops 2500000000 | bytes 3000000 | tf_op jit(solution)/shard_map/spectra/pallas_call | solution.py:742
  54.1 5.9 %collective-permute-done.14.refs_3_ = f32[4,4,128]{2,1,0:T(4,128)S(1)} collective-permute-done((f32[4,4,128]{2,1,0:T(4,128)S(1)}, f32[4,4,128]{2,1,0:T(4,128)S(1)}, u32[]{:S(2)}, u32[]{:S(2)}) %collective-permute-start.14) | collective-permute-done | bytes 8224 | tf_op jit(solution)/shard_map/ppermute | solution.py:802
  60.0 1.3 %charnock.1 = f32[4,512]{1,0:T(4,128)} custom-call(s32[3]{0:T(128)S(1)} %pad_add_fusion.where_ref, s32[8]{0:T(128)S(1)} %copy-done.4, s32[4,512]{1,0:T(4,128)S(1)} %copy-done.3, f32[1,4,128]{2,1,0:T(4,128)S(1)} %add_sqrt_fusion.refs_0_, f32[1,4,128]{2,1,0:T(4,128)S(1)} %collective-permute-done.12.refs_1_, f32[2,4,128]{2,1,0:T(4,128)S(1)} %collective-permute-done.13.refs_2_, ...), custom_call_target="tpu_custom_call" | custom-call | flops 1000000000 | bytes 100000 | tf_op jit(solution)/shard_map/charnock/pallas_call | solution.py:789
  61.2 0.0 collective-permute-done.4.refs_1_
  61.2 2.5 %synthesis.1 = bf16[4,8,8,512]{3,2,1,0:T(8,128)(2,1)} custom-call(s32[3]{0:T(128)S(1)} %pad_add_fusion.where_ref, bf16[4,2,4,16,384]{4,3,2,1,0:T(8,128)(2,1)S(1)} %pad_maximum_fusion.refs_0_.fourier_ref, bf16[4,2,4,16,384]{4,3,2,1,0:T(8,128)(2,1)S(1)} %collective-permute-done.4.refs_1_, bf16[4,2,640,512]{3,2,1,0:T(8,128)(2,1)S(1)} %grid_tables.1.refs_2_), custom_call_target="tpu_custom_call" | custom-call | flops 3000000000 | bytes 2000000 | tf_op jit(solution)/shard_map/synthesis/pallas_call | solution.py:371
  (11 shorter events, 0.0 us)
Async XLA Ops:
  0.7 11.3 %copy-start = (f32[16,32,648]{2,1,0:T(8,128)S(1)}, f32[16,32,648]{2,1,0:T(8,128)}, u32[]{:S(2)}) copy-start(f32[16,32,648]{2,1,0:T(8,128)} %spectra_ref.3) | copy-start | bytes 3981316
  0.7 11.3 %copy-start.2 = (s32[16,32]{1,0:T(8,128)S(1)}, s32[16,32]{1,0:T(8,128)}, u32[]{:S(2)}) copy-start(s32[16,32]{1,0:T(8,128)} %mask_ref.3) | copy-start | bytes 6148
  0.7 18.2 %copy-start.1 = (s32[16,256]{1,0:T(8,128)S(1)}, s32[16,256]{1,0:T(8,128)}, u32[]{:S(2)}) copy-start(s32[16,256]{1,0:T(8,128)} %column_ref.1) | copy-start | bytes 49156
  0.7 18.2 %copy-start.4 = (s32[8]{0:T(128)S(1)}, s32[8]{0:T(128)}, u32[]{:S(2)}) copy-start(s32[8]{0:T(128)} %count_ref.5) | copy-start | bytes 100
  8.9 5.2 %collective-permute-start = (bf16[4,16,384]{2,1,0:T(8,128)(2,1)S(1)}, bf16[4,16,384]{2,1,0:T(8,128)(2,1)S(1)}, u32[]{:S(2)}, u32[]{:S(2)}) collective-permute-start(bf16[4,16,384]{2,1,0:T(8,128)(2,1)S(1)} %get-tuple-element.15), channel_id=1, source_target_pairs={{0,8},{8,0},{1,9},{9,1},{2,10},{10,2},{3,11},{11,3},{4,12},{12,4},... | collective-permute-start | bytes 147464 | tf_op jit(solution)/shard_map/ppermute | solution.py:848
  12.7 12.8 %collective-permute-start.5 = (f32[2,32,649]{2,1,0:T(8,128)S(1)}, f32[2,32,649]{2,1,0:T(8,128)S(1)}, u32[]{:S(2)}, u32[]{:S(2)}) collective-permute-start(f32[2,32,649]{2,1,0:T(8,128)S(1)} %get-tuple-element.16), channel_id=1, source_target_pairs={{0,8},{8,0},{1,9},{9,1},{2,10},{10,2},{3,11},{11,3},{4,12},{12,4},... | collective-permute-start | bytes 498440 | tf_op jit(solution)/shard_map/ppermute | solution.py:644
  14.2 7.2 %collective-permute-start.3 = (bf16[2,4,16,384]{3,2,1,0:T(8,128)(2,1)S(1)}, bf16[2,4,16,384]{3,2,1,0:T(8,128)(2,1)S(1)}, u32[]{:S(2)}, u32[]{:S(2)}) collective-permute-start(bf16[2,4,16,384]{3,2,1,0:T(8,128)(2,1)S(1)} %get-tuple-element.26), channel_id=1, source_target_pairs={{0,6},{1,7},{2,4},{3,5},{4,2},{5,3},{6,0},{7,1},{8,14},{9,15},{10,... | collective-permute-start | bytes 294920 | tf_op jit(solution)/shard_map/ppermute | solution.py:802
  18.3 7.2 %collective-permute-start.2 = (bf16[2,4,16,384]{3,2,1,0:T(8,128)(2,1)S(1)}, bf16[2,4,16,384]{3,2,1,0:T(8,128)(2,1)S(1)}, u32[]{:S(2)}, u32[]{:S(2)}) collective-permute-start(bf16[2,4,16,384]{3,2,1,0:T(8,128)(2,1)S(1)} %get-tuple-element.26), channel_id=1, source_target_pairs={{0,4},{1,5},{2,6},{3,7},{4,0},{5,1},{6,2},{7,3},{8,12},{9,13},{10,... | collective-permute-start | bytes 294920 | tf_op jit(solution)/shard_map/ppermute | solution.py:802
  18.3 7.2 %collective-permute-start.1 = (bf16[2,4,16,384]{3,2,1,0:T(8,128)(2,1)S(1)}, bf16[2,4,16,384]{3,2,1,0:T(8,128)(2,1)S(1)}, u32[]{:S(2)}, u32[]{:S(2)}) collective-permute-start(bf16[2,4,16,384]{3,2,1,0:T(8,128)(2,1)S(1)} %get-tuple-element.26), channel_id=1, source_target_pairs={{0,2},{1,3},{2,0},{3,1},{4,6},{5,7},{6,4},{7,5},{8,10},{9,11},{10,... | collective-permute-start | bytes 294920 | tf_op jit(solution)/shard_map/ppermute | solution.py:802
  25.5 11.1 %copy-start.5 = (f32[2,16,648]{2,1,0:T(8,128)S(1)}, f32[2,16,648]{2,1,0:T(8,128)}, u32[]{:S(2)}) copy-start(f32[2,16,648]{2,1,0:T(8,128)} %constant.19.clone.bins_ref) | copy-start | bytes 248836
  26.1 8.6 %collective-permute-start.6 = (f32[2,18,649]{2,1,0:T(8,128)S(1)}, f32[2,18,649]{2,1,0:T(8,128)S(1)}, u32[]{:S(2)}, u32[]{:S(2)}) collective-permute-start(f32[2,18,649]{2,1,0:T(8,128)S(1)} %get-tuple-element.19), channel_id=1, source_target_pairs={{0,1},{1,2},{2,3},{3,4},{4,5},{5,6},{6,7},{8,9},{9,10},{10,11},{11... | collective-permute-start | bytes 280376 | tf_op jit(solution)/shard_map/ppermute | solution.py:648
  29.5 7.0 %collective-permute-start.7 = (f32[2,18,649]{2,1,0:T(8,128)S(1)}, f32[2,18,649]{2,1,0:T(8,128)S(1)}, u32[]{:S(2)}, u32[]{:S(2)}) collective-permute-start(f32[2,18,649]{2,1,0:T(8,128)S(1)} %get-tuple-element.20), channel_id=1, source_target_pairs={{1,0},{2,1},{3,2},{4,3},{5,4},{6,5},{7,6},{9,8},{10,9},{11,10},{12... | collective-permute-start | bytes 280376 | tf_op jit(solution)/shard_map/ppermute | solution.py:648
  31.9 7.3 %collective-permute-start.8 = (f32[4,128]{1,0:T(4,128)S(1)}, f32[4,128]{1,0:T(4,128)S(1)}, u32[]{:S(2)}, u32[]{:S(2)}) collective-permute-start(f32[4,128]{1,0:T(4,128)S(1)} %get-tuple-element.22), channel_id=1, source_target_pairs={{0,1},{1,0},{2,3},{3,2},{4,5},{5,4},{6,7},{7,6},{8,9},{9,8},{10,11... | collective-permute-start | bytes 6152 | tf_op jit(solution)/shard_map/ppermute | solution.py:802
  34.6 4.6 %collective-permute-start.10 = (f32[4,128]{1,0:T(4,128)S(1)}, f32[4,128]{1,0:T(4,128)S(1)}, u32[]{:S(2)}, u32[]{:S(2)}) collective-permute-start(f32[4,128]{1,0:T(4,128)S(1)} %get-tuple-element.22), channel_id=1, source_target_pairs={{0,17},{1,16},{2,19},{3,18},{4,21},{5,20},{6,23},{7,22},{16,1},{17... | collective-permute-start | bytes 6152 | tf_op jit(solution)/shard_map/ppermute | solution.py:811
  34.6 4.6 %collective-permute-start.9 = (f32[4,128]{1,0:T(4,128)S(1)}, f32[4,128]{1,0:T(4,128)S(1)}, u32[]{:S(2)}, u32[]{:S(2)}) collective-permute-start(f32[4,128]{1,0:T(4,128)S(1)} %get-tuple-element.21.own_ref), channel_id=1, source_target_pairs={{0,16},{16,0},{1,17},{17,1},{2,18},{18,2},{3,19},{19,3},{4,20},{20... | collective-permute-start | bytes 6152 | tf_op jit(solution)/shard_map/ppermute | solution.py:802
  40.8 1.2 %collective-permute-start.11 = (f32[2,4,128]{2,1,0:T(4,128)S(1)}, f32[2,4,128]{2,1,0:T(4,128)S(1)}, u32[]{:S(2)}, u32[]{:S(2)}) collective-permute-start(f32[2,4,128]{2,1,0:T(4,128)S(1)} %get-tuple-element.24.sums_ref), channel_id=1, source_target_pairs={{0,16},{16,0},{1,17},{17,1},{2,18},{18,2},{3,19},{19,3},{4,20},{20... | collective-permute-start | bytes 12296 | tf_op jit(solution)/shard_map/ppermute | solution.py:802
  42.0 3.7 %collective-permute-start.12 = (f32[1,4,128]{2,1,0:T(4,128)S(1)}, f32[1,4,128]{2,1,0:T(4,128)S(1)}, u32[]{:S(2)}, u32[]{:S(2)}) collective-permute-start(f32[1,4,128]{2,1,0:T(4,128)S(1)} %add_sqrt_fusion.refs_0_), channel_id=1, source_target_pairs={{0,2},{1,3},{2,0},{3,1},{4,6},{5,7},{6,4},{7,5},{8,10},{9,11},{10,... | collective-permute-start | bytes 6152 | tf_op jit(solution)/shard_map/ppermute | solution.py:802
  45.7 6.1 %collective-permute-start.13 = (f32[2,4,128]{2,1,0:T(4,128)S(1)}, f32[2,4,128]{2,1,0:T(4,128)S(1)}, u32[]{:S(2)}, u32[]{:S(2)}) collective-permute-start(f32[2,4,128]{2,1,0:T(4,128)S(1)} %pad_maximum_fusion.3), channel_id=1, source_target_pairs={{0,4},{1,5},{2,6},{3,7},{4,0},{5,1},{6,2},{7,3},{8,12},{9,13},{10,... | collective-permute-start | bytes 12296 | tf_op jit(solution)/shard_map/ppermute | solution.py:802
  48.8 12.5 %collective-permute-start.4 = (bf16[4,2,4,16,384]{4,3,2,1,0:T(8,128)(2,1)S(1)}, bf16[4,2,4,16,384]{4,3,2,1,0:T(8,128)(2,1)S(1)}, u32[]{:S(2)}, u32[]{:S(2)}) collective-permute-start(bf16[4,2,4,16,384]{4,3,2,1,0:T(8,128)(2,1)S(1)} %pad_maximum_fusion.refs_0_.fourier_ref), channel_id=1, source_target_pairs={{0,1},{1,0},{2,3},{3,2},{4,5},{5,4},{6,7},{7,6},{8,9},{9,8},{10,11... | collective-permute-start | bytes 1179656 | tf_op jit(solution)/shard_map/ppermute | solution.py:802
  51.8 8.1 %copy-start.3 = (s32[4,512]{1,0:T(4,128)S(1)}, s32[4,512]{1,0:T(4,128)}, u32[]{:S(2)}) copy-start(s32[4,512]{1,0:T(4,128)} %source_ref.1) | copy-start | bytes 24580
  51.8 8.1 %collective-permute-start.14 = (f32[4,4,128]{2,1,0:T(4,128)S(1)}, f32[4,4,128]{2,1,0:T(4,128)S(1)}, u32[]{:S(2)}, u32[]{:S(2)}) collective-permute-start(f32[4,4,128]{2,1,0:T(4,128)S(1)} %pad_maximum_fusion.2), channel_id=1, source_target_pairs={{0,1},{1,0},{2,3},{3,2},{4,5},{5,4},{6,7},{7,6},{8,9},{9,8},{10,11... | collective-permute-start | bytes 24584 | tf_op jit(solution)/shard_map/ppermute | solution.py:802
